TPU v7x, 256 devices: a whole 4x4x8 slice. The times are simulated.
256 devices in a mesh: seq: 256 (over y, z, x, core).
Axes of the slice: x: 4, y: 4, z: 8, core: 2. Of those that a mesh axis runs over, the one named last changes fastest.
Arguments:
- queries: bfloat16 [16, 8192], P(None, 'seq'), may hold values from -1000 to 1000
- span_keys: bfloat16 [16, 1024], P(None, 'seq'), may hold values from -6 to 6
- span_values: bfloat16 [16, 1024], P(None, 'seq'), may hold values from -6 to 6
- positions: int32 [3, 16], replicated, may hold values from 0 to 8191, as said below
- span_segments: int32 [16], replicated, may hold values from 0 to 3, as said below
- cache_keys: bfloat16 [131072, 1024], P('seq'), may hold values from -6 to 6
- cache_values: bfloat16 [131072, 1024], P('seq'), may hold values from -6 to 6
- cache_segments: int32 [131072], P('seq'), may hold values from 0 to 3
Outputs:
- attended: bfloat16 [16, 8192], replicated
Inputs may be any that keep to these rules, and one draw needn't show every extreme that they name: `positions`: row 0 holds time ids; rows 1 and 2 hold height and width ids, which are below 64. `span_segments`: never falling; every request 0 to 3 has one run of rows, and every run starts at an even row.
All inputs are finite; a program needn't handle non-finite values.
Results may differ from a plain program's by a relative error of at most 0.0054.
Values may be sent and summed in bfloat16 or wider, within the bound.
No kernel may reach another device: no remote copies, remote signals or barrier semaphores. Data moves between devices by JAX's collectives and lax.ppermute only.
A program may use at most 64 MiB of HBM per device.

v0:
```python
import math

import jax
import jax.numpy as jnp
from jax import lax
from jax.sharding import Mesh
from jax.sharding import PartitionSpec as P

H = 64
KVH = 8
HD = 128
SEQ = ("seq_0", "seq_1", "seq_2", "seq_3")


def copy_for_each(shard, axis):
    size = lax.axis_size(axis)
    return lax.all_to_all(
        jnp.broadcast_to(shard[None], (size, *shard.shape)), axis, 0, 0, tiled=True
    )


def in_order(tiles, dim):
    dims = list(tiles.shape[1:])
    dims[dim] *= tiles.shape[0]
    return jnp.moveaxis(tiles, 0, dim).reshape(dims)


def gathered_by_axis(shard, axes, dim):
    far, near = axes
    initial = copy_for_each(shard, far)
    tiles = jnp.swapaxes(copy_for_each(initial, near), 0, 1)
    return in_order(tiles.reshape(-1, *shard.shape), dim)


def sent_together(arrays, axis, dim, along):
    ends, at = ([], 0)
    for a in arrays[:-1]:
        at += a.shape[along]
        ends.append(at)
    both = jnp.concatenate(arrays, axis=along)
    return tuple(jnp.split(gathered_by_axis(both, axis, dim), ends, axis=along))


def of_everyone(shard, axis):
    return copy_for_each(shard, axis).max(axis=0)


def by_axis(shard, axes):
    far, near = axes
    return of_everyone(of_everyone(shard, near), far)


def split_up(shard, dim, size):
    before, after = (shard.shape[:dim], shard.shape[dim + 1 :])
    return jnp.moveaxis(shard.reshape(*before, size, -1, *after), dim, 0)


def sum_at_owner(shard, axis, dim):
    tiles = split_up(shard, dim, lax.axis_size(axis))
    arrived = lax.all_to_all(tiles, axis, split_axis=0, concat_axis=0, tiled=True)
    return arrived.astype(jnp.float32).sum(axis=0)


def summed_rows(shard, axes, dim):
    far, near = axes
    own = sum_at_owner(split_up(shard, dim, lax.axis_size(far)), near, dim + 1)
    return jnp.sum(
        lax.all_to_all(own.astype(jnp.bfloat16), far, 0, 0, tiled=True).astype(jnp.float32), axis=0
    )


def side_by_side(arrays, axis, dim, along):
    widths = [math.prod(a.shape[along:]) for a in arrays]
    both = jnp.concatenate(
        [a.reshape(*a.shape[:along], w) for a, w in zip(arrays, widths)], axis=along
    )
    whole = summed_rows(both, axis, dim)
    tiles = jnp.split(whole, [sum(widths[:k]) for k in range(1, len(widths))], axis=along)
    return tuple((b.reshape(*whole.shape[:along], *a.shape[along:]) for a, b in zip(arrays, tiles)))


def rope_tables(positions, head_dim):
    half = head_dim // 2
    index = jnp.arange(half, dtype=jnp.int32)
    inverse = jnp.power(jnp.float32(1000000.0), -2.0 * index.astype(jnp.float32) / head_dim)
    section = jnp.where(index < head_dim // 8, 0, jnp.where(index < 5 * head_dim // 16, 1, 2))
    chosen = jnp.where(
        section[None, :] == 0,
        positions[0][:, None],
        jnp.where(section[None, :] == 1, positions[1][:, None], positions[2][:, None]),
    )
    angle = chosen.astype(jnp.float32) * inverse[None, :]
    return (jnp.cos(angle), jnp.sin(angle))


def rotate(values, cosines, sines):
    half = values.shape[-1] // 2
    first = values[..., :half]
    second = values[..., half:]
    cosine = cosines[:, None, :]
    sine = sines[:, None, :]
    return jnp.concatenate(
        [first * cosine - second * sine, second * cosine + first * sine], axis=-1
    )


def head_state(q_rot, keys, values, visible):
    rows, kv_heads, group, head_dim = q_rot.shape
    scale = 1.0 / head_dim**0.5
    outs, peaks, totals = ([], [], [])
    for head in range(kv_heads):
        block = q_rot[:, head].reshape(rows * group, head_dim)
        key_cols = keys[:, head * head_dim : (head + 1) * head_dim]
        value_cols = values[:, head * head_dim : (head + 1) * head_dim]
        scores = (
            lax.dot_general(
                block, key_cols, (((1,), (1,)), ((), ())), preferred_element_type=jnp.float32
            )
            * scale
        )
        scores = scores.reshape(rows, group, -1)
        mask = visible[:, None, :]
        peak = jnp.max(jnp.where(mask, scores, jnp.float32(-1e30)), axis=-1)
        weights = jnp.where(mask, jnp.exp(scores - peak[..., None]), jnp.float32(0.0))
        total = jnp.sum(weights, axis=-1)
        out = jnp.dot(
            weights.astype(jnp.bfloat16).reshape(rows * group, -1),
            value_cols,
            preferred_element_type=jnp.float32,
        )
        outs.append(out.reshape(rows, group, head_dim))
        peaks.append(peak)
        totals.append(total)
    out_all = jnp.stack(outs, axis=1).reshape(rows * kv_heads * group, head_dim)
    peak_all = jnp.stack(peaks, axis=1).reshape(rows * kv_heads * group)
    total_all = jnp.stack(totals, axis=1).reshape(rows * kv_heads * group)
    return (out_all, peak_all, total_all)


def combine(left, right):
    out_a, peak_a, total_a = left
    out_b, peak_b, total_b = right
    peak = jnp.maximum(peak_a, peak_b)
    factor_a = jnp.exp(peak_a - peak)
    factor_b = jnp.exp(peak_b - peak)
    return (
        out_a * factor_a[:, None] + out_b * factor_b[:, None],
        peak,
        total_a * factor_a + total_b * factor_b,
    )


def per_device(
    queries,
    span_keys,
    span_values,
    positions,
    span_segments,
    cache_keys,
    cache_values,
    cache_segments,
):
    whole_queries, whole_keys, whole_values = (
        gathered_by_axis(queries, (("seq_0", "seq_1"), ("seq_2", "seq_3")), 1),
        *sent_together((span_keys, span_values), (("seq_0", "seq_1"), ("seq_2", "seq_3")), 1, 0),
    )
    rows = whole_queries.shape[0]
    group = H // KVH
    cosines, sines = rope_tables(positions, HD)
    q_rot = rotate(whole_queries.astype(jnp.float32).reshape(rows, H, HD), cosines, sines).astype(
        jnp.bfloat16
    )
    q_rot = q_rot.reshape(rows, KVH, group, HD)
    k_rot = rotate(whole_keys.astype(jnp.float32).reshape(rows, KVH, HD), cosines, sines)
    k_rot = k_rot.astype(jnp.bfloat16).reshape(rows, KVH * HD)
    index = jnp.arange(rows, dtype=jnp.int32)
    own_visible = (span_segments[:, None] == span_segments[None, :]) & (
        index[None, :] <= index[:, None]
    )
    span_state = head_state(q_rot, k_rot, whole_values, own_visible)
    visible = span_segments[:, None] == cache_segments[None, :]
    local_state = head_state(q_rot, cache_keys, cache_values, visible)
    local_out, local_peak, local_total = local_state
    peak = by_axis(local_peak, (("seq_0", "seq_1"), ("seq_2", "seq_3")))
    factor = jnp.exp(local_peak - peak)
    shares, totals = side_by_side(
        (
            (local_out * factor[:, None]).astype(jnp.bfloat16),
            (local_total * factor).astype(jnp.bfloat16),
        ),
        (("seq_0", "seq_1"), ("seq_2", "seq_3")),
        0,
        1,
    )
    count = totals.shape[0]
    start = lax.axis_index(SEQ) * count
    own_out = lax.dynamic_slice_in_dim(span_state[0], start, count, 0)
    own_peak = lax.dynamic_slice_in_dim(span_state[1], start, count, 0)
    own_total = lax.dynamic_slice_in_dim(span_state[2], start, count, 0)
    mine_peak = lax.dynamic_slice_in_dim(peak, start, count, 0)
    merged_out, _, merged_total = combine(
        (shares, mine_peak, totals), (own_out, own_peak, own_total)
    )
    finished = (merged_out / merged_total[:, None]).astype(jnp.bfloat16)
    gathered = gathered_by_axis(finished, (("seq_0", "seq_1"), ("seq_2", "seq_3")), 0)
    return gathered.reshape(rows, H * HD)


def solution(mesh):
    split = Mesh(mesh.devices.reshape(4, 8, 4, 2), ("seq_0", "seq_1", "seq_2", "seq_3"))
    return jax.shard_map(
        per_device,
        mesh=split,
        in_specs=(
            P(None, SEQ),
            P(None, SEQ),
            P(None, SEQ),
            P(),
            P(),
            P(SEQ, None),
            P(SEQ, None),
            P(SEQ),
        ),
        out_specs=P(),
        check_vma=False,
    )
```

profile of v0, /device:TPU:1, one launch (start us, length us, event | category | flops | bytes accessed | tf_op | source)
XLA Modules:
  0.0 185.5 jit_solution(16587802852819105903)
XLA Ops:
  0.0 0.8 pad_maximum_fusion.2
  1.4 12.0 %all-to-all-start.6 = ((bf16[32,32,4]{1,2,0:T(4,128)(2,1)}), bf16[32,32,4]{1,2,0:T(4,128)(2,1)S(1)}, u32[]{:S(2)}, u32[]{:S(2)}) async-start(bf16[32,32,4]{1,2,0:T(4,128)(2,1)} %broadcast_in_dim.330), calls=%async_computation.6 | async-start | bytes 65536 | tf_op jit(solution)/shard_map/all_to_all | solution.py:17
  13.5 0.8 slice_bitcast_fusion.18
  14.3 0.8 fusion.138
  16.7 5.5 %all-to-all-done.6 = bf16[32,32,4]{1,2,0:T(4,128)(2,1)S(1)} async-done(((bf16[32,32,4]{1,2,0:T(4,128)(2,1)}), bf16[32,32,4]{1,2,0:T(4,128)(2,1)S(1)}, u32[]{:S(2)}, u32[]{:S(2)}) %all-to-all-start.6) | async-done | bytes 8224 | tf_op jit(solution)/shard_map/all_to_all | solution.py:17
  22.2 3.8 %all-to-all-start = ((bf16[32,2,256]{2,1,0:T(2,128)(2,1)}), bf16[32,2,256]{2,1,0:T(2,128)(2,1)S(1)}, u32[]{:S(2)}, u32[]{:S(2)}) async-start(bf16[32,2,256]{2,1,0:T(2,128)(2,1)} %reshape.738), calls=%async_computation | async-start | bytes 65536 | tf_op jit(solution)/shard_map/all_to_all | solution.py:17
  26.1 0.9 reshape.736
  27.0 7.7 %all-to-all-done = bf16[32,2,256]{2,1,0:T(2,128)(2,1)S(1)} async-done(((bf16[32,2,256]{2,1,0:T(2,128)(2,1)}), bf16[32,2,256]{2,1,0:T(2,128)(2,1)S(1)}, u32[]{:S(2)}, u32[]{:S(2)}) %all-to-all-start) | async-done | bytes 32800 | tf_op jit(solution)/shard_map/all_to_all | solution.py:17
  34.7 7.5 %all-to-all-start.7 = ((bf16[8,2,2048]{2,1,0:T(2,128)(2,1)}), bf16[8,2,2048]{2,1,0:T(2,128)(2,1)S(1)}, u32[]{:S(2)}, u32[]{:S(2)}) async-start(bf16[8,2,2048]{2,1,0:T(2,128)(2,1)} %reshape.736), calls=%async_computation.7 | async-start | bytes 131072 | tf_op jit(solution)/shard_map/all_to_all | solution.py:17
  43.6 1.7 reshape.740
  45.2 1.9 %all-to-all-done.7 = bf16[8,2,2048]{2,1,0:T(2,128)(2,1)S(1)} async-done(((bf16[8,2,2048]{2,1,0:T(2,128)(2,1)}), bf16[8,2,2048]{2,1,0:T(2,128)(2,1)S(1)}, u32[]{:S(2)}, u32[]{:S(2)}) %all-to-all-start.7) | async-done | bytes 65568 | tf_op jit(solution)/shard_map/all_to_all | solution.py:17
  47.1 4.1 %all-to-all-start.1 = ((bf16[8,2,8192]{2,1,0:T(2,128)(2,1)}), bf16[8,2,8192]{2,1,0:T(2,128)(2,1)S(1)}, u32[]{:S(2)}, u32[]{:S(2)}) async-start(bf16[8,2,8192]{2,1,0:T(2,128)(2,1)} %reshape.740), calls=%async_computation.1 | async-start | bytes 524288 | tf_op jit(solution)/shard_map/all_to_all | solution.py:17
  52.7 5.0 %all-to-all-done.1 = bf16[8,2,8192]{2,1,0:T(2,128)(2,1)S(1)} async-done(((bf16[8,2,8192]{2,1,0:T(2,128)(2,1)}), bf16[8,2,8192]{2,1,0:T(2,128)(2,1)S(1)}, u32[]{:S(2)}, u32[]{:S(2)}) %all-to-all-start.1) | async-done | bytes 262176 | tf_op jit(solution)/shard_map/all_to_all | solution.py:17
  68.1 1.2 fusion.153
  73.4 1.2 fusion.25
  74.8 1.9 %fusion.40 = (f32[128]{0:T(128)}, f32[128]{0:T(128)}, f32[128]{0:T(128)}, f32[128]{0:T(128)S(1)}, f32[128]{0:T(128)S(1)}, /*index=5*/f32[128]{0:T(128)S(1)}, f32[128]{0:T(128)S(1)}, f32[128]{0:T(128)}, f32[128,512]{1,0:T(8,128)S(1)}) fusion(f32[128,512]{1,0:T(8,128)S(1)} %get-tuple-element.68, f32[128]{0:T(128)S(1)} %get-tuple-element.13, ...), kind=kOutput, calls=%fused_computation.96 | convolution fusion | flops 18021376 | bytes 2274304 | tf_op jit(solution)/shard_map/dot_general | solution.py:116
  79.6 4.3 %all-to-all-start.2 = ((f32[8,1,1024]{2,1,0:T(1,128)}), f32[8,1,1024]{2,1,0:T(1,128)S(1)}, u32[]{:S(2)}, u32[]{:S(2)}) async-start(f32[8,1,1024]{2,1,0:T(1,128)} %broadcast_in_dim.326), calls=%async_computation.2 | async-start | bytes 65536 | tf_op jit(solution)/shard_map/all_to_all | solution.py:17
  83.9 0.8 fusion.15
  84.8 0.9 fusion.14
  85.7 0.9 fusion.13
  86.6 0.9 fusion.12
  87.5 0.9 fusion.11
  88.7 1.1 fusion.38
  90.3 0.8 copy-done.2
  95.4 0.8 stack.130
  96.2 0.8 copy.358
  97.0 0.8 copy.362
  97.8 0.8 copy.365
  98.6 0.8 copy.368
  99.4 0.8 copy.371
  100.2 0.8 copy.374
  101.0 1.3 constant_dynamic-update-slice_fusion.22
  105.8 1.3 constant_dynamic-update-slice_fusion.30
  107.1 1.3 constant_dynamic-update-slice_fusion.29
  108.4 1.3 constant_dynamic-update-slice_fusion.28
  109.7 1.3 constant_dynamic-update-slice_fusion.27
  111.0 1.3 constant_dynamic-update-slice_fusion.26
  114.7 4.0 %all-to-all-start.3 = ((f32[32,1,1024]{2,1,0:T(1,128)}), f32[32,1,1024]{2,1,0:T(1,128)S(1)}, u32[]{:S(2)}, u32[]{:S(2)}) async-start(f32[32,1,1024]{2,1,0:T(1,128)} %broadcast_in_dim.327), calls=%async_computation.3 | async-start | bytes 262144 | tf_op jit(solution)/shard_map/all_to_all | solution.py:17
  119.7 8.0 %all-to-all-done.3 = f32[32,1,1024]{2,1,0:T(1,128)S(1)} async-done(((f32[32,1,1024]{2,1,0:T(1,128)}), f32[32,1,1024]{2,1,0:T(1,128)S(1)}, u32[]{:S(2)}, u32[]{:S(2)}) %all-to-all-start.3) | async-done | bytes 131104 | tf_op jit(solution)/shard_map/all_to_all | solution.py:17
  129.6 1.0 copy.339
  130.6 6.6 %all-to-all-start.4 = ((bf16[8,32,4,129]{3,2,1,0:T(4,128)(2,1)}), bf16[8,32,4,129]{3,2,1,0:T(4,128)(2,1)S(1)}, u32[]{:S(2)}, u32[]{:S(2)}) async-start(bf16[8,32,4,129]{3,2,1,0:T(4,128)(2,1)} %copy.339), calls=%async_computation.4 | async-start | bytes 1048576 | tf_op jit(solution)/shard_map/all_to_all | solution.py:60
  137.6 8.9 %all-to-all-done.4 = bf16[8,32,4,129]{3,2,1,0:T(4,128)(2,1)S(1)} async-done(((bf16[8,32,4,129]{3,2,1,0:T(4,128)(2,1)}), bf16[8,32,4,129]{3,2,1,0:T(4,128)(2,1)S(1)}, u32[]{:S(2)}, u32[]{:S(2)}) %all-to-all-start.4) | async-done | bytes 264224 | tf_op jit(solution)/shard_map/all_to_all | solution.py:60
  146.5 0.9 reduce_sum.173
  147.4 3.9 %all-to-all-start.5 = ((bf16[32,4,129]{2,1,0:T(4,128)(2,1)}), bf16[32,4,129]{2,1,0:T(4,128)(2,1)S(1)}, u32[]{:S(2)}, u32[]{:S(2)}) async-start(bf16[32,4,129]{2,1,0:T(4,128)(2,1)} %reduce_sum.173), calls=%async_computation.5 | async-start | bytes 131072 | tf_op jit(solution)/shard_map/all_to_all | solution.py:68
  151.4 8.7 %all-to-all-done.5 = bf16[32,4,129]{2,1,0:T(4,128)(2,1)S(1)} async-done(((bf16[32,4,129]{2,1,0:T(4,128)(2,1)}), bf16[32,4,129]{2,1,0:T(4,128)(2,1)S(1)}, u32[]{:S(2)}, u32[]{:S(2)}) %all-to-all-start.5) | async-done | bytes 33056 | tf_op jit(solution)/shard_map/all_to_all | solution.py:68
  160.4 11.9 %all_to_all.52 = bf16[32,4,128]{2,1,0:T(4,128)(2,1)S(1)} all-to-all(bf16[32,4,128]{2,1,0:T(4,128)(2,1)S(1)} %broadcast_in_dim.334), channel_id=1, replica_groups=mesh['seq_0'=4,'seq_1'=8,'seq_2'=4,'seq_3'=2] {'seq_0','seq_1'}, dimensions={0} | all-to-all | bytes 65536 | tf_op jit(solution)/shard_map/all_to_all | solution.py:17
  172.4 12.1 %all_to_all.53 = bf16[8,32,4,128]{3,2,1,0:T(4,128)(2,1)S(1)} all-to-all(bf16[8,32,4,128]{3,2,1,0:T(4,128)(2,1)S(1)} %broadcast_in_dim.335), channel_id=1, replica_groups=mesh['seq_0'=4,'seq_1'=8,'seq_2'=4,'seq_3'=2] {'seq_2','seq_3'}, dimensions={0} | all-to-all | bytes 524288 | tf_op jit(solution)/shard_map/all_to_all | solution.py:17
  184.7 0.9 reshape_reshape_reshape.3
  (206 shorter events, 37.1 us)
Async XLA Ops:
  1.4 20.8 %all-to-all-start.6 = ((bf16[32,32,4]{1,2,0:T(4,128)(2,1)}), bf16[32,32,4]{1,2,0:T(4,128)(2,1)S(1)}, u32[]{:S(2)}, u32[]{:S(2)}) async-start(bf16[32,32,4]{1,2,0:T(4,128)(2,1)} %broadcast_in_dim.330), calls=%async_computation.6 | async-start | bytes 65536 | tf_op jit(solution)/shard_map/all_to_all | solution.py:17
  22.2 12.5 %all-to-all-start = ((bf16[32,2,256]{2,1,0:T(2,128)(2,1)}), bf16[32,2,256]{2,1,0:T(2,128)(2,1)S(1)}, u32[]{:S(2)}, u32[]{:S(2)}) async-start(bf16[32,2,256]{2,1,0:T(2,128)(2,1)} %reshape.738), calls=%async_computation | async-start | bytes 65536 | tf_op jit(solution)/shard_map/all_to_all | solution.py:17
  34.7 12.4 %all-to-all-start.7 = ((bf16[8,2,2048]{2,1,0:T(2,128)(2,1)}), bf16[8,2,2048]{2,1,0:T(2,128)(2,1)S(1)}, u32[]{:S(2)}, u32[]{:S(2)}) async-start(bf16[8,2,2048]{2,1,0:T(2,128)(2,1)} %reshape.736), calls=%async_computation.7 | async-start | bytes 131072 | tf_op jit(solution)/shard_map/all_to_all | solution.py:17
  47.1 10.6 %all-to-all-start.1 = ((bf16[8,2,8192]{2,1,0:T(2,128)(2,1)}), bf16[8,2,8192]{2,1,0:T(2,128)(2,1)S(1)}, u32[]{:S(2)}, u32[]{:S(2)}) async-start(bf16[8,2,8192]{2,1,0:T(2,128)(2,1)} %reshape.740), calls=%async_computation.1 | async-start | bytes 524288 | tf_op jit(solution)/shard_map/all_to_all | solution.py:17
  59.9 1.2 copy-start.1
  62.7 21.2 %copy-start = (bf16[512,1024]{1,0:T(8,128)(2,1)S(1)}, bf16[512,1024]{1,0:T(8,128)(2,1)}, u32[]{:S(2)}) copy-start(bf16[512,1024]{1,0:T(8,128)(2,1)} %param.14) | copy-start | bytes 3145732
  74.6 2.1 %copy-start.23 = (f32[128]{0:T(128)}, f32[128]{0:T(128)S(1)}, u32[]{:S(2)}) copy-start(f32[128]{0:T(128)S(1)} %get-tuple-element.13) | copy-start | bytes 1540
  74.6 2.1 %copy-start.25 = (f32[128]{0:T(128)}, f32[128]{0:T(128)S(1)}, u32[]{:S(2)}) copy-start(f32[128]{0:T(128)S(1)} %get-tuple-element.14) | copy-start | bytes 1540
  76.7 0.5 copy-start.19
  76.7 0.6 copy-start.21
  76.7 0.7 copy-start.15
  76.7 0.7 copy-start.17
  79.6 34.4 %all-to-all-start.2 = ((f32[8,1,1024]{2,1,0:T(1,128)}), f32[8,1,1024]{2,1,0:T(1,128)S(1)}, u32[]{:S(2)}, u32[]{:S(2)}) async-start(f32[8,1,1024]{2,1,0:T(1,128)} %broadcast_in_dim.326), calls=%async_computation.2 | async-start | bytes 65536 | tf_op jit(solution)/shard_map/all_to_all | solution.py:17
  83.9 4.5 %copy-start.14 = (f32[128]{0:T(128)S(1)}, f32[128]{0:T(128)}, u32[]{:S(2)}) copy-start(f32[128]{0:T(128)} %get-tuple-element.7) | copy-start | bytes 1540
  83.9 4.8 %copy-start.13 = (f32[128]{0:T(128)S(1)}, f32[128]{0:T(128)}, u32[]{:S(2)}) copy-start(f32[128]{0:T(128)} %get-tuple-element.6) | copy-start | bytes 1540
  83.9 4.8 %copy-start.16 = (f32[128]{0:T(128)S(1)}, f32[128]{0:T(128)}, u32[]{:S(2)}) copy-start(f32[128]{0:T(128)} %copy-done.15) | copy-start | bytes 1540
  83.9 4.8 %copy-start.18 = (f32[128]{0:T(128)S(1)}, f32[128]{0:T(128)}, u32[]{:S(2)}) copy-start(f32[128]{0:T(128)} %copy-done.17) | copy-start | bytes 1540
  83.9 4.8 %copy-start.20 = (f32[128]{0:T(128)S(1)}, f32[128]{0:T(128)}, u32[]{:S(2)}) copy-start(f32[128]{0:T(128)} %copy-done.19) | copy-start | bytes 1540
  83.9 4.8 %copy-start.22 = (f32[128]{0:T(128)S(1)}, f32[128]{0:T(128)}, u32[]{:S(2)}) copy-start(f32[128]{0:T(128)} %copy-done.21) | copy-start | bytes 1540
  84.8 5.3 %copy-start.24 = (f32[128]{0:T(128)S(1)}, f32[128]{0:T(128)}, u32[]{:S(2)}) copy-start(f32[128]{0:T(128)} %copy-done.23) | copy-start | bytes 1540
  86.5 15.7 %copy-start.10 = (f32[16,1,8]{2,0,1:T(8,128)S(1)}, f32[16,1,8]{2,0,1:T(8,128)}, u32[]{:S(2)}) copy-start(f32[16,1,8]{2,0,1:T(8,128)} %stack.135) | copy-start | bytes 1540
  86.6 16.3 %copy-start.9 = (f32[16,1,8]{2,0,1:T(8,128)S(1)}, f32[16,1,8]{2,0,1:T(8,128)}, u32[]{:S(2)}) copy-start(f32[16,1,8]{2,0,1:T(8,128)} %stack.136) | copy-start | bytes 1540
  86.6 16.9 %copy-start.8 = (f32[16,1,8]{2,0,1:T(8,128)S(1)}, f32[16,1,8]{2,0,1:T(8,128)}, u32[]{:S(2)}) copy-start(f32[16,1,8]{2,0,1:T(8,128)} %stack.137) | copy-start | bytes 1540
  86.6 17.5 %copy-start.7 = (f32[16,1,8]{2,0,1:T(8,128)S(1)}, f32[16,1,8]{2,0,1:T(8,128)}, u32[]{:S(2)}) copy-start(f32[16,1,8]{2,0,1:T(8,128)} %stack.138) | copy-start | bytes 1540
  86.6 18.1 %copy-start.6 = (f32[16,1,8]{2,0,1:T(8,128)S(1)}, f32[16,1,8]{2,0,1:T(8,128)}, u32[]{:S(2)}) copy-start(f32[16,1,8]{2,0,1:T(8,128)} %stack.139) | copy-start | bytes 1540
  89.8 29.2 %copy-start.27 = (f32[128]{0:T(128)S(1)}, f32[128]{0:T(128)}, u32[]{:S(2)}) copy-start(f32[128]{0:T(128)} %get-tuple-element.22) | copy-start | bytes 1540
  90.0 29.4 %copy-start.12 = (bf16[128,16]{0,1:T(8,128)(2,1)S(1)}, bf16[128,16]{0,1:T(8,128)(2,1)}, u32[]{:S(2)}) copy-start(bf16[128,16]{0,1:T(8,128)(2,1)} %get-tuple-element.57) | copy-start | bytes 12292
  90.3 0.8 copy-start.2
  91.1 27.9 %copy-start.3 = (f32[16,8,8,128]{3,2,0,1:T(8,128)S(1)}, f32[16,8,8,128]{3,2,0,1:T(8,128)}, u32[]{:S(2)}) copy-start(f32[16,8,8,128]{3,2,0,1:T(8,128)} %copy-done.2) | copy-start | bytes 1572868
  114.7 13.0 %all-to-all-start.3 = ((f32[32,1,1024]{2,1,0:T(1,128)}), f32[32,1,1024]{2,1,0:T(1,128)S(1)}, u32[]{:S(2)}, u32[]{:S(2)}) async-start(f32[32,1,1024]{2,1,0:T(1,128)} %broadcast_in_dim.327), calls=%async_computation.3 | async-start | bytes 262144 | tf_op jit(solution)/shard_map/all_to_all | solution.py:17
  128.8 8.3 %copy-start.5 = (f32[16,8,8]{2,0,1:T(8,128)S(1)}, f32[16,8,8]{2,0,1:T(8,128)}, u32[]{:S(2)}) copy-start(f32[16,8,8]{2,0,1:T(8,128)} %constant_dynamic-update-slice_fusion.26) | copy-start | bytes 12292
  128.8 8.3 %copy-start.4 = (f32[16,8,8]{2,0,1:T(8,128)S(1)}, f32[16,8,8]{2,0,1:T(8,128)}, u32[]{:S(2)}) copy-start(f32[16,8,8]{2,0,1:T(8,128)} %constant_dynamic-update-slice_fusion.16) | copy-start | bytes 12292
  128.8 8.4 %copy-start.26 = (f32[128]{0:T(128)S(1)}, f32[128]{0:T(128)}, u32[]{:S(2)}) copy-start(f32[128]{0:T(128)} %get-tuple-element.21) | copy-start | bytes 1540
  128.9 8.5 %copy-start.11 = (bf16[128,16]{0,1:T(8,128)(2,1)S(1)}, bf16[128,16]{0,1:T(8,128)(2,1)}, u32[]{:S(2)}) copy-start(bf16[128,16]{0,1:T(8,128)(2,1)} %get-tuple-element.56) | copy-start | bytes 12292
  130.6 15.9 %all-to-all-start.4 = ((bf16[8,32,4,129]{3,2,1,0:T(4,128)(2,1)}), bf16[8,32,4,129]{3,2,1,0:T(4,128)(2,1)S(1)}, u32[]{:S(2)}, u32[]{:S(2)}) async-start(bf16[8,32,4,129]{3,2,1,0:T(4,128)(2,1)} %copy.339), calls=%async_computation.4 | async-start | bytes 1048576 | tf_op jit(solution)/shard_map/all_to_all | solution.py:60
  147.4 12.7 %all-to-all-start.5 = ((bf16[32,4,129]{2,1,0:T(4,128)(2,1)}), bf16[32,4,129]{2,1,0:T(4,128)(2,1)S(1)}, u32[]{:S(2)}, u32[]{:S(2)}) async-start(bf16[32,4,129]{2,1,0:T(4,128)(2,1)} %reduce_sum.173), calls=%async_computation.5 | async-start | bytes 131072 | tf_op jit(solution)/shard_map/all_to_all | solution.py:68
where the time goes:
time: 187 us; the launch traced here: 186 us
  local copies, waits for them, and re-layouts  49.5 us (26%)
  starting transfers between devices  46.2 us (25%)
  waiting for transfers between devices  45.7 us (24%)
  blocking collectives  24.1 us (13%)
  matrix products  11.7 us (6%)
  other arithmetic  7.51 us (4%)
    all_to_all x6, starting transfers between devices, copy_for_each(): lax.all_to_all(jnp.broadcast_to(shard[None], (size, *shard.shape)), axis,...  35.8 us
    all_to_all x6, waiting for transfers between devices, copy_for_each(): lax.all_to_all(jnp.broadcast_to(shard[None], (size, *shard.shape)), axis,...  28.2 us
    all_to_all x2, blocking collectives, copy_for_each(): lax.all_to_all(jnp.broadcast_to(shard[None], (size, *shard.shape)), axis,...  24.1 us
    unnamed x92, local copies, waits for them, and re-layouts  17.9 us
    another operation x20, local copies, waits for them, and re-layouts, head_state(): total_all = jnp.stack(totals, axis=1).reshape(rows * kv_heads * group)  9.47 us
    all_to_all x1, waiting for transfers between devices, sum_at_owner(): lax.all_to_all(tiles, axis, split_axis=0, concat_axis=0, tiled=True)  8.86 us
    all_to_all x1, waiting for transfers between devices, summed_rows(): lax.all_to_all(own.astype(jnp.bfloat16), far, 0, 0, tiled=True)  8.67 us
    another operation x20, local copies, waits for them, and re-layouts, head_state(): peak_all = jnp.stack(peaks, axis=1).reshape(rows * kv_heads * group)  6.74 us
  transfers between devices with their start and end apart: 8, of which 7 were waited for; matrix products, arithmetic and copies ran while one was open for 21% of the time, Pallas kernels for 0%

commit v1 on v0

v1 whole, which is shorter than its diff:
```python
import functools

import jax
import jax.numpy as jnp
from jax import lax
from jax.experimental import pallas as pl
from jax.experimental.pallas import tpu as pltpu
from jax.sharding import Mesh
from jax.sharding import PartitionSpec as P

H = 64
KVH = 8
HD = 128
ROWS = 16
ALL = ("y", "z", "x", "c")
NEAR = ("y", "x", "c")
LOG2E = 1.4426950408889634
NONE = -1e30
HIDDEN = -2e30
F32 = jnp.float32
BF16 = jnp.bfloat16
VMEM = pl.BlockSpec(memory_space=pltpu.VMEM)
SMEM = pl.BlockSpec(memory_space=pltpu.SMEM)
NT = (((1,), (1,)), ((), ()))


def call(body, name, out_shape, *args, specs=None, scratch=()):
    return pl.pallas_call(
        body,
        name=name,
        out_shape=out_shape,
        in_specs=specs or [VMEM] * len(args),
        out_specs=jax.tree.map(lambda _: VMEM, out_shape),
        scratch_shapes=scratch,
    )(*args)


def lanes(shape):
    return lax.broadcasted_iota(jnp.int32, shape, len(shape) - 1)


def move(value, by):
    by %= value.shape[-1]
    return pltpu.roll(value, by, value.ndim - 1) if by else value


def exchange(tiles, axes):
    return lax.all_to_all(tiles, axes, 0, 0, tiled=True)


def rope_tables(positions):
    half = HD // 2
    index = jnp.arange(half, dtype=jnp.int32)
    inverse = jnp.power(jnp.float32(1000000.0), -2.0 * index.astype(jnp.float32) / HD)
    section = jnp.where(index < HD // 8, 0, jnp.where(index < 5 * HD // 16, 1, 2))
    chosen = jnp.where(
        section[None, :] == 0,
        positions[0][:, None],
        jnp.where(section[None, :] == 1, positions[1][:, None], positions[2][:, None]),
    )
    angle = chosen.astype(jnp.float32) * inverse[None, :]
    cosine, sine = (jnp.cos(angle), jnp.sin(angle))
    return jnp.stack(
        [jnp.concatenate([cosine, cosine], 1), jnp.concatenate([sine, sine], 1)], axis=0
    )


def pack_body(q_ref, k_ref, v_ref, out_ref):
    fill = jnp.zeros((ROWS, 128 - 40), F32)
    tile = jnp.concatenate(
        [q_ref[...].astype(F32), k_ref[...].astype(F32), v_ref[...].astype(F32), fill], axis=1
    ).astype(BF16)
    for d in range(out_ref.shape[0]):
        out_ref[d] = tile


def regroup_body(in_ref, out_ref):
    lane = lanes((ROWS, 128))
    tiles = [in_ref[s].astype(F32) for s in range(16)]
    rows = []
    for m in range(4):
        dense = tiles[4 * m]
        for i in range(1, 4):
            dense = jnp.where(lane < 32 * i, dense, move(tiles[4 * m + i], 32 * i))
        rows.append(dense.astype(BF16))
    kv = jnp.zeros((ROWS, 128), F32)
    for s in range(16):
        z, c = divmod(s, 2)
        at = (z % 4) * 32 + (z // 4) * 8 + c * 4
        kv = jnp.where((lane >= at) & (lane < at + 4), move(tiles[s], at - 32), kv)
        kv = jnp.where((lane >= at + 16) & (lane < at + 20), move(tiles[s], at + 16 - 36), kv)
    rows.append(kv.astype(BF16))
    for d in range(out_ref.shape[0]):
        for n, r in enumerate(rows):
            out_ref[d, n * ROWS : (n + 1) * ROWS, :] = r


def turn_body(v_ref, out_ref):
    for g in range(KVH):
        out_ref[g] = v_ref[:, g * HD : (g + 1) * HD].T


def split_pair(value):
    high = value.astype(BF16).astype(F32)
    return high, (value - high).astype(BF16).astype(F32)


def state_rows(peak, total):
    row = lax.broadcasted_iota(jnp.int32, (8, 128), 0)
    parts = (*split_pair(peak), *split_pair(total))
    tile = jnp.zeros((8, 128), F32)
    for n, part in enumerate(parts):
        tile = jnp.where(row == n, part, tile)
    return tile.astype(BF16)


def attend_body(own_ref, in_ref, rope_ref, bias_ref, span_bias_ref, k_ref, vt_ref, out_ref, q_ref):
    lane = lanes((ROWS, 128))
    cosine, sine = rope_ref[0], rope_ref[1]
    signed = jnp.where(lane < 64, -sine, sine)
    for y in range(4):
        for m in range(4):
            for p in range(2):
                a = in_ref[y * 4 + 2 * p, m * ROWS : (m + 1) * ROWS, :].astype(F32)
                b = in_ref[y * 4 + 2 * p + 1, m * ROWS : (m + 1) * ROWS, :].astype(F32)
                a, b = a * cosine - b * sine, b * cosine + a * sine
                for n in range(2):
                    head = y * 16 + 4 * m + 2 * n + p
                    if n == 0:
                        whole = jnp.where(lane < 64, a, move(b, 64))
                    else:
                        whole = jnp.where(lane < 64, move(a, 64), b)
                    q_ref[head * ROWS : (head + 1) * ROWS, :] = whole.astype(BF16)
    factor = LOG2E / HD**0.5
    for g in range(KVH):
        y, upper = divmod(g, 2)
        found = []
        for kind in (upper, 2 + upper):
            value = jnp.zeros((ROWS, 128), F32)
            for x in range(4):
                tile = in_ref[y * 4 + x, 4 * ROWS : 5 * ROWS, :].astype(F32)
                value = jnp.where((lane // 8) % 4 == x, move(tile, 8 * (x - kind)), value)
            found.append(value)
        span_k = (found[0] * cosine + move(found[0], 64) * signed).astype(BF16)
        span_v = found[1].astype(BF16)
        q = q_ref[g * 128 : (g + 1) * 128, :]
        k = k_ref[:, g * HD : (g + 1) * HD]
        absent = jnp.where(own_ref[0] == g, 0.0, HIDDEN)
        s = lax.dot_general(k, q, NT, preferred_element_type=F32) * factor + bias_ref[...]
        t = lax.dot_general(span_k, q, NT, preferred_element_type=F32) * factor
        t = t + (span_bias_ref[...] + absent)
        peak = jnp.maximum(
            jnp.maximum(jnp.max(s, axis=0, keepdims=True), jnp.max(t, axis=0, keepdims=True)),
            NONE,
        )
        high, low = split_pair(peak)
        peak = high + low
        s = jnp.exp2(s - peak)
        t = jnp.exp2(t - peak)
        total = jnp.sum(s, axis=0, keepdims=True) + jnp.sum(t, axis=0, keepdims=True)
        out = jnp.dot(vt_ref[g], s.astype(BF16), preferred_element_type=F32)
        out = out + lax.dot_general(
            span_v, t.astype(BF16), (((0,), (0,)), ((), ())), preferred_element_type=F32
        )
        out = out.astype(BF16)
        state = state_rows(peak, total)
        for n in range(4):
            out_ref[g * 4 + n, 0:32, :] = out[n * 32 : (n + 1) * 32]
            out_ref[g * 4 + n, 32:40, :] = state


def merged(in_ref):
    count = in_ref.shape[0]
    peaks, totals = [], []
    for n in range(count):
        state = in_ref[n, 32:40, :].astype(F32)
        peaks.append(state[0:1] + state[1:2])
        totals.append(state[2:3] + state[3:4])
    peak = functools.reduce(jnp.maximum, peaks)
    out = jnp.zeros((32, 128), F32)
    total = jnp.zeros((1, 128), F32)
    for n in range(count):
        factor = jnp.exp2(peaks[n] - peak)
        out = out + in_ref[n, 0:32, :].astype(F32) * factor
        total = total + totals[n] * factor
    return out, peak, total


def merge_body(in_ref, out_ref):
    out, peak, total = merged(in_ref)
    out = out.astype(BF16)
    state = state_rows(peak, total)
    for d in range(out_ref.shape[0]):
        out_ref[d, 0:32, :] = out
        out_ref[d, 32:40, :] = state


def finish_body(in_ref, out_ref):
    out, _, total = merged(in_ref)
    out = (out / total).astype(BF16)
    for d in range(out_ref.shape[0]):
        out_ref[d] = out


def place_body(in_ref, out_ref):
    eye = jnp.where(
        lax.broadcasted_iota(jnp.int32, (128, 128), 0) == lanes((128, 128)), 1.0, 0.0
    ).astype(BF16)
    for g in range(KVH):
        block = in_ref[g * 4 : (g + 1) * 4].reshape(128, 128)
        block = lax.dot_general(eye, block, NT, preferred_element_type=F32).astype(BF16)
        for i in range(8):
            at = (g * 8 + i) * HD
            out_ref[:, at : at + HD] = block[i * ROWS : (i + 1) * ROWS]


def per_device(
    queries,
    span_keys,
    span_values,
    positions,
    span_segments,
    cache_keys,
    cache_values,
    cache_segments,
):
    shape = jax.ShapeDtypeStruct
    tiles = call(pack_body, "pack", shape((16, ROWS, 128), BF16), queries, span_keys, span_values)
    tiles = exchange(tiles, ("z", "c"))
    tiles = call(regroup_body, "regroup", shape((16, 5 * ROWS, 128), BF16), tiles)
    tiles = exchange(tiles, ("y", "x"))

    rope = rope_tables(positions)
    turned = call(turn_body, "turn", shape((KVH, HD, 512), BF16), cache_values)
    columns = jnp.tile(span_segments, 8)[None, :]
    bias = jnp.where(cache_segments[:, None] == columns, 0.0, HIDDEN).astype(F32)
    index = jnp.arange(ROWS, dtype=jnp.int32)
    seen = (span_segments[:, None] == span_segments[None, :]) & (index[:, None] <= index[None, :])
    span_bias = jnp.tile(jnp.where(seen, 0.0, HIDDEN).astype(F32), (1, 8))
    own = lax.axis_index(ALL).astype(jnp.int32).reshape(1)

    parts = call(
        attend_body,
        "attend",
        shape((32, 40, 128), BF16),
        own,
        tiles,
        rope,
        bias,
        span_bias,
        cache_keys,
        turned,
        specs=[SMEM] + [VMEM] * 6,
        scratch=[pltpu.VMEM((H * ROWS, HD), BF16)],
    )
    parts = exchange(parts, NEAR)
    parts = call(merge_body, "merge", shape((8, 40, 128), BF16), parts)
    parts = exchange(parts, ("z",))
    whole = call(finish_body, "finish", shape((32, 32, 128), BF16), parts)
    whole = exchange(whole, NEAR)
    return call(place_body, "place", shape((ROWS, H * HD), BF16), whole)


def solution(mesh):
    split = Mesh(mesh.devices.reshape(4, 8, 4, 2), ALL)
    return jax.shard_map(
        per_device,
        mesh=split,
        in_specs=(
            P(None, ALL),
            P(None, ALL),
            P(None, ALL),
            P(),
            P(),
            P(ALL, None),
            P(ALL, None),
            P(ALL),
        ),
        out_specs=P(),
        check_vma=False,
    )
```

time: 187 us -> 92.6 us (0.50)
  local copies, waits for them, and re-layouts: 49.5 us -> 5.42 us
  waiting for transfers between devices: 45.7 us -> 10.5 us
  starting transfers between devices: 46.2 us -> 16.7 us
  blocking collectives: 24.1 us -> 41.2 us
  Pallas kernels: 0 us -> 16.1 us
  matrix products: 11.7 us -> 0 us
  other arithmetic: 7.51 us -> 1.73 us
    all_to_all x8 -> x2, waiting for transfers between devices: 45.7 us -> 10.5 us  [exchange(): return lax.all_to_all(tiles, axes, 0, 0, tiled=True)]
    all_to_all x8 -> x2, starting transfers between devices: 46.2 us -> 16.7 us  [exchange(): return lax.all_to_all(tiles, axes, 0, 0, tiled=True)]
    all_to_all x2 -> x3, blocking collectives: 24.1 us -> 41.2 us  [exchange(): return lax.all_to_all(tiles, axes, 0, 0, tiled=True)]
    another operation x45 -> x3, local copies, waits for them, and re-layouts: 17.4 us -> 0.69 us  [the longest x2 0.69 us: per_device(): span_bias = jnp.tile(jnp.where(seen, 0.0, HIDDEN).astype(F32), (1, 8))]
    pallas_call x0 -> x7, Pallas kernels: none -> 16.1 us  [call(): pl.pallas_call(body, name=name, out_shape=out_shape, in_specs=specs or [V...]
    unnamed x92 -> x14, local copies, waits for them, and re-layouts: 17.9 us -> 4.64 us
    dot_general x32 -> x0, matrix products: 11.7 us -> none  [the longest x16 6.3 us: head_state(): jnp.dot(weights.astype(jnp.bfloat16).reshape(rows * group, -1), value_col...]
    convert_element_type x13 -> x0, local copies, waits for them, and re-layouts: 7.23 us -> none  [the longest x8 5.02 us: head_state(): weights.astype(jnp.bfloat16).reshape(rows * group, -1)]
  transfers between devices with their start and end apart: 8 -> 2, of which waited for: 7 -> 2; matrix products, arithmetic and copies ran while one was open for 21% -> 3% of each run, Pallas kernels for 0% -> 3%
where the time goes in v1:
time: 92.6 us; the launch traced here: 91.8 us
  blocking collectives  41.2 us (44%)
  starting transfers between devices  16.7 us (18%)
  Pallas kernels  16.1 us (17%)
  waiting for transfers between devices  10.5 us (11%)
  local copies, waits for them, and re-layouts  5.42 us (6%)
  other arithmetic  1.73 us (2%)
    all_to_all x3, blocking collectives, exchange(): return lax.all_to_all(tiles, axes, 0, 0, tiled=True)  41.2 us
    all_to_all x2, starting transfers between devices, exchange(): return lax.all_to_all(tiles, axes, 0, 0, tiled=True)  16.7 us
    pallas_call x7, Pallas kernels, call(): pl.pallas_call(body, name=name, out_shape=out_shape, in_specs=specs or [V...  16.1 us
    all_to_all x2, waiting for transfers between devices, exchange(): return lax.all_to_all(tiles, axes, 0, 0, tiled=True)  10.5 us
    unnamed x14, local copies, waits for them, and re-layouts  4.64 us
  transfers between devices with their start and end apart: 2, of which 2 were waited for; matrix products, arithmetic and copies ran while one was open for 3% of the time, Pallas kernels for 3%

profile of v1, /device:TPU:1, one launch (start us, length us, event | category | flops | bytes accessed | tf_op | source)
XLA Modules:
  0.0 91.8 jit_solution(15835099042869974409)
XLA Ops:
  0.0 0.0 copy-start.5
  0.0 1.4 %copy.9.k_ref = bf16[16,4]{1,0:T(8,128)(2,1)} copy(bf16[16,4]{0,1:T(4,128)(2,1)} %param.9) | data formatting | bytes 256 | tf_op args[1]
  1.4 0.0 copy-done.5
  1.4 0.7 copy.10.v_ref
  2.0 1.4 %pack.1 = bf16[16,16,128]{2,1,0:T(8,128)(2,1)} custom-call(bf16[16,32]{1,0:T(8,128)(2,1)} %q_ref.1, bf16[16,4]{1,0:T(8,128)(2,1)} %copy.9.k_ref, bf16[16,4]{1,0:T(8,128)(2,1)} %copy.10.v_ref), custom_call_target="tpu_custom_call" | custom-call | tf_op jit(solution)/shard_map/pack/pallas_call | solution.py:28
  3.4 10.0 %all-to-all-start = ((bf16[16,16,128]{2,1,0:T(8,128)(2,1)}), bf16[16,16,128]{2,1,0:T(8,128)(2,1)S(1)}, u32[]{:S(2)}, u32[]{:S(2)}) async-start(bf16[16,16,128]{2,1,0:T(8,128)(2,1)} %pack.1), calls=%async_computation | async-start | bytes 131072 | tf_op jit(solution)/shard_map/all_to_all | solution.py:48
  13.4 0.0 copy-start.4
  13.5 0.6 copy-done.4
  14.1 0.0 copy-start.2
  14.1 0.1 fusion.1
  14.2 0.5 copy-done.2
  14.8 0.1 fusion.3
  14.8 0.1 eq.53
  14.9 0.7 tile.8.span_bias_ref
  15.6 2.5 %turn.1.vt_ref = bf16[8,128,512]{2,1,0:T(8,128)(2,1)} custom-call(bf16[512,1024]{1,0:T(8,128)(2,1)} %v_ref.2), custom_call_target="tpu_custom_call" | custom-call | tf_op jit(solution)/shard_map/turn/pallas_call | solution.py:28
  18.1 0.1 maximum_bitcast_fusion
  18.2 3.0 %all-to-all-done.in_ref = bf16[16,16,128]{2,1,0:T(8,128)(2,1)S(1)} async-done(((bf16[16,16,128]{2,1,0:T(8,128)(2,1)}), bf16[16,16,128]{2,1,0:T(8,128)(2,1)S(1)}, u32[]{:S(2)}, u32[]{:S(2)}) %all-to-all-start) | async-done | bytes 65568 | tf_op jit(solution)/shard_map/all_to_all | solution.py:48
  21.2 0.0 copy-start.1
  21.2 0.6 copy-done.1
  21.8 1.7 %regroup.1 = bf16[16,80,128]{2,1,0:T(8,128)(2,1)} custom-call(bf16[16,16,128]{2,1,0:T(8,128)(2,1)} %copy-done.1), custom_call_target="tpu_custom_call" | custom-call | tf_op jit(solution)/shard_map/regroup/pallas_call | solution.py:28
  23.5 6.8 %all-to-all-start.1 = ((bf16[16,80,128]{2,1,0:T(8,128)(2,1)}), bf16[16,80,128]{2,1,0:T(8,128)(2,1)S(1)}, u32[]{:S(2)}, u32[]{:S(2)}) async-start(bf16[16,80,128]{2,1,0:T(8,128)(2,1)} %regroup.1), calls=%async_computation.1 | async-start | bytes 655360 | tf_op jit(solution)/shard_map/all_to_all | solution.py:48
  30.3 0.0 copy-start.3
  30.3 0.6 pad_maximum_fusion.rope_ref
  30.9 0.1 copy-done.3
  31.0 0.8 compare_select_fusion.bias_ref
  31.8 7.6 %all-to-all-done.1.in_ref = bf16[16,80,128]{2,1,0:T(8,128)(2,1)S(1)} async-done(((bf16[16,80,128]{2,1,0:T(8,128)(2,1)}), bf16[16,80,128]{2,1,0:T(8,128)(2,1)S(1)}, u32[]{:S(2)}, u32[]{:S(2)}) %all-to-all-start.1) | async-done | bytes 327712 | tf_op jit(solution)/shard_map/all_to_all | solution.py:48
  39.4 0.0 copy-start
  39.4 0.7 copy-done
  40.1 5.2 %attend.1 = bf16[32,40,128]{2,1,0:T(8,128)(2,1)} custom-call(s32[1]{0:T(128)} %bitcast.own_ref, bf16[16,80,128]{2,1,0:T(8,128)(2,1)} %copy-done, f32[2,16,128]{2,1,0:T(8,128)} %pad_maximum_fusion.rope_ref, f32[512,128]{1,0:T(8,128)} %compare_select_fusion.bias_ref, f32[16,128]{1,0:T(8,128)} %tile.8.span_bias_ref, bf16[512,1024]{1,0:T(8,128)(2,1)} %k_ref.2, ...), custom_call_target="tpu_custom_call" | custom-call | tf_op jit(solution)/shard_map/attend/pallas_call | solution.py:28
  45.3 15.1 %all_to_all.25.in_ref = bf16[32,40,128]{2,1,0:T(8,128)(2,1)} all-to-all(bf16[32,40,128]{2,1,0:T(8,128)(2,1)} %attend.1), channel_id=1, replica_groups=mesh['y'=4,'z'=8,'x'=4,'c'=2] {'y','x','c'}, dimensions={0} | all-to-all | bytes 655360 | tf_op jit(solution)/shard_map/all_to_all | solution.py:48
  60.4 1.7 %merge.1 = bf16[8,40,128]{2,1,0:T(8,128)(2,1)} custom-call(bf16[32,40,128]{2,1,0:T(8,128)(2,1)} %all_to_all.25.in_ref), custom_call_target="tpu_custom_call" | custom-call | tf_op jit(solution)/shard_map/merge/pallas_call | solution.py:28
  62.1 11.4 %all_to_all.26.in_ref = bf16[8,40,128]{2,1,0:T(8,128)(2,1)} all-to-all(bf16[8,40,128]{2,1,0:T(8,128)(2,1)} %merge.1), channel_id=1, replica_groups=mesh['y'=4,'z'=8,'x'=4,'c'=2] {'z'}, dimensions={0} | all-to-all | bytes 163840 | tf_op jit(solution)/shard_map/all_to_all | solution.py:48
  73.5 1.6 %finish.1 = bf16[32,32,128]{2,1,0:T(8,128)(2,1)} custom-call(bf16[8,40,128]{2,1,0:T(8,128)(2,1)} %all_to_all.26.in_ref), custom_call_target="tpu_custom_call" | custom-call | tf_op jit(solution)/shard_map/finish/pallas_call | solution.py:28
  75.2 14.7 %all_to_all.27.in_ref = bf16[32,32,128]{2,1,0:T(8,128)(2,1)} all-to-all(bf16[32,32,128]{2,1,0:T(8,128)(2,1)} %finish.1), channel_id=1, replica_groups=mesh['y'=4,'z'=8,'x'=4,'c'=2] {'y','x','c'}, dimensions={0} | all-to-all | bytes 524288 | tf_op jit(solution)/shard_map/all_to_all | solution.py:48
  89.9 1.9 %place.1 = bf16[16,8192]{1,0:T(8,128)(2,1)} custom-call(bf16[32,32,128]{2,1,0:T(8,128)(2,1)} %all_to_all.27.in_ref), custom_call_target="tpu_custom_call" | custom-call | tf_op jit(solution)/shard_map/place/pallas_call | solution.py:28
  (6 shorter events, 0.0 us)
Async XLA Ops:
  0.0 1.4 %copy-start.5 = (bf16[16,4]{0,1:T(4,128)(2,1)S(1)}, bf16[16,4]{0,1:T(4,128)(2,1)}, u32[]{:S(2)}) copy-start(bf16[16,4]{0,1:T(4,128)(2,1)} %param.10) | copy-start | bytes 388
  3.4 17.7 %all-to-all-start = ((bf16[16,16,128]{2,1,0:T(8,128)(2,1)}), bf16[16,16,128]{2,1,0:T(8,128)(2,1)S(1)}, u32[]{:S(2)}, u32[]{:S(2)}) async-start(bf16[16,16,128]{2,1,0:T(8,128)(2,1)} %pack.1), calls=%async_computation | async-start | bytes 131072 | tf_op jit(solution)/shard_map/all_to_all | solution.py:48
  13.4 0.7 copy-start.4
  14.1 0.7 copy-start.2
  21.2 0.6 copy-start.1
  23.5 15.8 %all-to-all-start.1 = ((bf16[16,80,128]{2,1,0:T(8,128)(2,1)}), bf16[16,80,128]{2,1,0:T(8,128)(2,1)S(1)}, u32[]{:S(2)}, u32[]{:S(2)}) async-start(bf16[16,80,128]{2,1,0:T(8,128)(2,1)} %regroup.1), calls=%async_computation.1 | async-start | bytes 655360 | tf_op jit(solution)/shard_map/all_to_all | solution.py:48
  30.3 0.7 copy-start.3
  39.4 0.7 copy-start

commit v2 on v1

--- a/solution.py
+++ b/solution.py
@@ -24,7 +24,7 @@
 NT = (((1,), (1,)), ((), ()))
 
 
-def call(body, name, out_shape, *args, specs=None, scratch=()):
+def call(body, name, out_shape, *args, specs=None, scratch=(), limit=8 << 20):
     return pl.pallas_call(
         body,
         name=name,
@@ -32,6 +32,7 @@
         in_specs=specs or [VMEM] * len(args),
         out_specs=jax.tree.map(lambda _: VMEM, out_shape),
         scratch_shapes=scratch,
+        compiler_params=pltpu.CompilerParams(vmem_limit_bytes=limit),
     )(*args)
 
 
@@ -66,10 +67,17 @@
 
 
 def pack_body(q_ref, k_ref, v_ref, out_ref):
-    fill = jnp.zeros((ROWS, 128 - 40), F32)
-    tile = jnp.concatenate(
-        [q_ref[...].astype(F32), k_ref[...].astype(F32), v_ref[...].astype(F32), fill], axis=1
-    ).astype(BF16)
+    def spread(count, at):
+        shape = (count, 128)
+        hit = lanes(shape) == lax.broadcasted_iota(jnp.int32, shape, 0) + at
+        return jnp.where(hit, 1.0, 0.0).astype(BF16)
+
+    tile = jnp.dot(q_ref[...], spread(32, 0), preferred_element_type=F32)
+    for ref, at in ((k_ref, 32), (v_ref, 36)):
+        tile = tile + lax.dot_general(
+            ref[...], spread(4, at), (((0,), (0,)), ((), ())), preferred_element_type=F32
+        )
+    tile = tile.astype(BF16)
     for d in range(out_ref.shape[0]):
         out_ref[d] = tile
 
@@ -225,9 +233,12 @@
     cache_segments,
 ):
     shape = jax.ShapeDtypeStruct
-    tiles = call(pack_body, "pack", shape((16, ROWS, 128), BF16), queries, span_keys, span_values)
+    tiles = call(pack_body, "pack", shape((16, ROWS, 128), BF16), queries, span_keys.T, span_values.T)
     tiles = exchange(tiles, ("z", "c"))
     tiles = call(regroup_body, "regroup", shape((16, 5 * ROWS, 128), BF16), tiles)
+    tiles, cache_values, cache_segments, span_segments = lax.optimization_barrier(
+        (tiles, cache_values, cache_segments, span_segments)
+    )
     tiles = exchange(tiles, ("y", "x"))
 
     rope = rope_tables(positions)

time: 92.6 us -> 79 us (0.85)
  Pallas kernels: 16.1 us -> 5.82 us
  waiting for transfers between devices: 10.5 us -> 14.7 us
  blocking collectives: 41.2 us -> 37.2 us
  local copies, waits for them, and re-layouts: 5.42 us -> 3.45 us
  other arithmetic: 1.73 us -> 0.43 us
    pallas_call x7, Pallas kernels: 16.1 us -> 5.82 us  [call(): pl.pallas_call(body, name=name, out_shape=out_shape, in_specs=specs or [V...]
    all_to_all x2, waiting for transfers between devices: 10.5 us -> 14.7 us  [exchange(): return lax.all_to_all(tiles, axes, 0, 0, tiled=True)]
    all_to_all x3, blocking collectives: 41.2 us -> 37.2 us  [exchange(): return lax.all_to_all(tiles, axes, 0, 0, tiled=True)]
    unnamed x14, local copies, waits for them, and re-layouts: 4.64 us -> 2.48 us
  transfers between devices with their start and end apart: 2 -> 2, of which waited for: 2 -> 2; matrix products, arithmetic and copies ran while one was open for 3% -> 2% of each run, Pallas kernels for 3% -> 0%
where the time goes in v2:
time: 79 us; the launch traced here: 78.6 us
  blocking collectives  37.2 us (47%)
  starting transfers between devices  16.9 us (21%)
  waiting for transfers between devices  14.7 us (19%)
  Pallas kernels  5.82 us (7%)
  local copies, waits for them, and re-layouts  3.45 us (4%)
    all_to_all x3, blocking collectives, exchange(): return lax.all_to_all(tiles, axes, 0, 0, tiled=True)  37.2 us
    all_to_all x2, starting transfers between devices, exchange(): return lax.all_to_all(tiles, axes, 0, 0, tiled=True)  16.9 us
    all_to_all x2, waiting for transfers between devices, exchange(): return lax.all_to_all(tiles, axes, 0, 0, tiled=True)  14.7 us
    pallas_call x7, Pallas kernels, call(): pl.pallas_call(body, name=name, out_shape=out_shape, in_specs=specs or [V...  5.82 us
    unnamed x14, local copies, waits for them, and re-layouts  2.48 us
  transfers between devices with their start and end apart: 2, of which 2 were waited for; matrix products, arithmetic and copies ran while one was open for 2% of the time, Pallas kernels for 0%

profile of v2, /device:TPU:1, one launch (start us, length us, event | category | flops | bytes accessed | tf_op | source)
XLA Modules:
  0.0 78.6 jit_solution(8567551973507486698)
XLA Ops:
  0.0 0.0 copy-start.1
  0.0 0.0 copy-start.2
  0.0 0.8 copy-done.2
  0.8 0.0 copy-start.3
  0.8 0.7 copy-done.3
  1.5 0.0 copy-start.4
  1.5 0.7 copy-done.4
  2.1 0.8 %pack.1 = bf16[16,16,128]{2,1,0:T(8,128)(2,1)} custom-call(bf16[16,32]{1,0:T(8,128)(2,1)S(1)} %copy-done.2, bf16[4,16]{1,0:T(4,128)(2,1)S(1)} %bitcast.13, bf16[4,16]{1,0:T(4,128)(2,1)S(1)} %bitcast.14), custom_call_target="tpu_custom_call" | custom-call | tf_op jit(solution)/shard_map/pack/pallas_call | solution.py:28
  2.9 10.0 %all-to-all-start = ((bf16[16,16,128]{2,1,0:T(8,128)(2,1)}), bf16[16,16,128]{2,1,0:T(8,128)(2,1)S(1)}, u32[]{:S(2)}, u32[]{:S(2)}) async-start(bf16[16,16,128]{2,1,0:T(8,128)(2,1)} %pack.1), calls=%async_computation | async-start | bytes 131072 | tf_op jit(solution)/shard_map/all_to_all | solution.py:49
  13.0 0.8 %slice_bitcast_fusion.2 = (s32[16]{0:T(128)S(1)}, s32[16]{0:T(128)S(1)}, s32[16]{0:T(128)S(1)}) fusion(s32[3,16]{1,0:T(4,128)} %param.11), kind=kLoop, calls=%fused_computation.15 | loop fusion | bytes 384 | tf_op jit(solution)/shard_map/jit(_where)/broadcast_in_dim | solution.py:57
  13.8 0.1 fusion.1
  13.9 0.1 maximum_bitcast_fusion
  14.0 6.7 %all-to-all-done.in_ref = bf16[16,16,128]{2,1,0:T(8,128)(2,1)S(1)} async-done(((bf16[16,16,128]{2,1,0:T(8,128)(2,1)}), bf16[16,16,128]{2,1,0:T(8,128)(2,1)S(1)}, u32[]{:S(2)}, u32[]{:S(2)}) %all-to-all-start) | async-done | bytes 65568 | tf_op jit(solution)/shard_map/all_to_all | solution.py:49
  20.7 0.8 %regroup.1 = bf16[16,80,128]{2,1,0:T(8,128)(2,1)} custom-call(bf16[16,16,128]{2,1,0:T(8,128)(2,1)S(1)} %all-to-all-done.in_ref), custom_call_target="tpu_custom_call" | custom-call | tf_op jit(solution)/shard_map/regroup/pallas_call | solution.py:28
  21.5 0.0 copy-start.5
  21.5 6.9 %all-to-all-start.1 = ((bf16[16,80,128]{2,1,0:T(8,128)(2,1)}), bf16[16,80,128]{2,1,0:T(8,128)(2,1)S(1)}, u32[]{:S(2)}, u32[]{:S(2)}) async-start(bf16[16,80,128]{2,1,0:T(8,128)(2,1)} %regroup.1), calls=%async_computation.1 | async-start | bytes 655360 | tf_op jit(solution)/shard_map/all_to_all | solution.py:49
  28.4 0.0 copy-done.5
  28.4 0.1 fusion.3
  28.5 0.1 eq.53
  28.6 0.1 tile.8.span_bias_ref
  28.7 0.0 copy-done.1
  28.7 0.0 copy-start.6
  28.7 0.0 copy-start
  28.7 0.3 turn.1.vt_ref
  29.0 0.3 copy-done.6
  29.4 0.1 compare_select_fusion.bias_ref
  29.5 8.0 %all-to-all-done.1.in_ref = bf16[16,80,128]{2,1,0:T(8,128)(2,1)S(1)} async-done(((bf16[16,80,128]{2,1,0:T(8,128)(2,1)}), bf16[16,80,128]{2,1,0:T(8,128)(2,1)S(1)}, u32[]{:S(2)}, u32[]{:S(2)}) %all-to-all-start.1) | async-done | bytes 327712 | tf_op jit(solution)/shard_map/all_to_all | solution.py:49
  37.5 0.0 copy-done
  37.5 2.7 %attend.1 = bf16[32,40,128]{2,1,0:T(8,128)(2,1)S(1)} custom-call(s32[1]{0:T(128)} %bitcast.own_ref, bf16[16,80,128]{2,1,0:T(8,128)(2,1)S(1)} %all-to-all-done.1.in_ref, f32[2,16,128]{2,1,0:T(8,128)S(1)} %pad_maximum_fusion.rope_ref, f32[512,128]{1,0:T(8,128)S(1)} %compare_select_fusion.bias_ref, f32[16,128]{1,0:T(8,128)S(1)} %tile.8.span_bias_ref, ...), custom_call_target="tpu_custom_call" | custom-call | tf_op jit(solution)/shard_map/attend/pallas_call | solution.py:28
  40.2 13.7 %all_to_all.25.in_ref = bf16[32,40,128]{2,1,0:T(8,128)(2,1)S(1)} all-to-all(bf16[32,40,128]{2,1,0:T(8,128)(2,1)S(1)} %attend.1), channel_id=1, replica_groups=mesh['y'=4,'z'=8,'x'=4,'c'=2] {'y','x','c'}, dimensions={0} | all-to-all | bytes 655360 | tf_op jit(solution)/shard_map/all_to_all | solution.py:49
  53.9 0.1 merge.1
  54.0 9.8 %all_to_all.26.in_ref = bf16[8,40,128]{2,1,0:T(8,128)(2,1)S(1)} all-to-all(bf16[8,40,128]{2,1,0:T(8,128)(2,1)S(1)} %merge.1), channel_id=1, replica_groups=mesh['y'=4,'z'=8,'x'=4,'c'=2] {'z'}, dimensions={0} | all-to-all | bytes 163840 | tf_op jit(solution)/shard_map/all_to_all | solution.py:49
  63.8 0.1 finish.1
  63.9 13.7 %all_to_all.27.in_ref = bf16[32,32,128]{2,1,0:T(8,128)(2,1)S(1)} all-to-all(bf16[32,32,128]{2,1,0:T(8,128)(2,1)S(1)} %finish.1), channel_id=1, replica_groups=mesh['y'=4,'z'=8,'x'=4,'c'=2] {'y','x','c'}, dimensions={0} | all-to-all | bytes 524288 | tf_op jit(solution)/shard_map/all_to_all | solution.py:49
  77.6 1.0 %place.1 = bf16[16,8192]{1,0:T(8,128)(2,1)} custom-call(bf16[32,32,128]{2,1,0:T(8,128)(2,1)S(1)} %all_to_all.27.in_ref), custom_call_target="tpu_custom_call" | custom-call | tf_op jit(solution)/shard_map/place/pallas_call | solution.py:28
  (6 shorter events, 0.0 us)
Async XLA Ops:
  0.0 28.7 %copy-start.1 = (bf16[512,1024]{1,0:T(8,128)(2,1)S(1)}, bf16[512,1024]{1,0:T(8,128)(2,1)}, u32[]{:S(2)}) copy-start(bf16[512,1024]{1,0:T(8,128)(2,1)} %v_ref) | copy-start | bytes 3145732
  0.0 0.8 copy-start.2
  0.8 0.7 copy-start.3
  1.5 0.7 copy-start.4
  2.9 17.7 %all-to-all-start = ((bf16[16,16,128]{2,1,0:T(8,128)(2,1)}), bf16[16,16,128]{2,1,0:T(8,128)(2,1)S(1)}, u32[]{:S(2)}, u32[]{:S(2)}) async-start(bf16[16,16,128]{2,1,0:T(8,128)(2,1)} %pack.1), calls=%async_computation | async-start | bytes 131072 | tf_op jit(solution)/shard_map/all_to_all | solution.py:49
  21.5 6.9 %copy-start.5 = (s32[16]{0:T(128)S(1)}, s32[16]{0:T(128)}, u32[]{:S(2)}) copy-start(s32[16]{0:T(128)} %param.12) | copy-start | bytes 196
  21.5 16.0 %all-to-all-start.1 = ((bf16[16,80,128]{2,1,0:T(8,128)(2,1)}), bf16[16,80,128]{2,1,0:T(8,128)(2,1)S(1)}, u32[]{:S(2)}, u32[]{:S(2)}) async-start(bf16[16,80,128]{2,1,0:T(8,128)(2,1)} %regroup.1), calls=%async_computation.1 | async-start | bytes 655360 | tf_op jit(solution)/shard_map/all_to_all | solution.py:49
  28.7 0.7 copy-start.6
  28.7 8.8 %copy-start = (bf16[512,1024]{1,0:T(8,128)(2,1)S(1)}, bf16[512,1024]{1,0:T(8,128)(2,1)}, u32[]{:S(2)}) copy-start(bf16[512,1024]{1,0:T(8,128)(2,1)} %k_ref.1) | copy-start | bytes 3145732

commit v3 on v1

v3 whole, which is shorter than its diff:
```python
import functools

import jax
import jax.numpy as jnp
from jax import lax
from jax.experimental import pallas as pl
from jax.experimental.pallas import tpu as pltpu
from jax.sharding import Mesh
from jax.sharding import PartitionSpec as P

H = 64
HD = 128
ROWS = 16
ALL = ("y", "z", "x", "c")
CHIPS = ("y", "z", "x")
PLANE = ("y", "x")
LOG2E = 1.4426950408889634
NONE = -1e30
HIDDEN = -2e30
F32 = jnp.float32
BF16 = jnp.bfloat16
VMEM = pl.BlockSpec(memory_space=pltpu.VMEM)
HBM = pl.BlockSpec(memory_space=pltpu.HBM)
NT = (((1,), (1,)), ((), ()))


def call(body, out_shape, *args, specs=None, scratch=(), limit=8 << 20):
    return pl.pallas_call(
        body,
        out_shape=out_shape,
        in_specs=specs or [VMEM] * len(args),
        out_specs=jax.tree.map(lambda _: VMEM, out_shape),
        scratch_shapes=scratch,
        compiler_params=pltpu.CompilerParams(vmem_limit_bytes=limit),
    )(*args)


def lanes(shape):
    return lax.broadcasted_iota(jnp.int32, shape, len(shape) - 1)


def move(value, by):
    by %= value.shape[-1]
    return pltpu.roll(value, by, value.ndim - 1) if by else value


def exchange(tiles, axes):
    return lax.all_to_all(tiles, axes, 0, 0, tiled=True)


def swap(value):
    return lax.ppermute(value, "c", ((0, 1), (1, 0)))


def rows_of(shape):
    return lax.broadcasted_iota(jnp.int32, shape, 0)


TN = (((0,), (0,)), ((), ()))


def dot(a, b, dims):
    return lax.dot_general(a, b, dims, preferred_element_type=F32)


def where_one(hit):
    return jnp.where(hit, 1.0, 0.0).astype(BF16)


def fetch(sources, targets, sems):
    return [pltpu.make_async_copy(a, b, sems.at[n]) for n, (a, b) in enumerate(zip(sources, targets))]


def pack_body(*refs):
    sources, (keep_ref, send_ref, pos_ref, seg_ref) = refs[:6], refs[6:10]
    q_ref, k_ref, v_ref, s_ref, sems = refs[10:]
    copies = fetch(sources, (q_ref, k_ref, v_ref, s_ref, pos_ref, seg_ref), sems)
    for copy in copies:
        copy.start()
    for copy in copies:
        copy.wait()
    c = lax.axis_index("c")

    def spread(count, at):
        return where_one(lanes((count, 128)) == rows_of((count, 128)) + at)

    q = jnp.dot(q_ref[...], spread(32, c * 32), preferred_element_type=F32)
    kv = jnp.zeros((8, 128), F32)
    for ref, at in ((k_ref, 64), (v_ref, 96)):
        kv = kv + dot(ref[...], spread(4, at + c * 4), TN)[0:8]
        kv = kv + dot(ref[...], spread(4, at + 16 + c * 4), TN)[8:16]
    low, high = q[0:8] + kv, q[8:16] + kv
    first = c == 0
    segments = s_ref[...].astype(F32).astype(BF16)
    for ref, tile in (
        (keep_ref, jnp.where(first, low, high)),
        (send_ref, jnp.where(first, high, low)),
    ):
        ref[0:8, :] = tile.astype(BF16)
        ref[8:12, :] = segments
        ref[12:16, :] = jnp.zeros((4, 128), BF16)


def spread_body(keep_ref, came_ref, out_ref):
    lane = lanes((8, 128))
    mine = jnp.where(lane < 64, lane // 32, (lane // 4) % 2) == lax.axis_index("c")
    tile = jnp.where(mine, keep_ref[0:8, :].astype(F32), came_ref[0:8, :].astype(F32)).astype(BF16)
    for d in range(out_ref.shape[0]):
        out_ref[d] = tile


def turn(angle):
    quarter = jnp.floor(angle * 0.6366197723675814 + 0.5)
    rest = angle - quarter * 1.5703125
    rest = rest - quarter * 4.837512969970703e-4
    rest = rest - quarter * 7.549789948768648e-8
    square = rest * rest
    sine = -1.9515295891e-4 * square + 8.3321608736e-3
    sine = (sine * square - 1.6666654611e-1) * square * rest + rest
    cosine = 2.443315711809948e-5 * square - 1.388731625493765e-3
    cosine = (cosine * square + 4.166664568298827e-2) * square * square - 0.5 * square + 1.0
    which = quarter.astype(jnp.int32) % 4
    odd = which % 2 == 1
    cosine, sine = jnp.where(odd, sine, cosine), jnp.where(odd, cosine, sine)
    cosine = jnp.where((which == 1) | (which == 2), -cosine, cosine)
    sine = jnp.where(which >= 2, -sine, sine)
    return cosine, sine


def rope_tables(positions):
    shape = (3, 128)
    index = lanes(shape) % 64
    section = jnp.where(index < 16, 0, jnp.where(index < 40, 1, 2))
    chosen = where_one(section == rows_of(shape))
    high = positions // 64
    low = positions - high * 64
    position = 64.0 * dot(high.astype(F32).astype(BF16), chosen, TN)
    position = position + dot(low.astype(F32).astype(BF16), chosen, TN)
    index = lanes((ROWS, 128)) % 64
    inverse = jnp.ones((ROWS, 128), F32)
    for bit in range(6):
        step = 1000000.0 ** (-2.0 * 2**bit / HD)
        inverse = jnp.where((index // 2**bit) % 2 == 1, inverse * step, inverse)
    cosine, sine = turn(position * inverse)
    return cosine, jnp.where(lanes((ROWS, 128)) < 64, -sine, sine)


def rotate(value, cosine, sine):
    return value * cosine + move(value, 64) * sine


def split_pair(value):
    high = value.astype(BF16).astype(F32)
    return high, (value - high).astype(BF16).astype(F32)


def state_rows(peak, total):
    row = rows_of((8, 128))
    parts = (*split_pair(peak), *split_pair(total))
    tile = jnp.zeros((8, 128), F32)
    for n, part in enumerate(parts):
        tile = jnp.where(row == n, part, tile)
    return tile.astype(BF16)


def attend_body(
    in_ref, keep_ref, came_ref, pos_ref, seg_ref, k2_ref, v2_ref, k_hbm, v_hbm,
    out_ref, q_ref, rope_ref, bias_ref, k_ref, v_ref, sems,
):
    copies = fetch((k_hbm, v_hbm), (k_ref, v_ref), sems)
    for copy in copies:
        copy.start()
    c = lax.axis_index("c")
    y0 = lax.axis_index("y")
    duty = (lax.axis_index("z") == 0) & (lax.axis_index("x") == 0)
    lane = lanes((8, 128))
    cosine, sine = rope_tables(pos_ref[...])
    rope_ref[0] = cosine
    rope_ref[1] = sine
    half = pl.ds(pl.multiple_of(c * 8, 8), 8)
    half_cosine, half_sine = rope_ref[0, half, :], rope_ref[1, half, :]

    for y in range(4):
        q_ref[y] = jnp.zeros((128, 256), BF16)
        for z in range(8):
            upper = z // 4
            for p in range(2):
                n = (y * 8 + z) * 4 + 2 * p
                a, b = in_ref[n].astype(F32), in_ref[n + 1].astype(F32)
                whole = jnp.where(lane < 64, a, move(b, 64))
                at = upper * 64 + ((z % 4) * 2 + p) * 8
                q_ref[y, at : at + 8, upper * 128 : (upper + 1) * 128] = rotate(
                    whole, half_cosine, half_sine
                ).astype(BF16)

    found = []
    for kind in range(2):
        for upper in range(2):
            parts = []
            for late in range(2):
                value = jnp.zeros((8, 128), F32)
                for z in range(4):
                    for x in range(4):
                        tile = in_ref[(y0 * 8 + upper * 4 + z) * 4 + x].astype(F32)
                        at = z * 32 + x * 8
                        value = jnp.where(
                            (lane >= at) & (lane < at + 8),
                            move(tile, at - 64 - kind * 32 - late * 16),
                            value,
                        )
                parts.append(value)
            found.append(jnp.concatenate(parts, axis=0))
    span_k = jnp.concatenate([rotate(f, cosine, sine) for f in found[:2]], axis=1).astype(BF16)
    span_v = jnp.concatenate(found[2:], axis=1).astype(BF16)

    row_of_lane = c * 8 + lanes((ROWS, 128)) % 8
    pick = where_one(rows_of((ROWS, 128)) == row_of_lane)
    kinds = where_one(rows_of((8, ROWS)) == seg_ref[...])
    wanted = dot(kinds, pick, (((1,), (0,)), ((), ()))).astype(BF16)
    for n, ref in enumerate((keep_ref, came_ref)):
        for part in range(4):
            held = ref[8 + part : 9 + part, :].astype(F32)
            have = where_one(rows_of((8, 128)).astype(F32) == held)
            at = n * 512 + part * 128
            bias_ref[at : at + 128, :] = (dot(have, wanted, TN) - 1.0) * -HIDDEN
    seen = dot(kinds, wanted, TN) * jnp.where(rows_of((ROWS, 128)) <= row_of_lane, 1.0, 0.0)
    span_bias = (seen - 1.0) * -HIDDEN

    for copy in copies:
        copy.wait()
    factor = LOG2E / HD**0.5
    span_s = dot(span_k, q_ref[y0], NT) * factor + span_bias
    for y in range(4):
        q = q_ref[y]
        at = slice(y * 256, (y + 1) * 256)
        absent = jnp.where(duty & (y0 == y), 0.0, HIDDEN)
        scores = [
            dot(ref[:, at], q, NT) * factor + bias_ref[n * 512 : (n + 1) * 512, :]
            for n, ref in enumerate((k_ref, k2_ref))
        ]
        scores.append(span_s + absent)
        peak = functools.reduce(
            jnp.maximum, [jnp.max(s, axis=0, keepdims=True) for s in scores], jnp.float32(NONE)
        )
        high, low = split_pair(peak)
        peak = high + low
        weights = [jnp.exp2(s - peak) for s in scores]
        total = sum(jnp.sum(w, axis=0, keepdims=True) for w in weights)
        out = dot(v_ref[:, at].T, weights[0].astype(BF16), (((1,), (0,)), ((), ())))
        out = out + dot(v2_ref[:, at].T, weights[1].astype(BF16), (((1,), (0,)), ((), ())))
        out = out + dot(span_v, weights[2].astype(BF16), TN)
        out = jnp.where(lanes((128, 128)) < 64, out[:128], out[128:]).astype(BF16)
        state = state_rows(peak, total)
        for n in range(4):
            out_ref[y * 4 + n, 0:32, :] = out[n * 32 : (n + 1) * 32]
            out_ref[y * 4 + n, 32:40, :] = state


def merged(in_ref):
    count = in_ref.shape[0]
    peaks, totals = [], []
    for n in range(count):
        state = in_ref[n, 32:40, :].astype(F32)
        peaks.append(state[0:1] + state[1:2])
        totals.append(state[2:3] + state[3:4])
    peak = functools.reduce(jnp.maximum, peaks)
    out = jnp.zeros((32, 128), F32)
    total = jnp.zeros((1, 128), F32)
    for n in range(count):
        factor = jnp.exp2(peaks[n] - peak)
        out = out + in_ref[n, 0:32, :].astype(F32) * factor
        total = total + totals[n] * factor
    return out, peak, total


def merge_body(in_ref, out_ref):
    out, peak, total = merged(in_ref)
    out = out.astype(BF16)
    state = state_rows(peak, total)
    for d in range(out_ref.shape[0]):
        out_ref[d, 0:32, :] = out
        out_ref[d, 32:40, :] = state


def finish_body(in_ref, out_ref):
    out, _, total = merged(in_ref)
    out = (out / total).astype(BF16)
    for d in range(out_ref.shape[0]):
        out_ref[d] = out


def turned(in_ref, store):
    eye = where_one(rows_of((128, 128)) == lanes((128, 128)))
    for y in range(4):
        block = dot(eye, in_ref[y * 4 : (y + 1) * 4].reshape(128, 128), NT).astype(BF16)
        for i in range(16):
            store((y * 16 + i) * HD, block[i * 8 : (i + 1) * 8])


def half_body(in_ref, out_ref):
    def store(at, piece):
        out_ref[:, at : at + HD] = piece

    turned(in_ref, store)


def place_body(in_ref, own_ref, out_ref):
    c = lax.axis_index("c")
    out_ref[pl.ds(pl.multiple_of(c * 8, 8), 8), :] = own_ref[...]
    rows = pl.ds(pl.multiple_of((1 - c) * 8, 8), 8)

    def store(at, piece):
        out_ref[rows, at : at + HD] = piece

    turned(in_ref, store)


def per_device(
    queries,
    span_keys,
    span_values,
    positions,
    span_segments,
    cache_keys,
    cache_values,
    cache_segments,
):
    shape = jax.ShapeDtypeStruct
    tile = shape((16, 128), BF16)
    keep, send, positions, span_segments = call(
        pack_body,
        (tile, tile, shape((3, ROWS), jnp.int32), shape((1, ROWS), jnp.int32)),
        queries,
        span_keys.T,
        span_values.T,
        cache_segments.reshape(4, 128),
        positions,
        span_segments.reshape(1, ROWS),
        specs=[HBM] * 6,
        scratch=[
            pltpu.VMEM((ROWS, 32), BF16),
            pltpu.VMEM((4, ROWS), BF16),
            pltpu.VMEM((4, ROWS), BF16),
            pltpu.VMEM((4, 128), jnp.int32),
            pltpu.SemaphoreType.DMA((6,)),
        ],
    )
    came = swap(send)
    came, cache_keys, cache_values = lax.optimization_barrier((came, cache_keys, cache_values))
    other_keys = swap(cache_keys)
    other_values = swap(cache_values)
    tiles = call(spread_body, shape((128, 8, 128), BF16), keep, came)
    tiles = exchange(tiles, CHIPS)
    parts = call(
        attend_body,
        shape((16, 40, 128), BF16),
        tiles,
        keep,
        came,
        positions,
        span_segments,
        other_keys,
        other_values,
        cache_keys,
        cache_values,
        specs=[VMEM] * 7 + [HBM] * 2,
        scratch=[
            pltpu.VMEM((4, 128, 256), BF16),
            pltpu.VMEM((2, ROWS, 128), F32),
            pltpu.VMEM((1024, 128), F32),
            pltpu.VMEM((512, 1024), BF16),
            pltpu.VMEM((512, 1024), BF16),
            pltpu.SemaphoreType.DMA((2,)),
        ],
        limit=12 << 20,
    )
    parts = exchange(parts, PLANE)
    parts = call(merge_body, shape((8, 40, 128), BF16), parts)
    parts = exchange(parts, ("z",))
    whole = call(finish_body, shape((16, 32, 128), BF16), parts)
    whole = exchange(whole, PLANE)
    other = swap(whole)
    own = call(half_body, shape((8, H * HD), BF16), whole)
    return call(place_body, shape((ROWS, H * HD), BF16), other, own)


def solution(mesh):
    split = Mesh(mesh.devices.reshape(4, 8, 4, 2), ALL)
    return jax.shard_map(
        per_device,
        mesh=split,
        in_specs=(
            P(None, ALL),
            P(None, ALL),
            P(None, ALL),
            P(),
            P(),
            P(ALL, None),
            P(ALL, None),
            P(ALL),
        ),
        out_specs=P(),
        check_vma=False,
    )
```

time: 92.6 us -> 81.7 us (0.88)
  blocking collectives: 41.2 us -> 57.3 us
  waiting for transfers between devices: 10.5 us -> 1.6 us
  starting transfers between devices: 16.7 us -> 9.22 us
  Pallas kernels: 16.1 us -> 8.64 us
  other arithmetic: 1.73 us -> 0 us
    all_to_all x2 -> x0, starting transfers between devices: 16.7 us -> none  [exchange(): return lax.all_to_all(tiles, axes, 0, 0, tiled=True)]
    all_to_all x3 -> x4, blocking collectives: 41.2 us -> 57.3 us  [exchange(): return lax.all_to_all(tiles, axes, 0, 0, tiled=True)]
    all_to_all x2 -> x0, waiting for transfers between devices: 10.5 us -> none  [exchange(): return lax.all_to_all(tiles, axes, 0, 0, tiled=True)]
    ppermute x0 -> x4, starting transfers between devices: none -> 9.22 us  [swap(): return lax.ppermute(value, 'c', ((0, 1), (1, 0)))]
    pallas_call x7, Pallas kernels: 16.1 us -> 8.64 us  [call(): pl.pallas_call(body, out_shape=out_shape, in_specs=specs or [VMEM] * len(...]
    ppermute x0 -> x4, waiting for transfers between devices: none -> 1.6 us  [swap(): return lax.ppermute(value, 'c', ((0, 1), (1, 0)))]
    unnamed x14 -> x16, local copies, waits for them, and re-layouts: 4.64 us -> 4.51 us
  transfers between devices with their start and end apart: 2 -> 4, of which waited for: 2 -> 2; matrix products, arithmetic and copies ran while one was open for 3% -> 0% of each run, Pallas kernels for 3% -> 0%
where the time goes in v3:
time: 81.7 us; the launch traced here: 81.3 us
  blocking collectives  57.3 us (70%)
  starting transfers between devices  9.22 us (11%)
  Pallas kernels  8.64 us (11%)
  local copies, waits for them, and re-layouts  4.51 us (6%)
  waiting for transfers between devices  1.6 us (2%)
    all_to_all x4, blocking collectives, exchange(): return lax.all_to_all(tiles, axes, 0, 0, tiled=True)  57.3 us
    ppermute x4, starting transfers between devices, swap(): return lax.ppermute(value, 'c', ((0, 1), (1, 0)))  9.22 us
    pallas_call x7, Pallas kernels, call(): pl.pallas_call(body, out_shape=out_shape, in_specs=specs or [VMEM] * len(...  8.64 us
    unnamed x16, local copies, waits for them, and re-layouts  4.51 us
  transfers between devices with their start and end apart: 4, of which 2 were waited for; matrix products, arithmetic and copies ran while one was open for 0% of the time, Pallas kernels for 0%

profile of v3, /device:TPU:1, one launch (start us, length us, event | category | flops | bytes accessed | tf_op | source)
XLA Modules:
  0.0 81.3 jit_solution(6493319234112680555)
XLA Ops:
  0.0 0.0 copy-start.2
  0.0 0.0 copy-start.3
  0.0 0.0 copy-start.5
  0.0 0.0 copy-start.7
  0.0 0.7 copy-done.2
  0.7 0.0 copy-done.3
  0.7 0.0 copy-done.5
  0.7 0.0 copy-done.7
  0.7 0.0 copy-start.4
  0.7 0.7 copy-done.4
  1.4 0.0 copy-start.6
  1.4 0.7 copy-done.6
  2.1 0.3 shard_map.82
  2.3 3.3 %collective-permute-start = (bf16[16,128]{1,0:T(8,128)(2,1)S(1)}, bf16[16,128]{1,0:T(8,128)(2,1)S(1)}, u32[]{:S(2)}, u32[]{:S(2)}) collective-permute-start(bf16[16,128]{1,0:T(8,128)(2,1)S(1)} %get-tuple-element.13), channel_id=1, source_target_pairs={{0,1},{1,0},{2,3},{3,2},{4,5},{5,4},{6,7},{7,6},{8,9},{9,8},{10,11... | collective-permute-start | bytes 12296 | tf_op jit(solution)/shard_map/ppermute | solution.py:52
  5.6 0.8 %collective-permute-done.came_ref = bf16[16,128]{1,0:T(8,128)(2,1)S(1)} collective-permute-done((bf16[16,128]{1,0:T(8,128)(2,1)S(1)}, bf16[16,128]{1,0:T(8,128)(2,1)S(1)}, u32[]{:S(2)}, u32[]{:S(2)}) %collective-permute-start) | collective-permute-done | bytes 4128 | tf_op jit(solution)/shard_map/ppermute | solution.py:52
  6.4 0.3 collective-permute-start.1
  6.8 0.2 collective-permute-start.2
  7.0 26.6 %all_to_all.20.in_ref = bf16[128,8,128]{2,1,0:T(8,128)(2,1)S(1)} all-to-all(bf16[128,8,128]{2,1,0:T(8,128)(2,1)S(1)} %shard_map.83), channel_id=1, replica_groups=mesh['y'=4,'z'=8,'x'=4,'c'=2] {'y','z','x'}, dimensions={0} | all-to-all | bytes 524288 | tf_op jit(solution)/shard_map/all_to_all | solution.py:48
  33.6 0.0 collective-permute-done.1.k2_ref
  33.6 0.0 collective-permute-done.2.v2_ref
  33.6 0.0 copy-start
  33.6 1.2 %copy-done = bf16[512,1024]{1,0:T(8,128)(2,1)S(1)} copy-done((bf16[512,1024]{1,0:T(8,128)(2,1)S(1)}, bf16[512,1024]{1,0:T(8,128)(2,1)}, u32[]{:S(2)}) %copy-start) | copy-done | bytes 1048600
  34.8 0.0 copy-start.1
  34.8 1.2 %copy-done.1 = bf16[512,1024]{1,0:T(8,128)(2,1)S(1)} copy-done((bf16[512,1024]{1,0:T(8,128)(2,1)S(1)}, bf16[512,1024]{1,0:T(8,128)(2,1)}, u32[]{:S(2)}) %copy-start.1) | copy-done | bytes 1048600
  36.0 7.1 %shard_map.84 = bf16[16,40,128]{2,1,0:T(8,128)(2,1)S(1)} custom-call(bf16[128,8,128]{2,1,0:T(8,128)(2,1)S(1)} %all_to_all.20.in_ref, bf16[16,128]{1,0:T(8,128)(2,1)S(1)} %get-tuple-element.12.keep_ref, bf16[16,128]{1,0:T(8,128)(2,1)S(1)} %collective-permute-done.came_ref, s32[3,16]{1,0:T(4,128)S(1)} %get-tuple-element.15.pos_ref, ...), custom_call_target="tpu_custom_call" | custom-call | tf_op jit(solution)/shard_map/pallas_call | solution.py:28
  43.1 10.9 %all_to_all.21.in_ref = bf16[16,40,128]{2,1,0:T(8,128)(2,1)S(1)} all-to-all(bf16[16,40,128]{2,1,0:T(8,128)(2,1)S(1)} %shard_map.84), channel_id=1, replica_groups=mesh['y'=4,'z'=8,'x'=4,'c'=2] {'y','x'}, dimensions={0} | all-to-all | bytes 327680 | tf_op jit(solution)/shard_map/all_to_all | solution.py:48
  54.0 0.1 shard_map.85
  54.1 9.9 %all_to_all.22.in_ref = bf16[8,40,128]{2,1,0:T(8,128)(2,1)S(1)} all-to-all(bf16[8,40,128]{2,1,0:T(8,128)(2,1)S(1)} %shard_map.85), channel_id=1, replica_groups=mesh['y'=4,'z'=8,'x'=4,'c'=2] {'z'}, dimensions={0} | all-to-all | bytes 163840 | tf_op jit(solution)/shard_map/all_to_all | solution.py:48
  64.0 10.0 %all_to_all.23.in_ref = bf16[16,32,128]{2,1,0:T(8,128)(2,1)S(1)} all-to-all(bf16[16,32,128]{2,1,0:T(8,128)(2,1)S(1)} %shard_map.86), channel_id=1, replica_groups=mesh['y'=4,'z'=8,'x'=4,'c'=2] {'y','x'}, dimensions={0} | all-to-all | bytes 262144 | tf_op jit(solution)/shard_map/all_to_all | solution.py:48
  74.0 5.4 %collective-permute-start.3 = (bf16[16,32,128]{2,1,0:T(8,128)(2,1)S(1)}, bf16[16,32,128]{2,1,0:T(8,128)(2,1)S(1)}, u32[]{:S(2)}, u32[]{:S(2)}) collective-permute-start(bf16[16,32,128]{2,1,0:T(8,128)(2,1)S(1)} %all_to_all.23.in_ref), channel_id=1, source_target_pairs={{0,1},{1,0},{2,3},{3,2},{4,5},{5,4},{6,7},{7,6},{8,9},{9,8},{10,11... | collective-permute-start | bytes 393224 | tf_op jit(solution)/shard_map/ppermute | solution.py:52
  79.4 0.2 shard_map.87.own_ref
  79.6 0.8 collective-permute-done.3.in_ref
  80.4 0.9 %shard_map.88 = bf16[16,8192]{1,0:T(8,128)(2,1)} custom-call(bf16[16,32,128]{2,1,0:T(8,128)(2,1)S(1)} %collective-permute-done.3.in_ref, bf16[8,8192]{1,0:T(8,128)(2,1)S(1)} %shard_map.87.own_ref), custom_call_target="tpu_custom_call" | custom-call | tf_op jit(solution)/shard_map/pallas_call | solution.py:28
  (2 shorter events, 0.1 us)
Async XLA Ops:
  0.0 0.7 copy-start.2
  0.0 0.7 copy-start.3
  0.0 0.7 copy-start.5
  0.0 0.7 copy-start.7
  0.7 0.7 copy-start.4
  1.4 0.7 copy-start.6
  2.3 4.1 %collective-permute-start = (bf16[16,128]{1,0:T(8,128)(2,1)S(1)}, bf16[16,128]{1,0:T(8,128)(2,1)S(1)}, u32[]{:S(2)}, u32[]{:S(2)}) collective-permute-start(bf16[16,128]{1,0:T(8,128)(2,1)S(1)} %get-tuple-element.13), channel_id=1, source_target_pairs={{0,1},{1,0},{2,3},{3,2},{4,5},{5,4},{6,7},{7,6},{8,9},{9,8},{10,11... | collective-permute-start | bytes 12296 | tf_op jit(solution)/shard_map/ppermute | solution.py:52
  6.4 27.1 %collective-permute-start.1 = (bf16[512,1024]{1,0:T(8,128)(2,1)}, bf16[512,1024]{1,0:T(8,128)(2,1)S(1)}, u32[]{:S(2)}, u32[]{:S(2)}) collective-permute-start(bf16[512,1024]{1,0:T(8,128)(2,1)} %k_hbm), channel_id=1, source_target_pairs={{0,1},{1,0},{2,3},{3,2},{4,5},{5,4},{6,7},{7,6},{8,9},{9,8},{10,11... | collective-permute-start | bytes 3145736 | tf_op jit(solution)/shard_map/ppermute | solution.py:52
  6.8 26.8 %collective-permute-start.2 = (bf16[512,1024]{1,0:T(8,128)(2,1)}, bf16[512,1024]{1,0:T(8,128)(2,1)S(1)}, u32[]{:S(2)}, u32[]{:S(2)}) collective-permute-start(bf16[512,1024]{1,0:T(8,128)(2,1)} %v_hbm), channel_id=1, source_target_pairs={{0,1},{1,0},{2,3},{3,2},{4,5},{5,4},{6,7},{7,6},{8,9},{9,8},{10,11... | collective-permute-start | bytes 3145736 | tf_op jit(solution)/shard_map/ppermute | solution.py:52
  33.6 1.2 %copy-start = (bf16[512,1024]{1,0:T(8,128)(2,1)S(1)}, bf16[512,1024]{1,0:T(8,128)(2,1)}, u32[]{:S(2)}) copy-start(bf16[512,1024]{1,0:T(8,128)(2,1)} %k_hbm) | copy-start | bytes 3145732
  34.8 1.2 %copy-start.1 = (bf16[512,1024]{1,0:T(8,128)(2,1)S(1)}, bf16[512,1024]{1,0:T(8,128)(2,1)}, u32[]{:S(2)}) copy-start(bf16[512,1024]{1,0:T(8,128)(2,1)} %v_hbm) | copy-start | bytes 3145732
  74.0 6.4 %collective-permute-start.3 = (bf16[16,32,128]{2,1,0:T(8,128)(2,1)S(1)}, bf16[16,32,128]{2,1,0:T(8,128)(2,1)S(1)}, u32[]{:S(2)}, u32[]{:S(2)}) collective-permute-start(bf16[16,32,128]{2,1,0:T(8,128)(2,1)S(1)} %all_to_all.23.in_ref), channel_id=1, source_target_pairs={{0,1},{1,0},{2,3},{3,2},{4,5},{5,4},{6,7},{7,6},{8,9},{9,8},{10,11... | collective-permute-start | bytes 393224 | tf_op jit(solution)/shard_map/ppermute | solution.py:52

commit v4 on v3

v4 whole, which is shorter than its diff:
```python
import functools

import jax
import jax.numpy as jnp
from jax import lax
from jax.experimental import pallas as pl
from jax.experimental.pallas import tpu as pltpu
from jax.sharding import Mesh
from jax.sharding import PartitionSpec as P

H = 64
KVH = 8
HD = 128
ROWS = 16
ALL = ("y", "z", "x", "c")
CHIPS = ("y", "z", "x")
PLANE = ("y", "x")
LOG2E = 1.4426950408889634
NONE = -1e30
HIDDEN = -2e30
F32 = jnp.float32
BF16 = jnp.bfloat16
VMEM = pl.BlockSpec(memory_space=pltpu.VMEM)
NT = (((1,), (1,)), ((), ()))


def call(body, name, out_shape, *args, specs=None, scratch=(), limit=8 << 20):
    return pl.pallas_call(
        body,
        name=name,
        out_shape=out_shape,
        in_specs=specs or [VMEM] * len(args),
        out_specs=jax.tree.map(lambda _: VMEM, out_shape),
        scratch_shapes=scratch,
        compiler_params=pltpu.CompilerParams(vmem_limit_bytes=limit),
    )(*args)


def lanes(shape):
    return lax.broadcasted_iota(jnp.int32, shape, len(shape) - 1)


def move(value, by):
    by %= value.shape[-1]
    return pltpu.roll(value, by, value.ndim - 1) if by else value


def exchange(tiles, axes):
    return lax.all_to_all(tiles, axes, 0, 0, tiled=True)


def swap(value):
    return lax.ppermute(value, "c", ((0, 1), (1, 0)))


def rows_of(shape):
    return lax.broadcasted_iota(jnp.int32, shape, 0)


TN = (((0,), (0,)), ((), ()))
NN = (((1,), (0,)), ((), ()))


def dot(a, b, dims):
    return lax.dot_general(a, b, dims, preferred_element_type=F32)


def where_one(hit):
    return jnp.where(hit, 1.0, 0.0).astype(BF16)


def pack_body(q_ref, k_ref, v_ref, out_ref):
    def spread(count, at):
        return where_one(lanes((count, 128)) == rows_of((count, 128)) + at)

    tile = jnp.zeros((8, 128), F32)
    for late in range(2):
        part = dot(q_ref[...], spread(32, late * 32), NN)
        for ref, at in ((k_ref, 64), (v_ref, 96)):
            part = part + dot(ref[...], spread(4, at + late * 16), TN)
        tile = tile + part[late * 8 : (late + 1) * 8]
    tile = tile.astype(BF16)
    for d in range(out_ref.shape[0]):
        out_ref[d] = tile


def turn(angle):
    quarter = jnp.floor(angle * 0.6366197723675814 + 0.5)
    rest = angle - quarter * 1.5703125
    rest = rest - quarter * 4.837512969970703e-4
    rest = rest - quarter * 7.549789948768648e-8
    square = rest * rest
    sine = -1.9515295891e-4 * square + 8.3321608736e-3
    sine = (sine * square - 1.6666654611e-1) * square * rest + rest
    cosine = 2.443315711809948e-5 * square - 1.388731625493765e-3
    cosine = (cosine * square + 4.166664568298827e-2) * square * square - 0.5 * square + 1.0
    which = quarter.astype(jnp.int32) % 4
    odd = which % 2 == 1
    cosine, sine = jnp.where(odd, sine, cosine), jnp.where(odd, cosine, sine)
    cosine = jnp.where((which == 1) | (which == 2), -cosine, cosine)
    sine = jnp.where(which >= 2, -sine, sine)
    return cosine, sine


def rope_tables(positions, index):
    section = jnp.where(index < 16, 0, jnp.where(index < 40, 1, 2))
    high = positions // 64
    position = jnp.zeros(index.shape, F32)
    for scale, part in ((64.0, high), (1.0, positions - high * 64)):
        chosen = dot(part.astype(F32).astype(BF16), where_one(rows_of((3, 3 * 128)) == lanes((3, 3 * 128)) // 128), TN)
        picked = chosen[:, 256:]
        for n in range(2):
            picked = jnp.where(section == n, chosen[:, n * 128 : (n + 1) * 128], picked)
        position = position + scale * picked
    inverse = jnp.ones(index.shape, F32)
    for bit in range(6):
        step = 1000000.0 ** (-2.0 * 2**bit / HD)
        inverse = jnp.where((index // 2**bit) % 2 == 1, inverse * step, inverse)
    return turn(position * inverse)


def rotate(value, cosine, sine):
    return value * cosine + move(value, 64) * sine


def split_pair(value):
    high = value.astype(BF16).astype(F32)
    return high, (value - high).astype(BF16).astype(F32)


def state_rows(peak, total):
    row = rows_of((8, 128))
    parts = (*split_pair(peak), *split_pair(total))
    tile = jnp.zeros((8, 128), F32)
    for n, part in enumerate(parts):
        tile = jnp.where(row == n, part, tile)
    return tile.astype(BF16)


def ready_body(in_ref, pos_ref, seg_ref, held_ref, v_ref, q_ref, vt_ref, bias_ref, table_ref):
    c = lax.axis_index("c")
    lane = lanes((ROWS, 128))
    for n in range(2):
        own = n == 0
        cosine, sine = rope_tables(pos_ref[...], lane % 32 + jnp.where(own, c, 1 - c) * 32)
        late = (lane // 32) % 2 == 1
        cosine = jnp.where(late[:8], cosine[8:], cosine[:8])
        sine = jnp.where(late[:8], sine[8:], sine[:8])
        table_ref[2 * n] = cosine
        table_ref[2 * n + 1] = jnp.where(lane[:8] < 64, -sine, sine)
    cosine, sine = rope_tables(pos_ref[...], lane % 64)
    table_ref[4], table_ref[5] = cosine[:8], cosine[8:]
    sine = jnp.where(lane < 64, -sine, sine)
    table_ref[6], table_ref[7] = sine[:8], sine[8:]
    rotate_pairs(in_ref, q_ref, table_ref[0], table_ref[1])
    for g in range(KVH):
        vt_ref[g] = v_ref[:, g * HD : (g + 1) * HD].T
    pick = where_one(rows_of((ROWS, 128)) == lane % ROWS)
    kinds = where_one(rows_of((8, ROWS)) == seg_ref[...])
    wanted = dot(kinds, pick, NN).astype(BF16)
    for part in range(4):
        have = where_one(rows_of((8, 128)) == held_ref[part : part + 1, :])
        bias_ref[part * 128 : (part + 1) * 128, :] = (dot(have, wanted, TN) - 1.0) * -HIDDEN
    seen = dot(kinds, wanted, TN) * jnp.where(rows_of((ROWS, 128)) <= lane % ROWS, 1.0, 0.0)
    bias_ref[512:, :] = (seen - 1.0) * -HIDDEN


def rotate_pairs(in_ref, out_ref, cosine, sine):
    lane = lanes((8, 128))
    for n in range(64):
        a, b = in_ref[2 * n].astype(F32), in_ref[2 * n + 1].astype(F32)
        out_ref[n] = rotate(jnp.where(lane < 64, a, move(b, 64)), cosine, sine)


def join_body(own_ref, in_ref, table_ref, q_ref, other_ref):
    c = lax.axis_index("c")
    rotate_pairs(in_ref, other_ref, table_ref[2], table_ref[3])
    lane = lanes((8, 128))
    first = c == 0
    near = lane % 64 < 32
    for n in range(64):
        own, other = own_ref[n], other_ref[n]
        low, high = jnp.where(first, own, other), jnp.where(first, other, own)
        z, p = (n // 2) % 8, n % 2
        head = (n // 16) * 16 + z * 2 + p
        q_ref[head * 16 : head * 16 + 8, :] = jnp.where(near, low, move(high, 32)).astype(BF16)
        q_ref[head * 16 + 8 : head * 16 + 16, :] = jnp.where(near, move(low, -32), high).astype(BF16)


def attend(q, k, vt, bias, span):
    factor = LOG2E / HD**0.5
    scores = [dot(k, q, NT) * factor + bias]
    if span is not None:
        scores.append(dot(span[0], q, NT) * factor + span[2])
    peak = functools.reduce(
        jnp.maximum, [jnp.max(s, axis=0, keepdims=True) for s in scores], jnp.float32(NONE)
    )
    high, low = split_pair(peak)
    peak = high + low
    weights = [jnp.exp2(s - peak) for s in scores]
    total = sum(jnp.sum(w, axis=0, keepdims=True) for w in weights)
    out = dot(vt, weights[0].astype(BF16), NN)
    if span is not None:
        out = out + dot(span[1], weights[1].astype(BF16), TN)
    return out.astype(BF16), state_rows(peak, total)


def emit(out_ref, i, result):
    for n in range(4):
        out_ref[i * 4 + n, 0:32, :] = result[0][n * 32 : (n + 1) * 32]
        out_ref[i * 4 + n, 32:40, :] = result[1]


def heads_at(base, i):
    return pl.ds(pl.multiple_of((base + i) * 128, 128), 128)


def first_body(q_ref, k_ref, vt_ref, bias_ref, out_ref):
    base = (1 - lax.axis_index("c")) * 4
    for i in range(4):
        at = heads_at(base, i)
        emit(out_ref, i, attend(q_ref[at, :], k_ref[:, at], vt_ref[base + i], bias_ref[0:512, :], None))


def second_body(q_ref, k_ref, vt_ref, bias_ref, in_ref, came_ref, table_ref, out_ref):
    c, y = lax.axis_index("c"), lax.axis_index("y")
    base = c * 4
    lane = lanes((8, 128))
    duty = (lax.axis_index("z") == 0) & (lax.axis_index("x") == 0)
    g = base + y
    start = (g // 2) * 32 + (g % 2) * 16
    found = []
    for kind in range(2):
        parts = []
        for late in range(2):
            value = jnp.zeros((8, 128), F32)
            for n in range(16):
                own, came = in_ref[start + n].astype(F32), came_ref[start + n].astype(F32)
                pair = (jnp.where(c == 0, own, came), jnp.where(c == 0, came, own))
                for core in range(2):
                    at = n * 8 + core * 4
                    value = jnp.where(
                        (lane >= at) & (lane < at + 4),
                        move(pair[core], at - 64 - kind * 32 - late * 16),
                        value,
                    )
            parts.append(value)
        if kind == 0:
            parts = [rotate(v, table_ref[4 + n], table_ref[6 + n]) for n, v in enumerate(parts)]
        found.append(jnp.concatenate(parts, axis=0).astype(BF16))
    for i in range(4):
        at = heads_at(base, i)
        absent = jnp.where(duty & (y == i), 0.0, HIDDEN)
        span = (found[0], found[1], bias_ref[512:, :] + absent)
        emit(out_ref, i, attend(q_ref[at, :], k_ref[:, at], vt_ref[base + i], bias_ref[0:512, :], span))


def couple_body(own_ref, came_ref, out_ref):
    for n in range(16):
        out, peak, total = merged([own_ref.at[n], came_ref.at[n]])
        out_ref[n, 0:32, :] = out.astype(BF16)
        out_ref[n, 32:40, :] = state_rows(peak, total)


def merged(refs):
    peaks, totals = [], []
    for ref in refs:
        state = ref[32:40, :].astype(F32)
        peaks.append(state[0:1] + state[1:2])
        totals.append(state[2:3] + state[3:4])
    peak = functools.reduce(jnp.maximum, peaks)
    out = jnp.zeros((32, 128), F32)
    total = jnp.zeros((1, 128), F32)
    for n, ref in enumerate(refs):
        factor = jnp.exp2(peaks[n] - peak)
        out = out + ref[0:32, :].astype(F32) * factor
        total = total + totals[n] * factor
    return out, peak, total


def merge_body(in_ref, out_ref):
    out, peak, total = merged([in_ref.at[n] for n in range(in_ref.shape[0])])
    out = out.astype(BF16)
    state = state_rows(peak, total)
    for d in range(out_ref.shape[0]):
        out_ref[d, 0:32, :] = out
        out_ref[d, 32:40, :] = state


def finish_body(in_ref, out_ref):
    out, _, total = merged([in_ref.at[n] for n in range(in_ref.shape[0])])
    out = (out / total).astype(BF16)
    for d in range(out_ref.shape[0]):
        out_ref[d] = out


def turned(in_ref, store):
    eye = where_one(rows_of((128, 128)) == lanes((128, 128)))
    for g in range(4):
        block = dot(eye, in_ref[g * 4 : (g + 1) * 4].reshape(128, 128), NT).astype(BF16)
        for i in range(8):
            store((g * 8 + i) * HD, block[i * ROWS : (i + 1) * ROWS])


def half_body(in_ref, out_ref):
    def store(at, piece):
        out_ref[:, at : at + HD] = piece

    turned(in_ref, store)


def place_body(in_ref, own_ref, out_ref):
    c = lax.axis_index("c")
    half = H * HD // 2
    out_ref[:, pl.ds(pl.multiple_of(c * half, half), half)] = own_ref[...]

    def store(at, piece):
        out_ref[:, pl.ds(pl.multiple_of((1 - c) * half + at, HD), HD)] = piece

    turned(in_ref, store)


def per_device(
    queries,
    span_keys,
    span_values,
    positions,
    span_segments,
    cache_keys,
    cache_values,
    cache_segments,
):
    shape = jax.ShapeDtypeStruct
    tiles = call(
        pack_body, "pack", shape((128, 8, 128), BF16), queries, span_keys.T, span_values.T
    )
    tiles = exchange(tiles, CHIPS)
    came = swap(tiles)
    own, turned_values, bias, tables = call(
        ready_body,
        "ready",
        (
            shape((64, 8, 128), F32),
            shape((KVH, HD, 512), BF16),
            shape((512 + ROWS, 128), F32),
            shape((8, 8, 128), F32),
        ),
        tiles,
        positions,
        span_segments.reshape(1, ROWS),
        cache_segments.reshape(4, 128),
        cache_values,
    )
    q = call(
        join_body,
        "join",
        shape((H * ROWS, HD), BF16),
        own,
        came,
        tables,
        scratch=[pltpu.VMEM((64, 8, 128), F32)],
    )
    message = shape((16, 40, 128), BF16)
    parts = call(first_body, "first", message, q, cache_keys, turned_values, bias)
    other = swap(parts)
    parts = call(
        second_body, "second", message, q, cache_keys, turned_values, bias, tiles, came, tables
    )
    parts = call(couple_body, "couple", message, parts, other)
    parts = exchange(parts, PLANE)
    parts = call(merge_body, "merge", shape((8, 40, 128), BF16), parts)
    parts = exchange(parts, ("z",))
    whole = call(finish_body, "finish", shape((16, 32, 128), BF16), parts)
    whole = exchange(whole, PLANE)
    other = swap(whole)
    own = call(half_body, "half", shape((ROWS, H * HD // 2), BF16), whole)
    return call(place_body, "place", shape((ROWS, H * HD), BF16), other, own)


def solution(mesh):
    split = Mesh(mesh.devices.reshape(4, 8, 4, 2), ALL)
    return jax.shard_map(
        per_device,
        mesh=split,
        in_specs=(
            P(None, ALL),
            P(None, ALL),
            P(None, ALL),
            P(),
            P(),
            P(ALL, None),
            P(ALL, None),
            P(ALL),
        ),
        out_specs=P(),
        check_vma=False,
    )
```

time: 81.7 us -> 83.8 us (1.026)
  Pallas kernels: 8.64 us -> 13.4 us
  starting transfers between devices: 9.22 us -> 7.33 us
  local copies, waits for them, and re-layouts: 4.51 us -> 3.27 us
  blocking collectives: 57.3 us -> 58.5 us
    pallas_call x7 -> x10, Pallas kernels: 8.64 us -> 13.4 us  [call(): pl.pallas_call(body, name=name, out_shape=out_shape, in_specs=specs or [V...]
    ppermute x4 -> x3, starting transfers between devices: 9.22 us -> 7.33 us  [swap(): return lax.ppermute(value, 'c', ((0, 1), (1, 0)))]
    unnamed x16, local copies, waits for them, and re-layouts: 4.51 us -> 3.27 us
    all_to_all x4, blocking collectives: 57.3 us -> 58.5 us  [exchange(): return lax.all_to_all(tiles, axes, 0, 0, tiled=True)]
  transfers between devices with their start and end apart: 4 -> 3, of which waited for: 2 -> 1; matrix products, arithmetic and copies ran while one was open for 0% -> 0% of each run, Pallas kernels for 0% -> 8%
where the time goes in v4:
time: 83.8 us; the launch traced here: 83.4 us
  blocking collectives  58.5 us (70%)
  Pallas kernels  13.4 us (16%)
  starting transfers between devices  7.33 us (9%)
  local copies, waits for them, and re-layouts  3.27 us (4%)
    all_to_all x4, blocking collectives, exchange(): return lax.all_to_all(tiles, axes, 0, 0, tiled=True)  58.5 us
    pallas_call x10, Pallas kernels, call(): pl.pallas_call(body, name=name, out_shape=out_shape, in_specs=specs or [V...  13.4 us
    ppermute x3, starting transfers between devices, swap(): return lax.ppermute(value, 'c', ((0, 1), (1, 0)))  7.33 us
    unnamed x16, local copies, waits for them, and re-layouts  3.27 us
  transfers between devices with their start and end apart: 3, of which 1 were waited for; matrix products, arithmetic and copies ran while one was open for 0% of the time, Pallas kernels for 8%

profile of v4, /device:TPU:1, one launch (start us, length us, event | category | flops | bytes accessed | tf_op | source)
XLA Modules:
  0.0 83.4 jit_solution(17171804767945928790)
XLA Ops:
  0.0 0.0 copy-start.6
  0.0 0.0 copy-start.5
  0.0 0.7 copy-done.6
  0.7 0.0 copy-done.5
  0.7 0.0 copy-start.2
  0.7 0.7 copy-done.2
  1.4 0.2 pack.1
  1.6 0.0 copy-start.4
  1.6 28.6 %all_to_all.20.in_ref = bf16[128,8,128]{2,1,0:T(8,128)(2,1)S(1)} all-to-all(bf16[128,8,128]{2,1,0:T(8,128)(2,1)S(1)} %pack.1), channel_id=1, replica_groups=mesh['y'=4,'z'=8,'x'=4,'c'=2] {'y','z','x'}, dimensions={0} | all-to-all | bytes 524288 | tf_op jit(solution)/shard_map/all_to_all | solution.py:49
  30.2 0.0 copy-start.3
  30.2 3.0 %collective-permute-start = (bf16[128,8,128]{2,1,0:T(8,128)(2,1)S(1)}, bf16[128,8,128]{2,1,0:T(8,128)(2,1)S(1)}, u32[]{:S(2)}, u32[]{:S(2)}) collective-permute-start(bf16[128,8,128]{2,1,0:T(8,128)(2,1)S(1)} %all_to_all.20.in_ref), channel_id=1, source_target_pairs={{0,1},{1,0},{2,3},{3,2},{4,5},{5,4},{6,7},{7,6},{8,9},{9,8},{10,11... | collective-permute-start | bytes 786440 | tf_op jit(solution)/shard_map/ppermute | solution.py:53
  33.3 0.0 copy-start.7
  33.3 0.0 copy-done.4
  33.3 0.0 copy-done.3
  33.3 0.6 copy-done.7
  33.9 0.0 copy-start.1
  33.9 1.2 %copy-done.1 = bf16[512,1024]{1,0:T(8,128)(2,1)S(1)} copy-done((bf16[512,1024]{1,0:T(8,128)(2,1)S(1)}, bf16[512,1024]{1,0:T(8,128)(2,1)}, u32[]{:S(2)}) %copy-start.1) | copy-done | bytes 1048600
  35.1 0.0 copy-start
  35.1 4.9 %ready.1 = (f32[64,8,128]{2,1,0:T(8,128)S(1)}, bf16[8,128,512]{2,1,0:T(8,128)(2,1)S(1)}, f32[528,128]{1,0:T(8,128)S(1)}, f32[8,8,128]{2,1,0:T(8,128)S(1)}) custom-call(bf16[128,8,128]{2,1,0:T(8,128)(2,1)S(1)} %all_to_all.20.in_ref, s32[3,16]{1,0:T(4,128)S(1)} %copy-done.3, s32[1,16]{1,0:T(1,128)S(1)} %bitcast.7, s32[4,128]{1,0:T(4,128)S(1)} %bitcast.4, ...), custom_call_target="tpu_custom_call" | custom-call | tf_op jit(solution)/shard_map/ready/pallas_call | solution.py:28
  40.1 0.0 collective-permute-done.in_ref.came_ref
  40.1 4.6 %join.1.q_ref = bf16[1024,128]{1,0:T(8,128)(2,1)S(1)} custom-call(f32[64,8,128]{2,1,0:T(8,128)S(1)} %get-tuple-element.9.own_ref, bf16[128,8,128]{2,1,0:T(8,128)(2,1)S(1)} %collective-permute-done.in_ref.came_ref, f32[8,8,128]{2,1,0:T(8,128)S(1)} %get-tuple-element.10.table_ref), custom_call_target="tpu_custom_call" | custom-call | tf_op jit(solution)/shard_map/join/pallas_call | solution.py:28
  44.7 0.0 copy-done
  44.7 0.9 %first.1 = bf16[16,40,128]{2,1,0:T(8,128)(2,1)S(1)} custom-call(bf16[1024,128]{1,0:T(8,128)(2,1)S(1)} %join.1.q_ref, bf16[512,1024]{1,0:T(8,128)(2,1)S(1)} %copy-done, bf16[8,128,512]{2,1,0:T(8,128)(2,1)S(1)} %get-tuple-element.11.vt_ref, f32[528,128]{1,0:T(8,128)S(1)} %get-tuple-element.12.bias_ref), custom_call_target="tpu_custom_call" | custom-call | tf_op jit(solution)/shard_map/first/pallas_call | solution.py:28
  45.7 0.1 collective-permute-start.1
  45.8 1.4 %second.1.own_ref = bf16[16,40,128]{2,1,0:T(8,128)(2,1)S(1)} custom-call(bf16[1024,128]{1,0:T(8,128)(2,1)S(1)} %join.1.q_ref, bf16[512,1024]{1,0:T(8,128)(2,1)S(1)} %copy-done, bf16[8,128,512]{2,1,0:T(8,128)(2,1)S(1)} %get-tuple-element.11.vt_ref, f32[528,128]{1,0:T(8,128)S(1)} %get-tuple-element.12.bias_ref, bf16[128,8,128]{2,1,0:T(8,128)(2,1)S(1)} %all_to_all.20.in_ref, ...), custom_call_target="tpu_custom_call" | custom-call | tf_op jit(solution)/shard_map/second/pallas_call | solution.py:28
  47.2 0.0 collective-permute-done.1.came_ref
  47.2 0.1 couple.1
  47.3 10.2 %all_to_all.21.in_ref = bf16[16,40,128]{2,1,0:T(8,128)(2,1)S(1)} all-to-all(bf16[16,40,128]{2,1,0:T(8,128)(2,1)S(1)} %couple.1), channel_id=1, replica_groups=mesh['y'=4,'z'=8,'x'=4,'c'=2] {'y','x'}, dimensions={0} | all-to-all | bytes 327680 | tf_op jit(solution)/shard_map/all_to_all | solution.py:49
  57.6 0.1 merge.1
  57.6 9.9 %all_to_all.22.in_ref = bf16[8,40,128]{2,1,0:T(8,128)(2,1)S(1)} all-to-all(bf16[8,40,128]{2,1,0:T(8,128)(2,1)S(1)} %merge.1), channel_id=1, replica_groups=mesh['y'=4,'z'=8,'x'=4,'c'=2] {'z'}, dimensions={0} | all-to-all | bytes 163840 | tf_op jit(solution)/shard_map/all_to_all | solution.py:49
  67.6 9.8 %all_to_all.23.in_ref = bf16[16,32,128]{2,1,0:T(8,128)(2,1)S(1)} all-to-all(bf16[16,32,128]{2,1,0:T(8,128)(2,1)S(1)} %finish.1), channel_id=1, replica_groups=mesh['y'=4,'z'=8,'x'=4,'c'=2] {'y','x'}, dimensions={0} | all-to-all | bytes 262144 | tf_op jit(solution)/shard_map/all_to_all | solution.py:49
  77.4 4.2 %collective-permute-start.2 = (bf16[16,32,128]{2,1,0:T(8,128)(2,1)S(1)}, bf16[16,32,128]{2,1,0:T(8,128)(2,1)S(1)}, u32[]{:S(2)}, u32[]{:S(2)}) collective-permute-start(bf16[16,32,128]{2,1,0:T(8,128)(2,1)S(1)} %all_to_all.23.in_ref), channel_id=1, source_target_pairs={{0,1},{1,0},{2,3},{3,2},{4,5},{5,4},{6,7},{7,6},{8,9},{9,8},{10,11... | collective-permute-start | bytes 393224 | tf_op jit(solution)/shard_map/ppermute | solution.py:53
  81.5 0.2 half.1.own_ref
  81.8 0.8 collective-permute-done.2.in_ref
  82.5 0.9 %place.1 = bf16[16,8192]{1,0:T(8,128)(2,1)} custom-call(bf16[16,32,128]{2,1,0:T(8,128)(2,1)S(1)} %collective-permute-done.2.in_ref, bf16[16,4096]{1,0:T(8,128)(2,1)S(1)} %half.1.own_ref), custom_call_target="tpu_custom_call" | custom-call | tf_op jit(solution)/shard_map/place/pallas_call | solution.py:28
  (1 shorter events, 0.0 us)
Async XLA Ops:
  0.0 0.7 copy-start.6
  0.0 0.7 copy-start.5
  0.7 0.7 copy-start.2
  1.6 31.7 %copy-start.4 = (s32[512]{0:T(512)S(1)}, s32[512]{0:T(512)}, u32[]{:S(2)}) copy-start(s32[512]{0:T(512)} %param.15) | copy-start | bytes 6148
  30.2 3.0 %copy-start.3 = (s32[3,16]{1,0:T(4,128)S(1)}, s32[3,16]{1,0:T(4,128)}, u32[]{:S(2)}) copy-start(s32[3,16]{1,0:T(4,128)} %pos_ref.1) | copy-start | bytes 580
  30.2 9.9 %collective-permute-start = (bf16[128,8,128]{2,1,0:T(8,128)(2,1)S(1)}, bf16[128,8,128]{2,1,0:T(8,128)(2,1)S(1)}, u32[]{:S(2)}, u32[]{:S(2)}) collective-permute-start(bf16[128,8,128]{2,1,0:T(8,128)(2,1)S(1)} %all_to_all.20.in_ref), channel_id=1, source_target_pairs={{0,1},{1,0},{2,3},{3,2},{4,5},{5,4},{6,7},{7,6},{8,9},{9,8},{10,11... | collective-permute-start | bytes 786440 | tf_op jit(solution)/shard_map/ppermute | solution.py:53
  33.3 0.7 copy-start.7
  33.9 1.2 %copy-start.1 = (bf16[512,1024]{1,0:T(8,128)(2,1)S(1)}, bf16[512,1024]{1,0:T(8,128)(2,1)}, u32[]{:S(2)}) copy-start(bf16[512,1024]{1,0:T(8,128)(2,1)} %v_ref.1) | copy-start | bytes 3145732
  35.1 9.6 %copy-start = (bf16[512,1024]{1,0:T(8,128)(2,1)S(1)}, bf16[512,1024]{1,0:T(8,128)(2,1)}, u32[]{:S(2)}) copy-start(bf16[512,1024]{1,0:T(8,128)(2,1)} %k_ref.3) | copy-start | bytes 3145732
  45.7 1.5 %collective-permute-start.1 = (bf16[16,40,128]{2,1,0:T(8,128)(2,1)S(1)}, bf16[16,40,128]{2,1,0:T(8,128)(2,1)S(1)}, u32[]{:S(2)}, u32[]{:S(2)}) collective-permute-start(bf16[16,40,128]{2,1,0:T(8,128)(2,1)S(1)} %first.1), channel_id=1, source_target_pairs={{0,1},{1,0},{2,3},{3,2},{4,5},{5,4},{6,7},{7,6},{8,9},{9,8},{10,11... | collective-permute-start | bytes 491528 | tf_op jit(solution)/shard_map/ppermute | solution.py:53
  77.4 5.2 %collective-permute-start.2 = (bf16[16,32,128]{2,1,0:T(8,128)(2,1)S(1)}, bf16[16,32,128]{2,1,0:T(8,128)(2,1)S(1)}, u32[]{:S(2)}, u32[]{:S(2)}) collective-permute-start(bf16[16,32,128]{2,1,0:T(8,128)(2,1)S(1)} %all_to_all.23.in_ref), channel_id=1, source_target_pairs={{0,1},{1,0},{2,3},{3,2},{4,5},{5,4},{6,7},{7,6},{8,9},{9,8},{10,11... | collective-permute-start | bytes 393224 | tf_op jit(solution)/shard_map/ppermute | solution.py:53

commit v5 on v4

--- a/solution.py
+++ b/solution.py
@@ -69,9 +69,12 @@
     return jnp.where(hit, 1.0, 0.0).astype(BF16)
 
 
-def pack_body(q_ref, k_ref, v_ref, out_ref):
+def pack_body(q_ref, k_ref, v_ref, *rest):
+    out_ref = rest[-1]
+    turn = (lax.axis_index("x") % 2) * 64
+
     def spread(count, at):
-        return where_one(lanes((count, 128)) == rows_of((count, 128)) + at)
+        return where_one(lanes((count, 128)) == rows_of((count, 128)) + (at + turn) % 128)
 
     tile = jnp.zeros((8, 128), F32)
     for late in range(2):
@@ -137,22 +140,11 @@
     return tile.astype(BF16)
 
 
-def ready_body(in_ref, pos_ref, seg_ref, held_ref, v_ref, q_ref, vt_ref, bias_ref, table_ref):
-    c = lax.axis_index("c")
+def ready_body(pos_ref, seg_ref, held_ref, v_ref, vt_ref, bias_ref, table_ref):
     lane = lanes((ROWS, 128))
-    for n in range(2):
-        own = n == 0
-        cosine, sine = rope_tables(pos_ref[...], lane % 32 + jnp.where(own, c, 1 - c) * 32)
-        late = (lane // 32) % 2 == 1
-        cosine = jnp.where(late[:8], cosine[8:], cosine[:8])
-        sine = jnp.where(late[:8], sine[8:], sine[:8])
-        table_ref[2 * n] = cosine
-        table_ref[2 * n + 1] = jnp.where(lane[:8] < 64, -sine, sine)
     cosine, sine = rope_tables(pos_ref[...], lane % 64)
-    table_ref[4], table_ref[5] = cosine[:8], cosine[8:]
-    sine = jnp.where(lane < 64, -sine, sine)
-    table_ref[6], table_ref[7] = sine[:8], sine[8:]
-    rotate_pairs(in_ref, q_ref, table_ref[0], table_ref[1])
+    table_ref[0] = cosine
+    table_ref[1] = jnp.where(lane < 64, -sine, sine)
     for g in range(KVH):
         vt_ref[g] = v_ref[:, g * HD : (g + 1) * HD].T
     pick = where_one(rows_of((ROWS, 128)) == lane % ROWS)
@@ -165,26 +157,31 @@
     bias_ref[512:, :] = (seen - 1.0) * -HIDDEN
 
 
-def rotate_pairs(in_ref, out_ref, cosine, sine):
-    lane = lanes((8, 128))
-    for n in range(64):
-        a, b = in_ref[2 * n].astype(F32), in_ref[2 * n + 1].astype(F32)
-        out_ref[n] = rotate(jnp.where(lane < 64, a, move(b, 64)), cosine, sine)
-
-
-def join_body(own_ref, in_ref, table_ref, q_ref, other_ref):
+def placing(core):
+    row, lane = rows_of((128, 256)), lanes((128, 256))
+    at = (row // 64) * 64 + core * 32 + row % 32 + ((row // 32) % 2) * 128
+    return where_one(lane == at)
+
+
+def join(own_ref, came_ref, table_ref, q_ref):
     c = lax.axis_index("c")
-    rotate_pairs(in_ref, other_ref, table_ref[2], table_ref[3])
-    lane = lanes((8, 128))
-    first = c == 0
-    near = lane % 64 < 32
-    for n in range(64):
-        own, other = own_ref[n], other_ref[n]
-        low, high = jnp.where(first, own, other), jnp.where(first, other, own)
-        z, p = (n // 2) % 8, n % 2
-        head = (n // 16) * 16 + z * 2 + p
-        q_ref[head * 16 : head * 16 + 8, :] = jnp.where(near, low, move(high, 32)).astype(BF16)
-        q_ref[head * 16 + 8 : head * 16 + 16, :] = jnp.where(near, move(low, -32), high).astype(BF16)
+    near = lanes((1, 8, 128)) < 64
+
+    def halves(ref):
+        tiles = ref[...].astype(F32).reshape(64, 2, 8, 128)
+        return jnp.where(near, tiles[:, 0], tiles[:, 1]).reshape(512, 128).astype(BF16)
+
+    whole = dot(halves(own_ref), placing(c), NN) + dot(halves(came_ref), placing(1 - c), NN)
+    for late in range(2):
+        part = whole[:, late * 128 : (late + 1) * 128]
+        at = slice(late * 8, (late + 1) * 8)
+        cosine, sine = table_ref[0, at, :], table_ref[1, at, :]
+        turned = move(part, 64).reshape(64, 8, 128)
+        part = (part.reshape(64, 8, 128) * cosine[None] + turned * sine[None]).astype(BF16)
+        for n in range(64):
+            z, p = (n // 2) % 8, n % 2
+            head = (n // 16) * 16 + z * 2 + p
+            q_ref[head * 16 + late * 8 : head * 16 + late * 8 + 8, :] = part[n]
 
 
 def attend(q, k, vt, bias, span):
@@ -215,7 +212,8 @@
     return pl.ds(pl.multiple_of((base + i) * 128, 128), 128)
 
 
-def first_body(q_ref, k_ref, vt_ref, bias_ref, out_ref):
+def first_body(own_ref, came_ref, table_ref, k_ref, vt_ref, bias_ref, out_ref, q_ref):
+    join(own_ref, came_ref, table_ref, q_ref)
     base = (1 - lax.axis_index("c")) * 4
     for i in range(4):
         at = heads_at(base, i)
@@ -239,14 +237,18 @@
                 pair = (jnp.where(c == 0, own, came), jnp.where(c == 0, came, own))
                 for core in range(2):
                     at = n * 8 + core * 4
+                    held = (1 - n % 2) * 64 + kind * 32 + late * 16
                     value = jnp.where(
                         (lane >= at) & (lane < at + 4),
-                        move(pair[core], at - 64 - kind * 32 - late * 16),
+                        move(pair[core], at - held),
                         value,
                     )
             parts.append(value)
         if kind == 0:
-            parts = [rotate(v, table_ref[4 + n], table_ref[6 + n]) for n, v in enumerate(parts)]
+            parts = [
+                rotate(v, table_ref[0, n * 8 : n * 8 + 8, :], table_ref[1, n * 8 : n * 8 + 8, :])
+                for n, v in enumerate(parts)
+            ]
         found.append(jnp.concatenate(parts, axis=0).astype(BF16))
     for i in range(4):
         at = heads_at(base, i)
@@ -331,37 +333,46 @@
     cache_segments,
 ):
     shape = jax.ShapeDtypeStruct
+    span_segments = span_segments.reshape(1, ROWS)
+    cache_segments = cache_segments.reshape(4, 128)
     tiles = call(
-        pack_body, "pack", shape((128, 8, 128), BF16), queries, span_keys.T, span_values.T
+        pack_body,
+        "pack",
+        shape((128, 8, 128), BF16),
+        queries,
+        span_keys.T,
+        span_values.T,
+        positions,
+        span_segments,
+        cache_segments,
     )
     tiles = exchange(tiles, CHIPS)
     came = swap(tiles)
-    own, turned_values, bias, tables = call(
+    turned_values, bias, tables = call(
         ready_body,
         "ready",
         (
-            shape((64, 8, 128), F32),
             shape((KVH, HD, 512), BF16),
             shape((512 + ROWS, 128), F32),
-            shape((8, 8, 128), F32),
+            shape((2, ROWS, 128), F32),
         ),
+        positions,
+        span_segments,
+        cache_segments,
+        cache_values,
+    )
+    message = shape((16, 40, 128), BF16)
+    parts, q = call(
+        first_body,
+        "first",
+        (message, shape((H * ROWS, HD), BF16)),
         tiles,
-        positions,
-        span_segments.reshape(1, ROWS),
-        cache_segments.reshape(4, 128),
-        cache_values,
-    )
-    q = call(
-        join_body,
-        "join",
-        shape((H * ROWS, HD), BF16),
-        own,
         came,
         tables,
-        scratch=[pltpu.VMEM((64, 8, 128), F32)],
-    )
-    message = shape((16, 40, 128), BF16)
-    parts = call(first_body, "first", message, q, cache_keys, turned_values, bias)
+        cache_keys,
+        turned_values,
+        bias,
+    )
     other = swap(parts)
     parts = call(
         second_body, "second", message, q, cache_keys, turned_values, bias, tiles, came, tables

time: 83.8 us -> 77.9 us (0.930)
  Pallas kernels: 13.4 us -> 4.71 us
  local copies, waits for them, and re-layouts: 3.27 us -> 6.06 us
    pallas_call x10 -> x9, Pallas kernels: 13.4 us -> 4.71 us  [call(): pl.pallas_call(body, name=name, out_shape=out_shape, in_specs=specs or [V...]
    unnamed x16 -> x18, local copies, waits for them, and re-layouts: 3.27 us -> 6.06 us
  transfers between devices with their start and end apart: 3 -> 3, of which waited for: 1 -> 1; matrix products, arithmetic and copies ran while one was open for 0% -> 0% of each run, Pallas kernels for 8% -> 3%
where the time goes in v5:
time: 77.9 us; the launch traced here: 77.5 us
  blocking collectives  58.5 us (75%)
  starting transfers between devices  7.32 us (9%)
  local copies, waits for them, and re-layouts  6.06 us (8%)
  Pallas kernels  4.71 us (6%)
  waiting for transfers between devices  0.78 us (1%)
    all_to_all x4, blocking collectives, exchange(): return lax.all_to_all(tiles, axes, 0, 0, tiled=True)  58.5 us
    ppermute x3, starting transfers between devices, swap(): return lax.ppermute(value, 'c', ((0, 1), (1, 0)))  7.32 us
    unnamed x18, local copies, waits for them, and re-layouts  6.06 us
    pallas_call x9, Pallas kernels, call(): pl.pallas_call(body, name=name, out_shape=out_shape, in_specs=specs or [V...  4.71 us
  transfers between devices with their start and end apart: 3, of which 1 were waited for; matrix products, arithmetic and copies ran while one was open for 0% of the time, Pallas kernels for 3%

profile of v5, /device:TPU:1, one launch (start us, length us, event | category | flops | bytes accessed | tf_op | source)
XLA Modules:
  0.0 77.5 jit_solution(3493704560969792552)
XLA Ops:
  0.0 0.0 copy-start
  0.0 0.0 copy-start.2
  0.0 0.8 copy-done.2
  0.8 0.0 copy-start.4
  0.8 0.7 copy-done.4
  1.5 0.0 copy-start.5
  1.5 0.7 copy-done.5
  2.1 0.0 copy-start.6
  2.1 0.7 copy-done.6
  2.8 0.0 copy-start.7
  2.8 0.7 copy-done.7
  3.5 0.0 copy-start.8
  3.5 0.7 copy-done.8
  4.2 0.2 pack.1
  4.4 28.6 %all_to_all.20.own_ref.in_ref = bf16[128,8,128]{2,1,0:T(8,128)(2,1)S(1)} all-to-all(bf16[128,8,128]{2,1,0:T(8,128)(2,1)S(1)} %pack.1), channel_id=1, replica_groups=mesh['y'=4,'z'=8,'x'=4,'c'=2] {'y','z','x'}, dimensions={0} | all-to-all | bytes 524288 | tf_op jit(solution)/shard_map/all_to_all | solution.py:49
  33.0 3.0 %collective-permute-start = (bf16[128,8,128]{2,1,0:T(8,128)(2,1)S(1)}, bf16[128,8,128]{2,1,0:T(8,128)(2,1)S(1)}, u32[]{:S(2)}, u32[]{:S(2)}) collective-permute-start(bf16[128,8,128]{2,1,0:T(8,128)(2,1)S(1)} %all_to_all.20.own_ref.in_ref), channel_id=1, source_target_pairs={{0,1},{1,0},{2,3},{3,2},{4,5},{5,4},{6,7},{7,6},{8,9},{9,8},{10,11... | collective-permute-start | bytes 786440 | tf_op jit(solution)/shard_map/ppermute | solution.py:53
  36.0 0.0 copy-start.1
  36.0 1.2 %copy-done.1 = bf16[512,1024]{1,0:T(8,128)(2,1)S(1)} copy-done((bf16[512,1024]{1,0:T(8,128)(2,1)S(1)}, bf16[512,1024]{1,0:T(8,128)(2,1)}, u32[]{:S(2)}) %copy-start.1) | copy-done | bytes 1048600
  37.2 0.0 copy-start.3
  37.2 0.7 copy-done.3
  37.9 0.4 ready.1
  38.3 0.0 collective-permute-done.came_ref
  38.3 0.0 copy-done
  38.3 1.3 %first.1 = (bf16[16,40,128]{2,1,0:T(8,128)(2,1)S(1)}, bf16[1024,128]{1,0:T(8,128)(2,1)S(1)}) custom-call(bf16[128,8,128]{2,1,0:T(8,128)(2,1)S(1)} %all_to_all.20.own_ref.in_ref, bf16[128,8,128]{2,1,0:T(8,128)(2,1)S(1)} %collective-permute-done.came_ref, f32[2,16,128]{2,1,0:T(8,128)S(1)} %get-tuple-element.10.table_ref, bf16[512,1024]{1,0:T(8,128)(2,1)S(1)} %copy-done, ...), custom_call_target="tpu_custom_call" | custom-call | tf_op jit(solution)/shard_map/first/pallas_call | solution.py:28
  39.7 0.1 collective-permute-start.1
  39.8 1.4 %second.1.own_ref = bf16[16,40,128]{2,1,0:T(8,128)(2,1)S(1)} custom-call(bf16[1024,128]{1,0:T(8,128)(2,1)S(1)} %get-tuple-element.13.q_ref, bf16[512,1024]{1,0:T(8,128)(2,1)S(1)} %copy-done, bf16[8,128,512]{2,1,0:T(8,128)(2,1)S(1)} %get-tuple-element.11.vt_ref, f32[528,128]{1,0:T(8,128)S(1)} %get-tuple-element.12.bias_ref, ...), custom_call_target="tpu_custom_call" | custom-call | tf_op jit(solution)/shard_map/second/pallas_call | solution.py:28
  41.2 0.0 collective-permute-done.1.came_ref
  41.2 0.1 couple.1
  41.4 10.3 %all_to_all.21.in_ref = bf16[16,40,128]{2,1,0:T(8,128)(2,1)S(1)} all-to-all(bf16[16,40,128]{2,1,0:T(8,128)(2,1)S(1)} %couple.1), channel_id=1, replica_groups=mesh['y'=4,'z'=8,'x'=4,'c'=2] {'y','x'}, dimensions={0} | all-to-all | bytes 327680 | tf_op jit(solution)/shard_map/all_to_all | solution.py:49
  51.6 0.1 merge.1
  51.7 9.9 %all_to_all.22.in_ref = bf16[8,40,128]{2,1,0:T(8,128)(2,1)S(1)} all-to-all(bf16[8,40,128]{2,1,0:T(8,128)(2,1)S(1)} %merge.1), channel_id=1, replica_groups=mesh['y'=4,'z'=8,'x'=4,'c'=2] {'z'}, dimensions={0} | all-to-all | bytes 163840 | tf_op jit(solution)/shard_map/all_to_all | solution.py:49
  61.6 9.8 %all_to_all.23.in_ref = bf16[16,32,128]{2,1,0:T(8,128)(2,1)S(1)} all-to-all(bf16[16,32,128]{2,1,0:T(8,128)(2,1)S(1)} %finish.1), channel_id=1, replica_groups=mesh['y'=4,'z'=8,'x'=4,'c'=2] {'y','x'}, dimensions={0} | all-to-all | bytes 262144 | tf_op jit(solution)/shard_map/all_to_all | solution.py:49
  71.4 4.2 %collective-permute-start.2 = (bf16[16,32,128]{2,1,0:T(8,128)(2,1)S(1)}, bf16[16,32,128]{2,1,0:T(8,128)(2,1)S(1)}, u32[]{:S(2)}, u32[]{:S(2)}) collective-permute-start(bf16[16,32,128]{2,1,0:T(8,128)(2,1)S(1)} %all_to_all.23.in_ref), channel_id=1, source_target_pairs={{0,1},{1,0},{2,3},{3,2},{4,5},{5,4},{6,7},{7,6},{8,9},{9,8},{10,11... | collective-permute-start | bytes 393224 | tf_op jit(solution)/shard_map/ppermute | solution.py:53
  75.6 0.2 half.1.own_ref
  75.8 0.8 collective-permute-done.2.in_ref
  76.6 0.9 %place.1 = bf16[16,8192]{1,0:T(8,128)(2,1)} custom-call(bf16[16,32,128]{2,1,0:T(8,128)(2,1)S(1)} %collective-permute-done.2.in_ref, bf16[16,4096]{1,0:T(8,128)(2,1)S(1)} %half.1.own_ref), custom_call_target="tpu_custom_call" | custom-call | tf_op jit(solution)/shard_map/place/pallas_call | solution.py:28
  (1 shorter events, 0.0 us)
Async XLA Ops:
  0.0 38.3 %copy-start = (bf16[512,1024]{1,0:T(8,128)(2,1)S(1)}, bf16[512,1024]{1,0:T(8,128)(2,1)}, u32[]{:S(2)}) copy-start(bf16[512,1024]{1,0:T(8,128)(2,1)} %k_ref.3) | copy-start | bytes 3145732
  0.0 0.8 copy-start.2
  0.8 0.7 copy-start.4
  1.5 0.7 copy-start.5
  2.1 0.7 copy-start.6
  2.8 0.7 copy-start.7
  3.5 0.7 copy-start.8
  33.0 5.3 %collective-permute-start = (bf16[128,8,128]{2,1,0:T(8,128)(2,1)S(1)}, bf16[128,8,128]{2,1,0:T(8,128)(2,1)S(1)}, u32[]{:S(2)}, u32[]{:S(2)}) collective-permute-start(bf16[128,8,128]{2,1,0:T(8,128)(2,1)S(1)} %all_to_all.20.own_ref.in_ref), channel_id=1, source_target_pairs={{0,1},{1,0},{2,3},{3,2},{4,5},{5,4},{6,7},{7,6},{8,9},{9,8},{10,11... | collective-permute-start | bytes 786440 | tf_op jit(solution)/shard_map/ppermute | solution.py:53
  36.0 1.2 %copy-start.1 = (bf16[512,1024]{1,0:T(8,128)(2,1)S(1)}, bf16[512,1024]{1,0:T(8,128)(2,1)}, u32[]{:S(2)}) copy-start(bf16[512,1024]{1,0:T(8,128)(2,1)} %v_ref.1) | copy-start | bytes 3145732
  37.2 0.7 copy-start.3
  39.7 1.5 %collective-permute-start.1 = (bf16[16,40,128]{2,1,0:T(8,128)(2,1)S(1)}, bf16[16,40,128]{2,1,0:T(8,128)(2,1)S(1)}, u32[]{:S(2)}, u32[]{:S(2)}) collective-permute-start(bf16[16,40,128]{2,1,0:T(8,128)(2,1)S(1)} %get-tuple-element.14), channel_id=1, source_target_pairs={{0,1},{1,0},{2,3},{3,2},{4,5},{5,4},{6,7},{7,6},{8,9},{9,8},{10,11... | collective-permute-start | bytes 491528 | tf_op jit(solution)/shard_map/ppermute | solution.py:53
  71.4 5.2 %collective-permute-start.2 = (bf16[16,32,128]{2,1,0:T(8,128)(2,1)S(1)}, bf16[16,32,128]{2,1,0:T(8,128)(2,1)S(1)}, u32[]{:S(2)}, u32[]{:S(2)}) collective-permute-start(bf16[16,32,128]{2,1,0:T(8,128)(2,1)S(1)} %all_to_all.23.in_ref), channel_id=1, source_target_pairs={{0,1},{1,0},{2,3},{3,2},{4,5},{5,4},{6,7},{7,6},{8,9},{9,8},{10,11... | collective-permute-start | bytes 393224 | tf_op jit(solution)/shard_map/ppermute | solution.py:53

commit v6 on v5

--- a/solution.py
+++ b/solution.py
@@ -23,6 +23,8 @@
 VMEM = pl.BlockSpec(memory_space=pltpu.VMEM)
 NT = (((1,), (1,)), ((), ()))
 
+HBM = pl.BlockSpec(memory_space=pltpu.HBM)
+
 
 def call(body, name, out_shape, *args, specs=None, scratch=(), limit=8 << 20):
     return pl.pallas_call(
@@ -69,8 +71,16 @@
     return jnp.where(hit, 1.0, 0.0).astype(BF16)
 
 
-def pack_body(q_ref, k_ref, v_ref, *rest):
-    out_ref = rest[-1]
+def pack_body(*refs):
+    out_ref, q_ref, k_ref, v_ref, sems = refs[6], *refs[10:]
+    copies = [
+        pltpu.make_async_copy(source, target, sems.at[n])
+        for n, (source, target) in enumerate(zip(refs[:6], (q_ref, k_ref, v_ref, *refs[7:10])))
+    ]
+    for copy in copies:
+        copy.start()
+    for copy in copies:
+        copy.wait()
     turn = (lax.axis_index("x") % 2) * 64
 
     def spread(count, at):
@@ -140,13 +150,18 @@
     return tile.astype(BF16)
 
 
-def ready_body(pos_ref, seg_ref, held_ref, v_ref, vt_ref, bias_ref, table_ref):
+def ready_body(pos_ref, seg_ref, held_ref, k_hbm, v_hbm, bias_ref, table_ref, k_ref, vt_ref, v_ref, sems):
+    copies = []
+    for g in range(KVH):
+        at = slice(g * HD, (g + 1) * HD)
+        copies.append(pltpu.make_async_copy(v_hbm.at[:, at], v_ref.at[:, at], sems.at[g]))
+    copies.append(pltpu.make_async_copy(k_hbm, k_ref, sems.at[KVH]))
+    for copy in copies:
+        copy.start()
     lane = lanes((ROWS, 128))
     cosine, sine = rope_tables(pos_ref[...], lane % 64)
     table_ref[0] = cosine
     table_ref[1] = jnp.where(lane < 64, -sine, sine)
-    for g in range(KVH):
-        vt_ref[g] = v_ref[:, g * HD : (g + 1) * HD].T
     pick = where_one(rows_of((ROWS, 128)) == lane % ROWS)
     kinds = where_one(rows_of((8, ROWS)) == seg_ref[...])
     wanted = dot(kinds, pick, NN).astype(BF16)
@@ -155,6 +170,10 @@
         bias_ref[part * 128 : (part + 1) * 128, :] = (dot(have, wanted, TN) - 1.0) * -HIDDEN
     seen = dot(kinds, wanted, TN) * jnp.where(rows_of((ROWS, 128)) <= lane % ROWS, 1.0, 0.0)
     bias_ref[512:, :] = (seen - 1.0) * -HIDDEN
+    for g in range(KVH):
+        copies[g].wait()
+        vt_ref[g] = v_ref[:, g * HD : (g + 1) * HD].T
+    copies[KVH].wait()
 
 
 def placing(core):
@@ -333,33 +352,39 @@
     cache_segments,
 ):
     shape = jax.ShapeDtypeStruct
-    span_segments = span_segments.reshape(1, ROWS)
-    cache_segments = cache_segments.reshape(4, 128)
-    tiles = call(
-        pack_body,
-        "pack",
-        shape((128, 8, 128), BF16),
+    small = (
         queries,
         span_keys.T,
         span_values.T,
         positions,
-        span_segments,
-        cache_segments,
+        span_segments.reshape(1, ROWS),
+        cache_segments.reshape(4, 128),
+    )
+    tiles, positions, span_segments, cache_segments = call(
+        pack_body,
+        "pack",
+        (shape((128, 8, 128), BF16), *(shape(a.shape, a.dtype) for a in small[3:])),
+        *(pltpu.with_memory_space_constraint(a, pltpu.HBM) for a in small),
+        specs=[HBM] * 6,
+        scratch=[pltpu.VMEM(a.shape, a.dtype) for a in small[:3]] + [pltpu.SemaphoreType.DMA((6,))],
     )
     tiles = exchange(tiles, CHIPS)
     came = swap(tiles)
-    turned_values, bias, tables = call(
+    bias, tables, keys, turned_values = call(
         ready_body,
         "ready",
         (
-            shape((KVH, HD, 512), BF16),
             shape((512 + ROWS, 128), F32),
             shape((2, ROWS, 128), F32),
+            shape((512, KVH * HD), BF16),
+            shape((KVH, HD, 512), BF16),
         ),
         positions,
         span_segments,
         cache_segments,
-        cache_values,
+        *(pltpu.with_memory_space_constraint(a, pltpu.HBM) for a in (cache_keys, cache_values)),
+        specs=[VMEM] * 3 + [HBM] * 2,
+        scratch=[pltpu.VMEM((512, KVH * HD), BF16), pltpu.SemaphoreType.DMA((KVH + 1,))],
     )
     message = shape((16, 40, 128), BF16)
     parts, q = call(
@@ -369,13 +394,13 @@
         tiles,
         came,
         tables,
-        cache_keys,
+        keys,
         turned_values,
         bias,
     )
     other = swap(parts)
     parts = call(
-        second_body, "second", message, q, cache_keys, turned_values, bias, tiles, came, tables
+        second_body, "second", message, q, keys, turned_values, bias, tiles, came, tables
     )
     parts = call(couple_body, "couple", message, parts, other)
     parts = exchange(parts, PLANE)

time: 77.9 us -> 74.1 us (0.951)
  local copies, waits for them, and re-layouts: 6.06 us -> 0 us
  Pallas kernels: 4.71 us -> 7.12 us
    unnamed x18 -> x0, local copies, waits for them, and re-layouts: 6.06 us -> none
    pallas_call x9, Pallas kernels: 4.71 us -> 7.12 us  [call(): pl.pallas_call(body, name=name, out_shape=out_shape, in_specs=specs or [V...]
  transfers between devices with their start and end apart: 3 -> 3, of which waited for: 1 -> 1; matrix products, arithmetic and copies ran while one was open for 0% -> 0% of each run, Pallas kernels for 3% -> 5%
where the time goes in v6:
time: 74.1 us; the launch traced here: 73.8 us
  blocking collectives  58.5 us (79%)
  starting transfers between devices  7.32 us (10%)
  Pallas kernels  7.12 us (10%)
  waiting for transfers between devices  0.78 us (1%)
    all_to_all x4, blocking collectives, exchange(): return lax.all_to_all(tiles, axes, 0, 0, tiled=True)  58.5 us
    ppermute x3, starting transfers between devices, swap(): return lax.ppermute(value, 'c', ((0, 1), (1, 0)))  7.32 us
    pallas_call x9, Pallas kernels, call(): pl.pallas_call(body, name=name, out_shape=out_shape, in_specs=specs or [V...  7.12 us
  transfers between devices with their start and end apart: 3, of which 1 were waited for; matrix products, arithmetic and copies ran while one was open for 0% of the time, Pallas kernels for 5%

profile of v6, /device:TPU:1, one launch (start us, length us, event | category | flops | bytes accessed | tf_op | source)
XLA Modules:
  0.0 73.8 jit_solution(14393470793997206768)
XLA Ops:
  0.0 1.0 %pack.1 = (bf16[128,8,128]{2,1,0:T(8,128)(2,1)S(1)}, s32[3,16]{1,0:T(4,128)S(1)}, s32[1,16]{1,0:T(1,128)S(1)}, s32[4,128]{1,0:T(4,128)S(1)}) custom-call(bf16[16,32]{1,0:T(8,128)(2,1)} %refs_0_.1, bf16[4,16]{1,0:T(4,128)(2,1)} %bitcast.5, bf16[4,16]{1,0:T(4,128)(2,1)} %bitcast.6, s32[3,16]{1,0:T(4,128)} %refs_3_.1, s32[1,16]{1,0:T(1,128)} %bitcast.7, ...), custom_call_target="tpu_custom_call" | custom-call | tf_op jit(solution)/shard_map/pack/pallas_call | solution.py:30
  1.0 28.6 %all_to_all.20.own_ref.in_ref = bf16[128,8,128]{2,1,0:T(8,128)(2,1)S(1)} all-to-all(bf16[128,8,128]{2,1,0:T(8,128)(2,1)S(1)} %get-tuple-element.15), channel_id=1, replica_groups=mesh['y'=4,'z'=8,'x'=4,'c'=2] {'y','z','x'}, dimensions={0} | all-to-all | bytes 524288 | tf_op jit(solution)/shard_map/all_to_all | solution.py:51
  29.7 3.0 %collective-permute-start = (bf16[128,8,128]{2,1,0:T(8,128)(2,1)S(1)}, bf16[128,8,128]{2,1,0:T(8,128)(2,1)S(1)}, u32[]{:S(2)}, u32[]{:S(2)}) collective-permute-start(bf16[128,8,128]{2,1,0:T(8,128)(2,1)S(1)} %all_to_all.20.own_ref.in_ref), channel_id=1, source_target_pairs={{0,1},{1,0},{2,3},{3,2},{4,5},{5,4},{6,7},{7,6},{8,9},{9,8},{10,11... | collective-permute-start | bytes 786440 | tf_op jit(solution)/shard_map/ppermute | solution.py:55
  32.7 2.0 %ready.1 = (f32[528,128]{1,0:T(8,128)S(1)}, f32[2,16,128]{2,1,0:T(8,128)S(1)}, bf16[512,1024]{1,0:T(8,128)(2,1)S(1)}, bf16[8,128,512]{2,1,0:T(8,128)(2,1)S(1)}) custom-call(s32[3,16]{1,0:T(4,128)S(1)} %get-tuple-element.16.pos_ref, s32[1,16]{1,0:T(1,128)S(1)} %get-tuple-element.17.seg_ref, s32[4,128]{1,0:T(4,128)S(1)} %get-tuple-element.18.held_ref, ...), custom_call_target="tpu_custom_call" | custom-call | tf_op jit(solution)/shard_map/ready/pallas_call | solution.py:30
  34.7 0.0 collective-permute-done.came_ref
  34.7 1.3 %first.1 = (bf16[16,40,128]{2,1,0:T(8,128)(2,1)S(1)}, bf16[1024,128]{1,0:T(8,128)(2,1)S(1)}) custom-call(bf16[128,8,128]{2,1,0:T(8,128)(2,1)S(1)} %all_to_all.20.own_ref.in_ref, bf16[128,8,128]{2,1,0:T(8,128)(2,1)S(1)} %collective-permute-done.came_ref, f32[2,16,128]{2,1,0:T(8,128)S(1)} %get-tuple-element.19.table_ref, ...), custom_call_target="tpu_custom_call" | custom-call | tf_op jit(solution)/shard_map/first/pallas_call | solution.py:30
  36.0 0.1 collective-permute-start.1
  36.1 1.4 %second.1.own_ref = bf16[16,40,128]{2,1,0:T(8,128)(2,1)S(1)} custom-call(bf16[1024,128]{1,0:T(8,128)(2,1)S(1)} %get-tuple-element.23.q_ref, bf16[512,1024]{1,0:T(8,128)(2,1)S(1)} %get-tuple-element.20.k_ref, bf16[8,128,512]{2,1,0:T(8,128)(2,1)S(1)} %get-tuple-element.21.vt_ref, f32[528,128]{1,0:T(8,128)S(1)} %get-tuple-element.22.bias_ref, ...), custom_call_target="tpu_custom_call" | custom-call | tf_op jit(solution)/shard_map/second/pallas_call | solution.py:30
  37.5 0.0 collective-permute-done.1.came_ref
  37.5 0.1 couple.1
  37.7 10.2 %all_to_all.21.in_ref = bf16[16,40,128]{2,1,0:T(8,128)(2,1)S(1)} all-to-all(bf16[16,40,128]{2,1,0:T(8,128)(2,1)S(1)} %couple.1), channel_id=1, replica_groups=mesh['y'=4,'z'=8,'x'=4,'c'=2] {'y','x'}, dimensions={0} | all-to-all | bytes 327680 | tf_op jit(solution)/shard_map/all_to_all | solution.py:51
  47.9 0.1 merge.1
  48.0 9.9 %all_to_all.22.in_ref = bf16[8,40,128]{2,1,0:T(8,128)(2,1)S(1)} all-to-all(bf16[8,40,128]{2,1,0:T(8,128)(2,1)S(1)} %merge.1), channel_id=1, replica_groups=mesh['y'=4,'z'=8,'x'=4,'c'=2] {'z'}, dimensions={0} | all-to-all | bytes 163840 | tf_op jit(solution)/shard_map/all_to_all | solution.py:51
  57.9 9.8 %all_to_all.23.in_ref = bf16[16,32,128]{2,1,0:T(8,128)(2,1)S(1)} all-to-all(bf16[16,32,128]{2,1,0:T(8,128)(2,1)S(1)} %finish.1), channel_id=1, replica_groups=mesh['y'=4,'z'=8,'x'=4,'c'=2] {'y','x'}, dimensions={0} | all-to-all | bytes 262144 | tf_op jit(solution)/shard_map/all_to_all | solution.py:51
  67.7 4.2 %collective-permute-start.2 = (bf16[16,32,128]{2,1,0:T(8,128)(2,1)S(1)}, bf16[16,32,128]{2,1,0:T(8,128)(2,1)S(1)}, u32[]{:S(2)}, u32[]{:S(2)}) collective-permute-start(bf16[16,32,128]{2,1,0:T(8,128)(2,1)S(1)} %all_to_all.23.in_ref), channel_id=1, source_target_pairs={{0,1},{1,0},{2,3},{3,2},{4,5},{5,4},{6,7},{7,6},{8,9},{9,8},{10,11... | collective-permute-start | bytes 393224 | tf_op jit(solution)/shard_map/ppermute | solution.py:55
  71.9 0.2 half.1.own_ref
  72.1 0.8 %collective-permute-done.2.in_ref = bf16[16,32,128]{2,1,0:T(8,128)(2,1)S(1)} collective-permute-done((bf16[16,32,128]{2,1,0:T(8,128)(2,1)S(1)}, bf16[16,32,128]{2,1,0:T(8,128)(2,1)S(1)}, u32[]{:S(2)}, u32[]{:S(2)}) %collective-permute-start.2) | collective-permute-done | bytes 131104 | tf_op jit(solution)/shard_map/ppermute | solution.py:55
  72.9 0.9 %place.1 = bf16[16,8192]{1,0:T(8,128)(2,1)} custom-call(bf16[16,32,128]{2,1,0:T(8,128)(2,1)S(1)} %collective-permute-done.2.in_ref, bf16[16,4096]{1,0:T(8,128)(2,1)S(1)} %half.1.own_ref), custom_call_target="tpu_custom_call" | custom-call | tf_op jit(solution)/shard_map/place/pallas_call | solution.py:30
  (1 shorter events, 0.0 us)
Async XLA Ops:
  29.7 5.0 %collective-permute-start = (bf16[128,8,128]{2,1,0:T(8,128)(2,1)S(1)}, bf16[128,8,128]{2,1,0:T(8,128)(2,1)S(1)}, u32[]{:S(2)}, u32[]{:S(2)}) collective-permute-start(bf16[128,8,128]{2,1,0:T(8,128)(2,1)S(1)} %all_to_all.20.own_ref.in_ref), channel_id=1, source_target_pairs={{0,1},{1,0},{2,3},{3,2},{4,5},{5,4},{6,7},{7,6},{8,9},{9,8},{10,11... | collective-permute-start | bytes 786440 | tf_op jit(solution)/shard_map/ppermute | solution.py:55
  36.0 1.5 %collective-permute-start.1 = (bf16[16,40,128]{2,1,0:T(8,128)(2,1)S(1)}, bf16[16,40,128]{2,1,0:T(8,128)(2,1)S(1)}, u32[]{:S(2)}, u32[]{:S(2)}) collective-permute-start(bf16[16,40,128]{2,1,0:T(8,128)(2,1)S(1)} %get-tuple-element.24), channel_id=1, source_target_pairs={{0,1},{1,0},{2,3},{3,2},{4,5},{5,4},{6,7},{7,6},{8,9},{9,8},{10,11... | collective-permute-start | bytes 491528 | tf_op jit(solution)/shard_map/ppermute | solution.py:55
  67.7 5.2 %collective-permute-start.2 = (bf16[16,32,128]{2,1,0:T(8,128)(2,1)S(1)}, bf16[16,32,128]{2,1,0:T(8,128)(2,1)S(1)}, u32[]{:S(2)}, u32[]{:S(2)}) collective-permute-start(bf16[16,32,128]{2,1,0:T(8,128)(2,1)S(1)} %all_to_all.23.in_ref), channel_id=1, source_target_pairs={{0,1},{1,0},{2,3},{3,2},{4,5},{5,4},{6,7},{7,6},{8,9},{9,8},{10,11... | collective-permute-start | bytes 393224 | tf_op jit(solution)/shard_map/ppermute | solution.py:55

commit v7 on v6

--- a/solution.py
+++ b/solution.py
@@ -72,14 +72,14 @@
 
 
 def pack_body(*refs):
-    out_ref, q_ref, k_ref, v_ref, sems = refs[6], *refs[10:]
+    out_ref, q_ref, k_ref, v_ref, sems = refs[7], *refs[12:]
     copies = [
         pltpu.make_async_copy(source, target, sems.at[n])
-        for n, (source, target) in enumerate(zip(refs[:6], (q_ref, k_ref, v_ref, *refs[7:10])))
+        for n, (source, target) in enumerate(zip(refs[:7], (q_ref, k_ref, v_ref, *refs[8:12])))
     ]
     for copy in copies:
         copy.start()
-    for copy in copies:
+    for copy in copies[:6]:
         copy.wait()
     turn = (lax.axis_index("x") % 2) * 64
 
@@ -95,6 +95,7 @@
     tile = tile.astype(BF16)
     for d in range(out_ref.shape[0]):
         out_ref[d] = tile
+    copies[6].wait()
 
 
 def turn(angle):
@@ -150,12 +151,11 @@
     return tile.astype(BF16)
 
 
-def ready_body(pos_ref, seg_ref, held_ref, k_hbm, v_hbm, bias_ref, table_ref, k_ref, vt_ref, v_ref, sems):
+def ready_body(pos_ref, seg_ref, held_ref, v_hbm, bias_ref, table_ref, vt_ref, v_ref, sems):
     copies = []
     for g in range(KVH):
         at = slice(g * HD, (g + 1) * HD)
         copies.append(pltpu.make_async_copy(v_hbm.at[:, at], v_ref.at[:, at], sems.at[g]))
-    copies.append(pltpu.make_async_copy(k_hbm, k_ref, sems.at[KVH]))
     for copy in copies:
         copy.start()
     lane = lanes((ROWS, 128))
@@ -173,7 +173,6 @@
     for g in range(KVH):
         copies[g].wait()
         vt_ref[g] = v_ref[:, g * HD : (g + 1) * HD].T
-    copies[KVH].wait()
 
 
 def placing(core):
@@ -203,77 +202,107 @@
             q_ref[head * 16 + late * 8 : head * 16 + late * 8 + 8, :] = part[n]
 
 
-def attend(q, k, vt, bias, span):
-    factor = LOG2E / HD**0.5
-    scores = [dot(k, q, NT) * factor + bias]
-    if span is not None:
-        scores.append(dot(span[0], q, NT) * factor + span[2])
-    peak = functools.reduce(
-        jnp.maximum, [jnp.max(s, axis=0, keepdims=True) for s in scores], jnp.float32(NONE)
-    )
+FACTOR = LOG2E / HD**0.5
+
+
+def softened(scores):
+    peak = jnp.maximum(jnp.max(scores, axis=0, keepdims=True), NONE)
     high, low = split_pair(peak)
     peak = high + low
-    weights = [jnp.exp2(s - peak) for s in scores]
-    total = sum(jnp.sum(w, axis=0, keepdims=True) for w in weights)
-    out = dot(vt, weights[0].astype(BF16), NN)
-    if span is not None:
-        out = out + dot(span[1], weights[1].astype(BF16), TN)
-    return out.astype(BF16), state_rows(peak, total)
-
-
-def emit(out_ref, i, result):
-    for n in range(4):
-        out_ref[i * 4 + n, 0:32, :] = result[0][n * 32 : (n + 1) * 32]
-        out_ref[i * 4 + n, 32:40, :] = result[1]
+    weights = jnp.exp2(scores - peak)
+    return weights.astype(BF16), peak, jnp.sum(weights, axis=0, keepdims=True)
 
 
 def heads_at(base, i):
     return pl.ds(pl.multiple_of((base + i) * 128, 128), 128)
 
 
+def attend(base, q_ref, k_ref, vt_ref, bias_ref, out_ref):
+    for pair in ((0, 1), (2, 3)):
+        scores = [
+            dot(k_ref[:, heads_at(base, i)], q_ref[heads_at(base, i), :], NT) * FACTOR
+            + bias_ref[0:512, :]
+            for i in pair
+        ]
+        parts = [softened(s) for s in scores]
+        outs = [dot(vt_ref[base + i], w[0], NN) for i, w in zip(pair, parts)]
+        for i, out, (_, peak, total) in zip(pair, outs, parts):
+            emit(out_ref, i * 4, out.astype(BF16), state_rows(peak, total))
+
+
+def emit(out_ref, first, out, state):
+    for n in range(4):
+        out_ref[first + n, 0:32, :] = out[n * 32 : (n + 1) * 32]
+        out_ref[first + n, 32:40, :] = state
+
+
 def first_body(own_ref, came_ref, table_ref, k_ref, vt_ref, bias_ref, out_ref, q_ref):
     join(own_ref, came_ref, table_ref, q_ref)
-    base = (1 - lax.axis_index("c")) * 4
-    for i in range(4):
-        at = heads_at(base, i)
-        emit(out_ref, i, attend(q_ref[at, :], k_ref[:, at], vt_ref[base + i], bias_ref[0:512, :], None))
+    attend((1 - lax.axis_index("c")) * 4, q_ref, k_ref, vt_ref, bias_ref, out_ref)
 
 
 def second_body(q_ref, k_ref, vt_ref, bias_ref, in_ref, came_ref, table_ref, out_ref):
     c, y = lax.axis_index("c"), lax.axis_index("y")
-    base = c * 4
-    lane = lanes((8, 128))
-    duty = (lax.axis_index("z") == 0) & (lax.axis_index("x") == 0)
-    g = base + y
-    start = (g // 2) * 32 + (g % 2) * 16
-    found = []
-    for kind in range(2):
-        parts = []
-        for late in range(2):
-            value = jnp.zeros((8, 128), F32)
-            for n in range(16):
-                own, came = in_ref[start + n].astype(F32), came_ref[start + n].astype(F32)
-                pair = (jnp.where(c == 0, own, came), jnp.where(c == 0, came, own))
-                for core in range(2):
-                    at = n * 8 + core * 4
-                    held = (1 - n % 2) * 64 + kind * 32 + late * 16
-                    value = jnp.where(
-                        (lane >= at) & (lane < at + 4),
-                        move(pair[core], at - held),
-                        value,
-                    )
-            parts.append(value)
-        if kind == 0:
-            parts = [
-                rotate(v, table_ref[0, n * 8 : n * 8 + 8, :], table_ref[1, n * 8 : n * 8 + 8, :])
-                for n, v in enumerate(parts)
-            ]
-        found.append(jnp.concatenate(parts, axis=0).astype(BF16))
-    for i in range(4):
-        at = heads_at(base, i)
-        absent = jnp.where(duty & (y == i), 0.0, HIDDEN)
-        span = (found[0], found[1], bias_ref[512:, :] + absent)
-        emit(out_ref, i, attend(q_ref[at, :], k_ref[:, at], vt_ref[base + i], bias_ref[0:512, :], span))
+    attend(c * 4, q_ref, k_ref, vt_ref, bias_ref, out_ref)
+
+    @pl.when((lax.axis_index("z") == 0) & (lax.axis_index("x") == 0))
+    def _():
+        lane = lanes((8, 128))
+        g = c * 4 + y
+        start = (g // 2) * 32 + (g % 2) * 16
+        found = []
+        for kind in range(2):
+            parts = []
+            for late in range(2):
+                value = jnp.zeros((8, 128), F32)
+                for n in range(16):
+                    own, came = in_ref[start + n].astype(F32), came_ref[start + n].astype(F32)
+                    pair = (jnp.where(c == 0, own, came), jnp.where(c == 0, came, own))
+                    for core in range(2):
+                        at = n * 8 + core * 4
+                        held = (1 - n % 2) * 64 + kind * 32 + late * 16
+                        value = jnp.where(
+                            (lane >= at) & (lane < at + 4), move(pair[core], at - held), value
+                        )
+                parts.append(value)
+            if kind == 0:
+                parts = [
+                    rotate(v, table_ref[0, n * 8 : n * 8 + 8, :], table_ref[1, n * 8 : n * 8 + 8, :])
+                    for n, v in enumerate(parts)
+                ]
+            found.append(jnp.concatenate(parts, axis=0).astype(BF16))
+        scores = dot(found[0], q_ref[heads_at(c * 4, y), :], NT) * FACTOR + bias_ref[512:, :]
+        weights, peak, total = softened(scores)
+        own = dot(found[1], weights, TN)
+        for n in range(4):
+            tile = out_ref.at[y * 4 + n]
+            out, peaks, totals = merge(
+                [tile[0:32, :].astype(F32), own[n * 32 : (n + 1) * 32]],
+                *zip(state_of(tile, 32), (peak, total)),
+            )
+            tile[0:32, :] = out.astype(BF16)
+            tile[32:40, :] = state_rows(peaks, totals)
+
+
+def state_of(ref, at):
+    state = ref[at : at + 8, :].astype(F32)
+    return state[0:1] + state[1:2], state[2:3] + state[3:4]
+
+
+def merge(outs, peaks, totals):
+    peak = functools.reduce(jnp.maximum, peaks)
+    factors = [jnp.exp2(p - peak) for p in peaks]
+    out = sum(o * f for o, f in zip(outs, factors))
+    return out, peak, sum(t * f for t, f in zip(totals, factors))
+
+
+def merged(refs, at=0):
+    outs = [ref[at : at + 32, :].astype(F32) for ref in refs]
+    return merge(outs, *zip(*(state_of(ref, at + 32) for ref in refs)))
+
+
+def tiles_of(ref):
+    return [ref.at[n] for n in range(ref.shape[0])]
 
 
 def couple_body(own_ref, came_ref, out_ref):
@@ -283,62 +312,38 @@
         out_ref[n, 32:40, :] = state_rows(peak, total)
 
 
-def merged(refs):
-    peaks, totals = [], []
-    for ref in refs:
-        state = ref[32:40, :].astype(F32)
-        peaks.append(state[0:1] + state[1:2])
-        totals.append(state[2:3] + state[3:4])
-    peak = functools.reduce(jnp.maximum, peaks)
-    out = jnp.zeros((32, 128), F32)
-    total = jnp.zeros((1, 128), F32)
-    for n, ref in enumerate(refs):
-        factor = jnp.exp2(peaks[n] - peak)
-        out = out + ref[0:32, :].astype(F32) * factor
-        total = total + totals[n] * factor
-    return out, peak, total
-
-
 def merge_body(in_ref, out_ref):
-    out, peak, total = merged([in_ref.at[n] for n in range(in_ref.shape[0])])
-    out = out.astype(BF16)
-    state = state_rows(peak, total)
+    out, peak, total = merged(tiles_of(in_ref))
+    out_ref[0:32, :] = out.astype(BF16)
+    out_ref[32:40, :] = state_rows(peak, total)
+
+
+def pair_body(own_ref, came_ref, out_ref):
+    first = lax.axis_index("c") == 0
+    own, came = own_ref[...].astype(F32), came_ref[...].astype(F32)
+    tiles = (jnp.where(first, own, came).astype(BF16), jnp.where(first, came, own).astype(BF16))
     for d in range(out_ref.shape[0]):
-        out_ref[d, 0:32, :] = out
-        out_ref[d, 32:40, :] = state
+        for n, tile in enumerate(tiles):
+            out_ref[d, n * 40 : (n + 1) * 40, :] = tile
 
 
 def finish_body(in_ref, out_ref):
-    out, _, total = merged([in_ref.at[n] for n in range(in_ref.shape[0])])
-    out = (out / total).astype(BF16)
-    for d in range(out_ref.shape[0]):
-        out_ref[d] = out
-
-
-def turned(in_ref, store):
+    for n in range(2):
+        out, _, total = merged(tiles_of(in_ref), n * 40)
+        out = (out / total).astype(BF16)
+        for d in range(out_ref.shape[0]):
+            out_ref[d, n * 32 : (n + 1) * 32, :] = out
+
+
+def place_body(in_ref, out_ref):
     eye = where_one(rows_of((128, 128)) == lanes((128, 128)))
-    for g in range(4):
-        block = dot(eye, in_ref[g * 4 : (g + 1) * 4].reshape(128, 128), NT).astype(BF16)
+    for g in range(KVH):
+        half, y = divmod(g, 4)
+        block = in_ref[y * 4 : (y + 1) * 4, half * 32 : (half + 1) * 32, :].reshape(128, 128)
+        block = dot(eye, block, NT).astype(BF16)
         for i in range(8):
-            store((g * 8 + i) * HD, block[i * ROWS : (i + 1) * ROWS])
-
-
-def half_body(in_ref, out_ref):
-    def store(at, piece):
-        out_ref[:, at : at + HD] = piece
-
-    turned(in_ref, store)
-
-
-def place_body(in_ref, own_ref, out_ref):
-    c = lax.axis_index("c")
-    half = H * HD // 2
-    out_ref[:, pl.ds(pl.multiple_of(c * half, half), half)] = own_ref[...]
-
-    def store(at, piece):
-        out_ref[:, pl.ds(pl.multiple_of((1 - c) * half + at, HD), HD)] = piece
-
-    turned(in_ref, store)
+            at = (g * 8 + i) * HD
+            out_ref[:, at : at + HD] = block[i * ROWS : (i + 1) * ROWS]
 
 
 def per_device(
@@ -359,32 +364,32 @@
         positions,
         span_segments.reshape(1, ROWS),
         cache_segments.reshape(4, 128),
-    )
-    tiles, positions, span_segments, cache_segments = call(
+        cache_keys,
+    )
+    tiles, positions, span_segments, cache_segments, keys = call(
         pack_body,
         "pack",
         (shape((128, 8, 128), BF16), *(shape(a.shape, a.dtype) for a in small[3:])),
         *(pltpu.with_memory_space_constraint(a, pltpu.HBM) for a in small),
-        specs=[HBM] * 6,
-        scratch=[pltpu.VMEM(a.shape, a.dtype) for a in small[:3]] + [pltpu.SemaphoreType.DMA((6,))],
+        specs=[HBM] * 7,
+        scratch=[pltpu.VMEM(a.shape, a.dtype) for a in small[:3]] + [pltpu.SemaphoreType.DMA((7,))],
     )
     tiles = exchange(tiles, CHIPS)
     came = swap(tiles)
-    bias, tables, keys, turned_values = call(
+    bias, tables, turned_values = call(
         ready_body,
         "ready",
         (
             shape((512 + ROWS, 128), F32),
             shape((2, ROWS, 128), F32),
-            shape((512, KVH * HD), BF16),
             shape((KVH, HD, 512), BF16),
         ),
         positions,
         span_segments,
         cache_segments,
-        *(pltpu.with_memory_space_constraint(a, pltpu.HBM) for a in (cache_keys, cache_values)),
-        specs=[VMEM] * 3 + [HBM] * 2,
-        scratch=[pltpu.VMEM((512, KVH * HD), BF16), pltpu.SemaphoreType.DMA((KVH + 1,))],
+        pltpu.with_memory_space_constraint(cache_values, pltpu.HBM),
+        specs=[VMEM] * 3 + [HBM],
+        scratch=[pltpu.VMEM((512, KVH * HD), BF16), pltpu.SemaphoreType.DMA((KVH,))],
     )
     message = shape((16, 40, 128), BF16)
     parts, q = call(
@@ -404,13 +409,12 @@
     )
     parts = call(couple_body, "couple", message, parts, other)
     parts = exchange(parts, PLANE)
-    parts = call(merge_body, "merge", shape((8, 40, 128), BF16), parts)
+    part = call(merge_body, "merge", shape((40, 128), BF16), parts)
+    parts = call(pair_body, "pair", shape((8, 80, 128), BF16), part, swap(part))
     parts = exchange(parts, ("z",))
-    whole = call(finish_body, "finish", shape((16, 32, 128), BF16), parts)
+    whole = call(finish_body, "finish", shape((16, 64, 128), BF16), parts)
     whole = exchange(whole, PLANE)
-    other = swap(whole)
-    own = call(half_body, "half", shape((ROWS, H * HD // 2), BF16), whole)
-    return call(place_body, "place", shape((ROWS, H * HD), BF16), other, own)
+    return call(place_body, "place", shape((ROWS, H * HD), BF16), whole)
 
 
 def solution(mesh):

time: 74.1 us -> 74.5 us (level)
  starting transfers between devices: 7.32 us -> 4.49 us
  blocking collectives: 58.5 us -> 61 us
    ppermute x3, starting transfers between devices: 7.32 us -> 4.49 us  [swap(): return lax.ppermute(value, 'c', ((0, 1), (1, 0)))]
    all_to_all x4, blocking collectives: 58.5 us -> 61 us  [exchange(): return lax.all_to_all(tiles, axes, 0, 0, tiled=True)]
  transfers between devices with their start and end apart: 3 -> 3, of which waited for: 1 -> 2; matrix products, arithmetic and copies ran while one was open for 0% -> 0% of each run, Pallas kernels for 5% -> 4%
where the time goes in v7:
time: 74.5 us; the launch traced here: 73.7 us
  blocking collectives  61 us (82%)
  Pallas kernels  7.2 us (10%)
  starting transfers between devices  4.49 us (6%)
  waiting for transfers between devices  0.89 us (1%)
    all_to_all x4, blocking collectives, exchange(): return lax.all_to_all(tiles, axes, 0, 0, tiled=True)  61 us
    pallas_call x9, Pallas kernels, call(): pl.pallas_call(body, name=name, out_shape=out_shape, in_specs=specs or [V...  7.2 us
    ppermute x3, starting transfers between devices, swap(): return lax.ppermute(value, 'c', ((0, 1), (1, 0)))  4.49 us
  transfers between devices with their start and end apart: 3, of which 2 were waited for; matrix products, arithmetic and copies ran while one was open for 0% of the time, Pallas kernels for 4%

profile of v7, /device:TPU:1, one launch (start us, length us, event | category | flops | bytes accessed | tf_op | source)
XLA Modules:
  0.0 73.7 jit_solution(2412704146351257163)
XLA Ops:
  0.0 1.4 %pack.1 = (bf16[128,8,128]{2,1,0:T(8,128)(2,1)S(1)}, s32[3,16]{1,0:T(4,128)S(1)}, s32[1,16]{1,0:T(1,128)S(1)}, s32[4,128]{1,0:T(4,128)S(1)}, bf16[512,1024]{1,0:T(8,128)(2,1)S(1)}) custom-call(bf16[16,32]{1,0:T(8,128)(2,1)} %refs_0_.1, bf16[4,16]{1,0:T(4,128)(2,1)} %bitcast.5, bf16[4,16]{1,0:T(4,128)(2,1)} %bitcast.6, s32[3,16]{1,0:T(4,128)} %refs_3_.1, ...), custom_call_target="tpu_custom_call" | custom-call | tf_op jit(solution)/shard_map/pack/pallas_call | solution.py:30
  1.4 28.6 %all_to_all.20.own_ref.in_ref = bf16[128,8,128]{2,1,0:T(8,128)(2,1)S(1)} all-to-all(bf16[128,8,128]{2,1,0:T(8,128)(2,1)S(1)} %get-tuple-element.15), channel_id=1, replica_groups=mesh['y'=4,'z'=8,'x'=4,'c'=2] {'y','z','x'}, dimensions={0} | all-to-all | bytes 524288 | tf_op jit(solution)/shard_map/all_to_all | solution.py:51
  30.0 3.0 %collective-permute-start = (bf16[128,8,128]{2,1,0:T(8,128)(2,1)S(1)}, bf16[128,8,128]{2,1,0:T(8,128)(2,1)S(1)}, u32[]{:S(2)}, u32[]{:S(2)}) collective-permute-start(bf16[128,8,128]{2,1,0:T(8,128)(2,1)S(1)} %all_to_all.20.own_ref.in_ref), channel_id=1, source_target_pairs={{0,1},{1,0},{2,3},{3,2},{4,5},{5,4},{6,7},{7,6},{8,9},{9,8},{10,11... | collective-permute-start | bytes 786440 | tf_op jit(solution)/shard_map/ppermute | solution.py:55
  33.0 1.9 %ready.1 = (f32[528,128]{1,0:T(8,128)S(1)}, f32[2,16,128]{2,1,0:T(8,128)S(1)}, bf16[8,128,512]{2,1,0:T(8,128)(2,1)S(1)}) custom-call(s32[3,16]{1,0:T(4,128)S(1)} %get-tuple-element.16.pos_ref, s32[1,16]{1,0:T(1,128)S(1)} %get-tuple-element.17.seg_ref, s32[4,128]{1,0:T(4,128)S(1)} %get-tuple-element.18.held_ref, bf16[512,1024]{1,0:T(8,128)(2,1)} %v_hbm.1), custom_call_target="tpu_custom_call" | custom-call | tf_op jit(solution)/shard_map/ready/pallas_call | solution.py:30
  35.0 0.0 collective-permute-done.came_ref
  35.0 1.3 %first.1 = (bf16[16,40,128]{2,1,0:T(8,128)(2,1)S(1)}, bf16[1024,128]{1,0:T(8,128)(2,1)S(1)}) custom-call(bf16[128,8,128]{2,1,0:T(8,128)(2,1)S(1)} %all_to_all.20.own_ref.in_ref, bf16[128,8,128]{2,1,0:T(8,128)(2,1)S(1)} %collective-permute-done.came_ref, f32[2,16,128]{2,1,0:T(8,128)S(1)} %get-tuple-element.19.table_ref, ...), custom_call_target="tpu_custom_call" | custom-call | tf_op jit(solution)/shard_map/first/pallas_call | solution.py:30
  36.3 0.1 collective-permute-start.1
  36.4 1.3 %second.1.own_ref = bf16[16,40,128]{2,1,0:T(8,128)(2,1)S(1)} custom-call(bf16[1024,128]{1,0:T(8,128)(2,1)S(1)} %get-tuple-element.23.q_ref, bf16[512,1024]{1,0:T(8,128)(2,1)S(1)} %get-tuple-element.20.k_ref, bf16[8,128,512]{2,1,0:T(8,128)(2,1)S(1)} %get-tuple-element.21.vt_ref, f32[528,128]{1,0:T(8,128)S(1)} %get-tuple-element.22.bias_ref, ...), custom_call_target="tpu_custom_call" | custom-call | tf_op jit(solution)/shard_map/second/pallas_call | solution.py:30
  37.7 0.1 collective-permute-done.1.came_ref
  37.8 0.1 couple.1
  37.9 10.5 %all_to_all.21.in_ref = bf16[16,40,128]{2,1,0:T(8,128)(2,1)S(1)} all-to-all(bf16[16,40,128]{2,1,0:T(8,128)(2,1)S(1)} %couple.1), channel_id=1, replica_groups=mesh['y'=4,'z'=8,'x'=4,'c'=2] {'y','x'}, dimensions={0} | all-to-all | bytes 327680 | tf_op jit(solution)/shard_map/all_to_all | solution.py:51
  48.4 0.1 merge.1.own_ref
  48.5 1.4 %collective-permute-start.2 = (bf16[40,128]{1,0:T(8,128)(2,1)S(1)}, bf16[40,128]{1,0:T(8,128)(2,1)S(1)}, u32[]{:S(2)}, u32[]{:S(2)}) collective-permute-start(bf16[40,128]{1,0:T(8,128)(2,1)S(1)} %merge.1.own_ref), channel_id=1, source_target_pairs={{0,1},{1,0},{2,3},{3,2},{4,5},{5,4},{6,7},{7,6},{8,9},{9,8},{10,11... | collective-permute-start | bytes 30728 | tf_op jit(solution)/shard_map/ppermute | solution.py:55
  49.9 0.8 %collective-permute-done.2.came_ref = bf16[40,128]{1,0:T(8,128)(2,1)S(1)} collective-permute-done((bf16[40,128]{1,0:T(8,128)(2,1)S(1)}, bf16[40,128]{1,0:T(8,128)(2,1)S(1)}, u32[]{:S(2)}, u32[]{:S(2)}) %collective-permute-start.2) | collective-permute-done | bytes 10272 | tf_op jit(solution)/shard_map/ppermute | solution.py:55
  50.7 11.5 %all_to_all.22.in_ref = bf16[8,80,128]{2,1,0:T(8,128)(2,1)S(1)} all-to-all(bf16[8,80,128]{2,1,0:T(8,128)(2,1)S(1)} %pair.1), channel_id=1, replica_groups=mesh['y'=4,'z'=8,'x'=4,'c'=2] {'z'}, dimensions={0} | all-to-all | bytes 327680 | tf_op jit(solution)/shard_map/all_to_all | solution.py:51
  62.3 0.1 finish.1
  62.3 10.3 %all_to_all.23.in_ref = bf16[16,64,128]{2,1,0:T(8,128)(2,1)S(1)} all-to-all(bf16[16,64,128]{2,1,0:T(8,128)(2,1)S(1)} %finish.1), channel_id=1, replica_groups=mesh['y'=4,'z'=8,'x'=4,'c'=2] {'y','x'}, dimensions={0} | all-to-all | bytes 524288 | tf_op jit(solution)/shard_map/all_to_all | solution.py:51
  72.7 1.0 %place.1 = bf16[16,8192]{1,0:T(8,128)(2,1)} custom-call(bf16[16,64,128]{2,1,0:T(8,128)(2,1)S(1)} %all_to_all.23.in_ref), custom_call_target="tpu_custom_call" | custom-call | tf_op jit(solution)/shard_map/place/pallas_call | solution.py:30
  (1 shorter events, 0.0 us)
Async XLA Ops:
  30.0 5.0 %collective-permute-start = (bf16[128,8,128]{2,1,0:T(8,128)(2,1)S(1)}, bf16[128,8,128]{2,1,0:T(8,128)(2,1)S(1)}, u32[]{:S(2)}, u32[]{:S(2)}) collective-permute-start(bf16[128,8,128]{2,1,0:T(8,128)(2,1)S(1)} %all_to_all.20.own_ref.in_ref), channel_id=1, source_target_pairs={{0,1},{1,0},{2,3},{3,2},{4,5},{5,4},{6,7},{7,6},{8,9},{9,8},{10,11... | collective-permute-start | bytes 786440 | tf_op jit(solution)/shard_map/ppermute | solution.py:55
  36.3 1.5 %collective-permute-start.1 = (bf16[16,40,128]{2,1,0:T(8,128)(2,1)S(1)}, bf16[16,40,128]{2,1,0:T(8,128)(2,1)S(1)}, u32[]{:S(2)}, u32[]{:S(2)}) collective-permute-start(bf16[16,40,128]{2,1,0:T(8,128)(2,1)S(1)} %get-tuple-element.24), channel_id=1, source_target_pairs={{0,1},{1,0},{2,3},{3,2},{4,5},{5,4},{6,7},{7,6},{8,9},{9,8},{10,11... | collective-permute-start | bytes 491528 | tf_op jit(solution)/shard_map/ppermute | solution.py:55
  48.5 2.2 %collective-permute-start.2 = (bf16[40,128]{1,0:T(8,128)(2,1)S(1)}, bf16[40,128]{1,0:T(8,128)(2,1)S(1)}, u32[]{:S(2)}, u32[]{:S(2)}) collective-permute-start(bf16[40,128]{1,0:T(8,128)(2,1)S(1)} %merge.1.own_ref), channel_id=1, source_target_pairs={{0,1},{1,0},{2,3},{3,2},{4,5},{5,4},{6,7},{7,6},{8,9},{9,8},{10,11... | collective-permute-start | bytes 30728 | tf_op jit(solution)/shard_map/ppermute | solution.py:55

commit v8 on v7

--- a/solution.py
+++ b/solution.py
@@ -55,6 +55,10 @@
     return lax.ppermute(value, "c", ((0, 1), (1, 0)))
 
 
+def stay(value):
+    return lax.ppermute(value, "c", ((0, 0), (1, 1)))
+
+
 def rows_of(shape):
     return lax.broadcasted_iota(jnp.int32, shape, 0)
 
@@ -72,14 +76,14 @@
 
 
 def pack_body(*refs):
-    out_ref, q_ref, k_ref, v_ref, sems = refs[7], *refs[12:]
+    out_ref, q_ref, k_ref, v_ref, sems = refs[6], *refs[10:]
     copies = [
         pltpu.make_async_copy(source, target, sems.at[n])
-        for n, (source, target) in enumerate(zip(refs[:7], (q_ref, k_ref, v_ref, *refs[8:12])))
+        for n, (source, target) in enumerate(zip(refs[:6], (q_ref, k_ref, v_ref, *refs[7:10])))
     ]
     for copy in copies:
         copy.start()
-    for copy in copies[:6]:
+    for copy in copies:
         copy.wait()
     turn = (lax.axis_index("x") % 2) * 64
 
@@ -95,7 +99,6 @@
     tile = tile.astype(BF16)
     for d in range(out_ref.shape[0]):
         out_ref[d] = tile
-    copies[6].wait()
 
 
 def turn(angle):
@@ -151,13 +154,7 @@
     return tile.astype(BF16)
 
 
-def ready_body(pos_ref, seg_ref, held_ref, v_hbm, bias_ref, table_ref, vt_ref, v_ref, sems):
-    copies = []
-    for g in range(KVH):
-        at = slice(g * HD, (g + 1) * HD)
-        copies.append(pltpu.make_async_copy(v_hbm.at[:, at], v_ref.at[:, at], sems.at[g]))
-    for copy in copies:
-        copy.start()
+def ready_body(pos_ref, seg_ref, held_ref, v_ref, bias_ref, table_ref, vt_ref):
     lane = lanes((ROWS, 128))
     cosine, sine = rope_tables(pos_ref[...], lane % 64)
     table_ref[0] = cosine
@@ -171,7 +168,6 @@
     seen = dot(kinds, wanted, TN) * jnp.where(rows_of((ROWS, 128)) <= lane % ROWS, 1.0, 0.0)
     bias_ref[512:, :] = (seen - 1.0) * -HIDDEN
     for g in range(KVH):
-        copies[g].wait()
         vt_ref[g] = v_ref[:, g * HD : (g + 1) * HD].T
 
 
@@ -278,14 +274,14 @@
             tile = out_ref.at[y * 4 + n]
             out, peaks, totals = merge(
                 [tile[0:32, :].astype(F32), own[n * 32 : (n + 1) * 32]],
-                *zip(state_of(tile, 32), (peak, total)),
+                *zip(state_of(tile), (peak, total)),
             )
             tile[0:32, :] = out.astype(BF16)
             tile[32:40, :] = state_rows(peaks, totals)
 
 
-def state_of(ref, at):
-    state = ref[at : at + 8, :].astype(F32)
+def state_of(ref):
+    state = ref[32:40, :].astype(F32)
     return state[0:1] + state[1:2], state[2:3] + state[3:4]
 
 
@@ -296,9 +292,9 @@
     return out, peak, sum(t * f for t, f in zip(totals, factors))
 
 
-def merged(refs, at=0):
-    outs = [ref[at : at + 32, :].astype(F32) for ref in refs]
-    return merge(outs, *zip(*(state_of(ref, at + 32) for ref in refs)))
+def merged(refs):
+    outs = [ref[0:32, :].astype(F32) for ref in refs]
+    return merge(outs, *zip(*map(state_of, refs)))
 
 
 def tiles_of(ref):
@@ -314,8 +310,15 @@
 
 def merge_body(in_ref, out_ref):
     out, peak, total = merged(tiles_of(in_ref))
-    out_ref[0:32, :] = out.astype(BF16)
-    out_ref[32:40, :] = state_rows(peak, total)
+    out, state = out.astype(BF16), state_rows(peak, total)
+    for d in range(out_ref.shape[0]):
+        out_ref[d, 0:32, :] = out
+        out_ref[d, 32:40, :] = state
+
+
+def finish_body(in_ref, out_ref):
+    out, _, total = merged(tiles_of(in_ref))
+    out_ref[...] = (out / total).astype(BF16)
 
 
 def pair_body(own_ref, came_ref, out_ref):
@@ -324,15 +327,7 @@
     tiles = (jnp.where(first, own, came).astype(BF16), jnp.where(first, came, own).astype(BF16))
     for d in range(out_ref.shape[0]):
         for n, tile in enumerate(tiles):
-            out_ref[d, n * 40 : (n + 1) * 40, :] = tile
-
-
-def finish_body(in_ref, out_ref):
-    for n in range(2):
-        out, _, total = merged(tiles_of(in_ref), n * 40)
-        out = (out / total).astype(BF16)
-        for d in range(out_ref.shape[0]):
-            out_ref[d, n * 32 : (n + 1) * 32, :] = out
+            out_ref[d, n * 32 : (n + 1) * 32, :] = tile
 
 
 def place_body(in_ref, out_ref):
@@ -364,17 +359,17 @@
         positions,
         span_segments.reshape(1, ROWS),
         cache_segments.reshape(4, 128),
-        cache_keys,
-    )
-    tiles, positions, span_segments, cache_segments, keys = call(
+    )
+    tiles, positions, span_segments, cache_segments = call(
         pack_body,
         "pack",
         (shape((128, 8, 128), BF16), *(shape(a.shape, a.dtype) for a in small[3:])),
         *(pltpu.with_memory_space_constraint(a, pltpu.HBM) for a in small),
-        specs=[HBM] * 7,
-        scratch=[pltpu.VMEM(a.shape, a.dtype) for a in small[:3]] + [pltpu.SemaphoreType.DMA((7,))],
-    )
-    tiles = exchange(tiles, CHIPS)
+        specs=[HBM] * 6,
+        scratch=[pltpu.VMEM(a.shape, a.dtype) for a in small[:3]] + [pltpu.SemaphoreType.DMA((6,))],
+    )
+    keys, values = stay(cache_keys), stay(cache_values)
+    tiles, keys, values = lax.optimization_barrier((exchange(tiles, CHIPS), keys, values))
     came = swap(tiles)
     bias, tables, turned_values = call(
         ready_body,
@@ -387,9 +382,7 @@
         positions,
         span_segments,
         cache_segments,
-        pltpu.with_memory_space_constraint(cache_values, pltpu.HBM),
-        specs=[VMEM] * 3 + [HBM],
-        scratch=[pltpu.VMEM((512, KVH * HD), BF16), pltpu.SemaphoreType.DMA((KVH,))],
+        values,
     )
     message = shape((16, 40, 128), BF16)
     parts, q = call(
@@ -409,10 +402,10 @@
     )
     parts = call(couple_body, "couple", message, parts, other)
     parts = exchange(parts, PLANE)
-    part = call(merge_body, "merge", shape((40, 128), BF16), parts)
-    parts = call(pair_body, "pair", shape((8, 80, 128), BF16), part, swap(part))
+    parts = call(merge_body, "merge", shape((8, 40, 128), BF16), parts)
     parts = exchange(parts, ("z",))
-    whole = call(finish_body, "finish", shape((16, 64, 128), BF16), parts)
+    tile = call(finish_body, "finish", shape((32, 128), BF16), parts)
+    whole = call(pair_body, "pair", shape((16, 64, 128), BF16), tile, swap(tile))
     whole = exchange(whole, PLANE)
     return call(place_body, "place", shape((ROWS, H * HD), BF16), whole)
 

time: 74.5 us -> 75.5 us (1.013)
  starting transfers between devices: 4.49 us -> 8.87 us
  Pallas kernels: 7.2 us -> 5.27 us
  blocking collectives: 61 us -> 59.4 us
    ppermute x0 -> x2, starting transfers between devices: none -> 2.45 us  [stay(): return lax.ppermute(value, 'c', ((0, 0), (1, 1)))]
    pallas_call x9, Pallas kernels: 7.2 us -> 5.27 us  [call(): pl.pallas_call(body, name=name, out_shape=out_shape, in_specs=specs or [V...]
    ppermute x3, starting transfers between devices: 4.49 us -> 6.42 us  [swap(): return lax.ppermute(value, 'c', ((0, 1), (1, 0)))]
    all_to_all x4, blocking collectives: 61 us -> 59.4 us  [exchange(): return lax.all_to_all(tiles, axes, 0, 0, tiled=True)]
  transfers between devices with their start and end apart: 3 -> 5, of which waited for: 2 -> 2; matrix products, arithmetic and copies ran while one was open for 0% -> 0% of each run, Pallas kernels for 4% -> 4%
where the time goes in v8:
time: 75.5 us; the launch traced here: 75.2 us
  blocking collectives  59.4 us (79%)
  starting transfers between devices  8.87 us (12%)
  Pallas kernels  5.27 us (7%)
  waiting for transfers between devices  1.6 us (2%)
    all_to_all x4, blocking collectives, exchange(): return lax.all_to_all(tiles, axes, 0, 0, tiled=True)  59.4 us
    ppermute x3, starting transfers between devices, swap(): return lax.ppermute(value, 'c', ((0, 1), (1, 0)))  6.42 us
    pallas_call x9, Pallas kernels, call(): pl.pallas_call(body, name=name, out_shape=out_shape, in_specs=specs or [V...  5.27 us
    ppermute x2, starting transfers between devices, stay(): return lax.ppermute(value, 'c', ((0, 0), (1, 1)))  2.45 us
    ppermute x3, waiting for transfers between devices, swap(): return lax.ppermute(value, 'c', ((0, 1), (1, 0)))  1.59 us
  transfers between devices with their start and end apart: 5, of which 2 were waited for; matrix products, arithmetic and copies ran while one was open for 0% of the time, Pallas kernels for 4%

profile of v8, /device:TPU:1, one launch (start us, length us, event | category | flops | bytes accessed | tf_op | source)
XLA Modules:
  0.0 75.2 jit_solution(337278914856984355)
XLA Ops:
  0.0 1.2 %collective-permute-start = (bf16[512,1024]{1,0:T(8,128)(2,1)}, bf16[512,1024]{1,0:T(8,128)(2,1)S(1)}, u32[]{:S(2)}, u32[]{:S(2)}) collective-permute-start(bf16[512,1024]{1,0:T(8,128)(2,1)} %param.13), channel_id=1, source_target_pairs={{0,0},{1,1},{2,2},{3,3},{4,4},{5,5},{6,6},{7,7},{8,8},{9,9},{10,10... | collective-permute-start | bytes 3145736 | tf_op jit(solution)/shard_map/ppermute | solution.py:59
  1.2 1.2 %collective-permute-start.1 = (bf16[512,1024]{1,0:T(8,128)(2,1)}, bf16[512,1024]{1,0:T(8,128)(2,1)S(1)}, u32[]{:S(2)}, u32[]{:S(2)}) collective-permute-start(bf16[512,1024]{1,0:T(8,128)(2,1)} %param.14), channel_id=1, source_target_pairs={{0,0},{1,1},{2,2},{3,3},{4,4},{5,5},{6,6},{7,7},{8,8},{9,9},{10,10... | collective-permute-start | bytes 3145736 | tf_op jit(solution)/shard_map/ppermute | solution.py:59
  2.5 1.0 %pack.1 = (bf16[128,8,128]{2,1,0:T(8,128)(2,1)S(1)}, s32[3,16]{1,0:T(4,128)S(1)}, s32[1,16]{1,0:T(1,128)S(1)}, s32[4,128]{1,0:T(4,128)S(1)}) custom-call(bf16[16,32]{1,0:T(8,128)(2,1)} %refs_0_.1, bf16[4,16]{1,0:T(4,128)(2,1)} %bitcast.5, bf16[4,16]{1,0:T(4,128)(2,1)} %bitcast.6, s32[3,16]{1,0:T(4,128)} %refs_3_.1, s32[1,16]{1,0:T(1,128)} %bitcast.7, ...), custom_call_target="tpu_custom_call" | custom-call | tf_op jit(solution)/shard_map/pack/pallas_call | solution.py:30
  3.5 28.6 %all_to_all.20.own_ref.in_ref = bf16[128,8,128]{2,1,0:T(8,128)(2,1)S(1)} all-to-all(bf16[128,8,128]{2,1,0:T(8,128)(2,1)S(1)} %get-tuple-element.17), channel_id=1, replica_groups=mesh['y'=4,'z'=8,'x'=4,'c'=2] {'y','z','x'}, dimensions={0} | all-to-all | bytes 524288 | tf_op jit(solution)/shard_map/all_to_all | solution.py:51
  32.1 0.0 collective-permute-done.k_ref
  32.1 0.0 collective-permute-done.1.v_ref
  32.1 3.0 %collective-permute-start.2 = (bf16[128,8,128]{2,1,0:T(8,128)(2,1)S(1)}, bf16[128,8,128]{2,1,0:T(8,128)(2,1)S(1)}, u32[]{:S(2)}, u32[]{:S(2)}) collective-permute-start(bf16[128,8,128]{2,1,0:T(8,128)(2,1)S(1)} %all_to_all.20.own_ref.in_ref), channel_id=1, source_target_pairs={{0,1},{1,0},{2,3},{3,2},{4,5},{5,4},{6,7},{7,6},{8,9},{9,8},{10,11... | collective-permute-start | bytes 786440 | tf_op jit(solution)/shard_map/ppermute | solution.py:55
  35.1 0.4 ready.1
  35.5 0.8 %collective-permute-done.2.came_ref = bf16[128,8,128]{2,1,0:T(8,128)(2,1)S(1)} collective-permute-done((bf16[128,8,128]{2,1,0:T(8,128)(2,1)S(1)}, bf16[128,8,128]{2,1,0:T(8,128)(2,1)S(1)}, u32[]{:S(2)}, u32[]{:S(2)}) %collective-permute-start.2) | collective-permute-done | bytes 262176 | tf_op jit(solution)/shard_map/ppermute | solution.py:55
  36.3 1.3 %first.1 = (bf16[16,40,128]{2,1,0:T(8,128)(2,1)S(1)}, bf16[1024,128]{1,0:T(8,128)(2,1)S(1)}) custom-call(bf16[128,8,128]{2,1,0:T(8,128)(2,1)S(1)} %all_to_all.20.own_ref.in_ref, bf16[128,8,128]{2,1,0:T(8,128)(2,1)S(1)} %collective-permute-done.2.came_ref, f32[2,16,128]{2,1,0:T(8,128)S(1)} %get-tuple-element.23.table_ref, ...), custom_call_target="tpu_custom_call" | custom-call | tf_op jit(solution)/shard_map/first/pallas_call | solution.py:30
  37.6 0.5 collective-permute-start.3
  38.1 1.3 %second.1.own_ref = bf16[16,40,128]{2,1,0:T(8,128)(2,1)S(1)} custom-call(bf16[1024,128]{1,0:T(8,128)(2,1)S(1)} %get-tuple-element.27.q_ref, bf16[512,1024]{1,0:T(8,128)(2,1)S(1)} %collective-permute-done.k_ref, bf16[8,128,512]{2,1,0:T(8,128)(2,1)S(1)} %get-tuple-element.25.vt_ref, f32[528,128]{1,0:T(8,128)S(1)} %get-tuple-element.26.bias_ref, ...), custom_call_target="tpu_custom_call" | custom-call | tf_op jit(solution)/shard_map/second/pallas_call | solution.py:30
  39.4 0.0 collective-permute-done.3.came_ref
  39.4 0.1 couple.1
  39.5 10.0 %all_to_all.21.in_ref = bf16[16,40,128]{2,1,0:T(8,128)(2,1)S(1)} all-to-all(bf16[16,40,128]{2,1,0:T(8,128)(2,1)S(1)} %couple.1), channel_id=1, replica_groups=mesh['y'=4,'z'=8,'x'=4,'c'=2] {'y','x'}, dimensions={0} | all-to-all | bytes 327680 | tf_op jit(solution)/shard_map/all_to_all | solution.py:51
  49.5 0.1 merge.1
  49.6 9.9 %all_to_all.22.in_ref = bf16[8,40,128]{2,1,0:T(8,128)(2,1)S(1)} all-to-all(bf16[8,40,128]{2,1,0:T(8,128)(2,1)S(1)} %merge.1), channel_id=1, replica_groups=mesh['y'=4,'z'=8,'x'=4,'c'=2] {'z'}, dimensions={0} | all-to-all | bytes 163840 | tf_op jit(solution)/shard_map/all_to_all | solution.py:51
  59.5 2.9 %collective-permute-start.4 = (bf16[32,128]{1,0:T(8,128)(2,1)S(1)}, bf16[32,128]{1,0:T(8,128)(2,1)S(1)}, u32[]{:S(2)}, u32[]{:S(2)}) collective-permute-start(bf16[32,128]{1,0:T(8,128)(2,1)S(1)} %finish.1.own_ref), channel_id=1, source_target_pairs={{0,1},{1,0},{2,3},{3,2},{4,5},{5,4},{6,7},{7,6},{8,9},{9,8},{10,11... | collective-permute-start | bytes 24584 | tf_op jit(solution)/shard_map/ppermute | solution.py:55
  62.4 0.8 %collective-permute-done.4.came_ref = bf16[32,128]{1,0:T(8,128)(2,1)S(1)} collective-permute-done((bf16[32,128]{1,0:T(8,128)(2,1)S(1)}, bf16[32,128]{1,0:T(8,128)(2,1)S(1)}, u32[]{:S(2)}, u32[]{:S(2)}) %collective-permute-start.4) | collective-permute-done | bytes 8224 | tf_op jit(solution)/shard_map/ppermute | solution.py:55
  63.3 10.9 %all_to_all.23.in_ref = bf16[16,64,128]{2,1,0:T(8,128)(2,1)S(1)} all-to-all(bf16[16,64,128]{2,1,0:T(8,128)(2,1)S(1)} %pair.1), channel_id=1, replica_groups=mesh['y'=4,'z'=8,'x'=4,'c'=2] {'y','x'}, dimensions={0} | all-to-all | bytes 524288 | tf_op jit(solution)/shard_map/all_to_all | solution.py:51
  74.2 1.0 %place.1 = bf16[16,8192]{1,0:T(8,128)(2,1)} custom-call(bf16[16,64,128]{2,1,0:T(8,128)(2,1)S(1)} %all_to_all.23.in_ref), custom_call_target="tpu_custom_call" | custom-call | tf_op jit(solution)/shard_map/place/pallas_call | solution.py:30
  (2 shorter events, 0.1 us)
Async XLA Ops:
  0.0 32.1 %collective-permute-start = (bf16[512,1024]{1,0:T(8,128)(2,1)}, bf16[512,1024]{1,0:T(8,128)(2,1)S(1)}, u32[]{:S(2)}, u32[]{:S(2)}) collective-permute-start(bf16[512,1024]{1,0:T(8,128)(2,1)} %param.13), channel_id=1, source_target_pairs={{0,0},{1,1},{2,2},{3,3},{4,4},{5,5},{6,6},{7,7},{8,8},{9,9},{10,10... | collective-permute-start | bytes 3145736 | tf_op jit(solution)/shard_map/ppermute | solution.py:59
  1.2 30.9 %collective-permute-start.1 = (bf16[512,1024]{1,0:T(8,128)(2,1)}, bf16[512,1024]{1,0:T(8,128)(2,1)S(1)}, u32[]{:S(2)}, u32[]{:S(2)}) collective-permute-start(bf16[512,1024]{1,0:T(8,128)(2,1)} %param.14), channel_id=1, source_target_pairs={{0,0},{1,1},{2,2},{3,3},{4,4},{5,5},{6,6},{7,7},{8,8},{9,9},{10,10... | collective-permute-start | bytes 3145736 | tf_op jit(solution)/shard_map/ppermute | solution.py:59
  32.1 4.2 %collective-permute-start.2 = (bf16[128,8,128]{2,1,0:T(8,128)(2,1)S(1)}, bf16[128,8,128]{2,1,0:T(8,128)(2,1)S(1)}, u32[]{:S(2)}, u32[]{:S(2)}) collective-permute-start(bf16[128,8,128]{2,1,0:T(8,128)(2,1)S(1)} %all_to_all.20.own_ref.in_ref), channel_id=1, source_target_pairs={{0,1},{1,0},{2,3},{3,2},{4,5},{5,4},{6,7},{7,6},{8,9},{9,8},{10,11... | collective-permute-start | bytes 786440 | tf_op jit(solution)/shard_map/ppermute | solution.py:55
  37.6 1.8 %collective-permute-start.3 = (bf16[16,40,128]{2,1,0:T(8,128)(2,1)S(1)}, bf16[16,40,128]{2,1,0:T(8,128)(2,1)S(1)}, u32[]{:S(2)}, u32[]{:S(2)}) collective-permute-start(bf16[16,40,128]{2,1,0:T(8,128)(2,1)S(1)} %get-tuple-element.28), channel_id=1, source_target_pairs={{0,1},{1,0},{2,3},{3,2},{4,5},{5,4},{6,7},{7,6},{8,9},{9,8},{10,11... | collective-permute-start | bytes 491528 | tf_op jit(solution)/shard_map/ppermute | solution.py:55
  59.5 3.8 %collective-permute-start.4 = (bf16[32,128]{1,0:T(8,128)(2,1)S(1)}, bf16[32,128]{1,0:T(8,128)(2,1)S(1)}, u32[]{:S(2)}, u32[]{:S(2)}) collective-permute-start(bf16[32,128]{1,0:T(8,128)(2,1)S(1)} %finish.1.own_ref), channel_id=1, source_target_pairs={{0,1},{1,0},{2,3},{3,2},{4,5},{5,4},{6,7},{7,6},{8,9},{9,8},{10,11... | collective-permute-start | bytes 24584 | tf_op jit(solution)/shard_map/ppermute | solution.py:55

commit v9 on v8

--- a/solution.py
+++ b/solution.py
@@ -26,13 +26,13 @@
 HBM = pl.BlockSpec(memory_space=pltpu.HBM)
 
 
-def call(body, name, out_shape, *args, specs=None, scratch=(), limit=8 << 20):
+def call(body, name, out_shape, *args, specs=None, scratch=(), limit=8 << 20, out_specs=None):
     return pl.pallas_call(
         body,
         name=name,
         out_shape=out_shape,
         in_specs=specs or [VMEM] * len(args),
-        out_specs=jax.tree.map(lambda _: VMEM, out_shape),
+        out_specs=out_specs or jax.tree.map(lambda _: VMEM, out_shape),
         scratch_shapes=scratch,
         compiler_params=pltpu.CompilerParams(vmem_limit_bytes=limit),
     )(*args)
@@ -53,10 +53,6 @@
 
 def swap(value):
     return lax.ppermute(value, "c", ((0, 1), (1, 0)))
-
-
-def stay(value):
-    return lax.ppermute(value, "c", ((0, 0), (1, 1)))
 
 
 def rows_of(shape):
@@ -154,7 +150,13 @@
     return tile.astype(BF16)
 
 
-def ready_body(pos_ref, seg_ref, held_ref, v_ref, bias_ref, table_ref, vt_ref):
+def ready_body(pos_ref, seg_ref, held_ref, k_hbm, v_hbm, bias_ref, table_ref, k_ref, vt_ref, v_ref, sems):
+    copies = [
+        pltpu.make_async_copy(source, target, sems.at[n])
+        for n, (source, target) in enumerate(((v_hbm, v_ref), (k_hbm, k_ref)))
+    ]
+    for copy in copies:
+        copy.start()
     lane = lanes((ROWS, 128))
     cosine, sine = rope_tables(pos_ref[...], lane % 64)
     table_ref[0] = cosine
@@ -167,8 +169,10 @@
         bias_ref[part * 128 : (part + 1) * 128, :] = (dot(have, wanted, TN) - 1.0) * -HIDDEN
     seen = dot(kinds, wanted, TN) * jnp.where(rows_of((ROWS, 128)) <= lane % ROWS, 1.0, 0.0)
     bias_ref[512:, :] = (seen - 1.0) * -HIDDEN
+    copies[0].wait()
     for g in range(KVH):
         vt_ref[g] = v_ref[:, g * HD : (g + 1) * HD].T
+    copies[1].wait()
 
 
 def placing(core):
@@ -330,7 +334,8 @@
             out_ref[d, n * 32 : (n + 1) * 32, :] = tile
 
 
-def place_body(in_ref, out_ref):
+def place_body(in_ref, out_hbm, out_ref, sems):
+    copies = []
     eye = where_one(rows_of((128, 128)) == lanes((128, 128)))
     for g in range(KVH):
         half, y = divmod(g, 4)
@@ -339,6 +344,14 @@
         for i in range(8):
             at = (g * 8 + i) * HD
             out_ref[:, at : at + HD] = block[i * ROWS : (i + 1) * ROWS]
+        if g % 2:
+            part = slice((g - 1) * 8 * HD, (g + 1) * 8 * HD)
+            copies.append(
+                pltpu.make_async_copy(out_ref.at[:, part], out_hbm.at[:, part], sems.at[g // 2])
+            )
+            copies[-1].start()
+    for copy in copies:
+        copy.wait()
 
 
 def per_device(
@@ -368,21 +381,23 @@
         specs=[HBM] * 6,
         scratch=[pltpu.VMEM(a.shape, a.dtype) for a in small[:3]] + [pltpu.SemaphoreType.DMA((6,))],
     )
-    keys, values = stay(cache_keys), stay(cache_values)
-    tiles, keys, values = lax.optimization_barrier((exchange(tiles, CHIPS), keys, values))
+    tiles = exchange(tiles, CHIPS)
     came = swap(tiles)
-    bias, tables, turned_values = call(
+    bias, tables, keys, turned_values = call(
         ready_body,
         "ready",
         (
             shape((512 + ROWS, 128), F32),
             shape((2, ROWS, 128), F32),
+            shape((512, KVH * HD), BF16),
             shape((KVH, HD, 512), BF16),
         ),
         positions,
         span_segments,
         cache_segments,
-        values,
+        *(pltpu.with_memory_space_constraint(a, pltpu.HBM) for a in (cache_keys, cache_values)),
+        specs=[VMEM] * 3 + [HBM] * 2,
+        scratch=[pltpu.VMEM((512, KVH * HD), BF16), pltpu.SemaphoreType.DMA((2,))],
     )
     message = shape((16, 40, 128), BF16)
     parts, q = call(
@@ -407,7 +422,14 @@
     tile = call(finish_body, "finish", shape((32, 128), BF16), parts)
     whole = call(pair_body, "pair", shape((16, 64, 128), BF16), tile, swap(tile))
     whole = exchange(whole, PLANE)
-    return call(place_body, "place", shape((ROWS, H * HD), BF16), whole)
+    return call(
+        place_body,
+        "place",
+        shape((ROWS, H * HD), BF16),
+        whole,
+        scratch=[pltpu.VMEM((ROWS, H * HD), BF16), pltpu.SemaphoreType.DMA((4,))],
+        out_specs=HBM,
+    )
 
 
 def solution(mesh):

time: 75.5 us -> 73.4 us (0.972)
  starting transfers between devices: 8.87 us -> 5.64 us
  Pallas kernels: 5.27 us -> 6.64 us
    ppermute x2 -> x0, starting transfers between devices: 2.45 us -> none  [stay(): return lax.ppermute(value, 'c', ((0, 0), (1, 1)))]
    pallas_call x9, Pallas kernels: 5.27 us -> 6.64 us  [call(): pl.pallas_call(body, name=name, out_shape=out_shape, in_specs=specs or [V...]
    ppermute x3, starting transfers between devices: 6.42 us -> 5.64 us  [swap(): return lax.ppermute(value, 'c', ((0, 1), (1, 0)))]
  transfers between devices with their start and end apart: 5 -> 3, of which waited for: 2 -> 2; matrix products, arithmetic and copies ran while one was open for 0% -> 0% of each run, Pallas kernels for 4% -> 4%
where the time goes in v9:
time: 73.4 us; the launch traced here: 73.1 us
  blocking collectives  59.9 us (82%)
  Pallas kernels  6.64 us (9%)
  starting transfers between devices  5.64 us (8%)
  waiting for transfers between devices  0.89 us (1%)
    all_to_all x4, blocking collectives, exchange(): return lax.all_to_all(tiles, axes, 0, 0, tiled=True)  59.9 us
    pallas_call x9, Pallas kernels, call(): pl.pallas_call(body, name=name, out_shape=out_shape, in_specs=specs or [V...  6.64 us
    ppermute x3, starting transfers between devices, swap(): return lax.ppermute(value, 'c', ((0, 1), (1, 0)))  5.64 us
  transfers between devices with their start and end apart: 3, of which 2 were waited for; matrix products, arithmetic and copies ran while one was open for 0% of the time, Pallas kernels for 4%

profile of v9, /device:TPU:1, one launch (start us, length us, event | category | flops | bytes accessed | tf_op | source)
XLA Modules:
  0.0 73.1 jit_solution(3758799467922273919)
XLA Ops:
  0.0 1.0 %pack.1 = (bf16[128,8,128]{2,1,0:T(8,128)(2,1)S(1)}, s32[3,16]{1,0:T(4,128)S(1)}, s32[1,16]{1,0:T(1,128)S(1)}, s32[4,128]{1,0:T(4,128)S(1)}) custom-call(bf16[16,32]{1,0:T(8,128)(2,1)} %refs_0_.1, bf16[4,16]{1,0:T(4,128)(2,1)} %bitcast.5, bf16[4,16]{1,0:T(4,128)(2,1)} %bitcast.6, s32[3,16]{1,0:T(4,128)} %refs_3_.1, s32[1,16]{1,0:T(1,128)} %bitcast.7, ...), custom_call_target="tpu_custom_call" | custom-call | tf_op jit(solution)/shard_map/pack/pallas_call | solution.py:30
  1.0 28.6 %all_to_all.20.own_ref.in_ref = bf16[128,8,128]{2,1,0:T(8,128)(2,1)S(1)} all-to-all(bf16[128,8,128]{2,1,0:T(8,128)(2,1)S(1)} %get-tuple-element.15), channel_id=1, replica_groups=mesh['y'=4,'z'=8,'x'=4,'c'=2] {'y','z','x'}, dimensions={0} | all-to-all | bytes 524288 | tf_op jit(solution)/shard_map/all_to_all | solution.py:51
  29.7 3.0 %collective-permute-start = (bf16[128,8,128]{2,1,0:T(8,128)(2,1)S(1)}, bf16[128,8,128]{2,1,0:T(8,128)(2,1)S(1)}, u32[]{:S(2)}, u32[]{:S(2)}) collective-permute-start(bf16[128,8,128]{2,1,0:T(8,128)(2,1)S(1)} %all_to_all.20.own_ref.in_ref), channel_id=1, source_target_pairs={{0,1},{1,0},{2,3},{3,2},{4,5},{5,4},{6,7},{7,6},{8,9},{9,8},{10,11... | collective-permute-start | bytes 786440 | tf_op jit(solution)/shard_map/ppermute | solution.py:55
  32.7 1.8 %ready.1 = (f32[528,128]{1,0:T(8,128)S(1)}, f32[2,16,128]{2,1,0:T(8,128)S(1)}, bf16[512,1024]{1,0:T(8,128)(2,1)S(1)}, bf16[8,128,512]{2,1,0:T(8,128)(2,1)S(1)}) custom-call(s32[3,16]{1,0:T(4,128)S(1)} %get-tuple-element.16.pos_ref, s32[1,16]{1,0:T(1,128)S(1)} %get-tuple-element.17.seg_ref, s32[4,128]{1,0:T(4,128)S(1)} %get-tuple-element.18.held_ref, ...), custom_call_target="tpu_custom_call" | custom-call | tf_op jit(solution)/shard_map/ready/pallas_call | solution.py:30
  34.5 0.0 collective-permute-done.came_ref
  34.5 1.3 %first.1 = (bf16[16,40,128]{2,1,0:T(8,128)(2,1)S(1)}, bf16[1024,128]{1,0:T(8,128)(2,1)S(1)}) custom-call(bf16[128,8,128]{2,1,0:T(8,128)(2,1)S(1)} %all_to_all.20.own_ref.in_ref, bf16[128,8,128]{2,1,0:T(8,128)(2,1)S(1)} %collective-permute-done.came_ref, f32[2,16,128]{2,1,0:T(8,128)S(1)} %get-tuple-element.19.table_ref, ...), custom_call_target="tpu_custom_call" | custom-call | tf_op jit(solution)/shard_map/first/pallas_call | solution.py:30
  35.8 0.1 collective-permute-start.1
  35.9 1.3 %second.1.own_ref = bf16[16,40,128]{2,1,0:T(8,128)(2,1)S(1)} custom-call(bf16[1024,128]{1,0:T(8,128)(2,1)S(1)} %get-tuple-element.23.q_ref, bf16[512,1024]{1,0:T(8,128)(2,1)S(1)} %get-tuple-element.20.k_ref, bf16[8,128,512]{2,1,0:T(8,128)(2,1)S(1)} %get-tuple-element.21.vt_ref, f32[528,128]{1,0:T(8,128)S(1)} %get-tuple-element.22.bias_ref, ...), custom_call_target="tpu_custom_call" | custom-call | tf_op jit(solution)/shard_map/second/pallas_call | solution.py:30
  37.2 0.1 collective-permute-done.1.came_ref
  37.3 0.1 couple.1
  37.4 10.5 %all_to_all.21.in_ref = bf16[16,40,128]{2,1,0:T(8,128)(2,1)S(1)} all-to-all(bf16[16,40,128]{2,1,0:T(8,128)(2,1)S(1)} %couple.1), channel_id=1, replica_groups=mesh['y'=4,'z'=8,'x'=4,'c'=2] {'y','x'}, dimensions={0} | all-to-all | bytes 327680 | tf_op jit(solution)/shard_map/all_to_all | solution.py:51
  47.9 0.1 merge.1
  48.0 9.8 %all_to_all.22.in_ref = bf16[8,40,128]{2,1,0:T(8,128)(2,1)S(1)} all-to-all(bf16[8,40,128]{2,1,0:T(8,128)(2,1)S(1)} %merge.1), channel_id=1, replica_groups=mesh['y'=4,'z'=8,'x'=4,'c'=2] {'z'}, dimensions={0} | all-to-all | bytes 163840 | tf_op jit(solution)/shard_map/all_to_all | solution.py:51
  57.8 2.5 %collective-permute-start.2 = (bf16[32,128]{1,0:T(8,128)(2,1)S(1)}, bf16[32,128]{1,0:T(8,128)(2,1)S(1)}, u32[]{:S(2)}, u32[]{:S(2)}) collective-permute-start(bf16[32,128]{1,0:T(8,128)(2,1)S(1)} %finish.1.own_ref), channel_id=1, source_target_pairs={{0,1},{1,0},{2,3},{3,2},{4,5},{5,4},{6,7},{7,6},{8,9},{9,8},{10,11... | collective-permute-start | bytes 24584 | tf_op jit(solution)/shard_map/ppermute | solution.py:55
  60.3 0.8 %collective-permute-done.2.came_ref = bf16[32,128]{1,0:T(8,128)(2,1)S(1)} collective-permute-done((bf16[32,128]{1,0:T(8,128)(2,1)S(1)}, bf16[32,128]{1,0:T(8,128)(2,1)S(1)}, u32[]{:S(2)}, u32[]{:S(2)}) %collective-permute-start.2) | collective-permute-done | bytes 8224 | tf_op jit(solution)/shard_map/ppermute | solution.py:55
  61.2 10.9 %all_to_all.23.in_ref = bf16[16,64,128]{2,1,0:T(8,128)(2,1)S(1)} all-to-all(bf16[16,64,128]{2,1,0:T(8,128)(2,1)S(1)} %pair.1), channel_id=1, replica_groups=mesh['y'=4,'z'=8,'x'=4,'c'=2] {'y','x'}, dimensions={0} | all-to-all | bytes 524288 | tf_op jit(solution)/shard_map/all_to_all | solution.py:51
  72.1 1.0 %place.1 = bf16[16,8192]{1,0:T(8,128)(2,1)} custom-call(bf16[16,64,128]{2,1,0:T(8,128)(2,1)S(1)} %all_to_all.23.in_ref), custom_call_target="tpu_custom_call" | custom-call | tf_op jit(solution)/shard_map/place/pallas_call | solution.py:30
  (2 shorter events, 0.1 us)
Async XLA Ops:
  29.7 4.8 %collective-permute-start = (bf16[128,8,128]{2,1,0:T(8,128)(2,1)S(1)}, bf16[128,8,128]{2,1,0:T(8,128)(2,1)S(1)}, u32[]{:S(2)}, u32[]{:S(2)}) collective-permute-start(bf16[128,8,128]{2,1,0:T(8,128)(2,1)S(1)} %all_to_all.20.own_ref.in_ref), channel_id=1, source_target_pairs={{0,1},{1,0},{2,3},{3,2},{4,5},{5,4},{6,7},{7,6},{8,9},{9,8},{10,11... | collective-permute-start | bytes 786440 | tf_op jit(solution)/shard_map/ppermute | solution.py:55
  35.8 1.5 %collective-permute-start.1 = (bf16[16,40,128]{2,1,0:T(8,128)(2,1)S(1)}, bf16[16,40,128]{2,1,0:T(8,128)(2,1)S(1)}, u32[]{:S(2)}, u32[]{:S(2)}) collective-permute-start(bf16[16,40,128]{2,1,0:T(8,128)(2,1)S(1)} %get-tuple-element.24), channel_id=1, source_target_pairs={{0,1},{1,0},{2,3},{3,2},{4,5},{5,4},{6,7},{7,6},{8,9},{9,8},{10,11... | collective-permute-start | bytes 491528 | tf_op jit(solution)/shard_map/ppermute | solution.py:55
  57.8 3.3 %collective-permute-start.2 = (bf16[32,128]{1,0:T(8,128)(2,1)S(1)}, bf16[32,128]{1,0:T(8,128)(2,1)S(1)}, u32[]{:S(2)}, u32[]{:S(2)}) collective-permute-start(bf16[32,128]{1,0:T(8,128)(2,1)S(1)} %finish.1.own_ref), channel_id=1, source_target_pairs={{0,1},{1,0},{2,3},{3,2},{4,5},{5,4},{6,7},{7,6},{8,9},{9,8},{10,11... | collective-permute-start | bytes 24584 | tf_op jit(solution)/shard_map/ppermute | solution.py:55

commit v10 on v9

--- a/solution.py
+++ b/solution.py
@@ -150,13 +150,9 @@
     return tile.astype(BF16)
 
 
-def ready_body(pos_ref, seg_ref, held_ref, k_hbm, v_hbm, bias_ref, table_ref, k_ref, vt_ref, v_ref, sems):
-    copies = [
-        pltpu.make_async_copy(source, target, sems.at[n])
-        for n, (source, target) in enumerate(((v_hbm, v_ref), (k_hbm, k_ref)))
-    ]
-    for copy in copies:
-        copy.start()
+def ready_body(pos_ref, seg_ref, held_ref, v_hbm, bias_ref, table_ref, vt_ref, v_ref, sem):
+    copy = pltpu.make_async_copy(v_hbm, v_ref, sem)
+    copy.start()
     lane = lanes((ROWS, 128))
     cosine, sine = rope_tables(pos_ref[...], lane % 64)
     table_ref[0] = cosine
@@ -169,10 +165,9 @@
         bias_ref[part * 128 : (part + 1) * 128, :] = (dot(have, wanted, TN) - 1.0) * -HIDDEN
     seen = dot(kinds, wanted, TN) * jnp.where(rows_of((ROWS, 128)) <= lane % ROWS, 1.0, 0.0)
     bias_ref[512:, :] = (seen - 1.0) * -HIDDEN
-    copies[0].wait()
+    copy.wait()
     for g in range(KVH):
         vt_ref[g] = v_ref[:, g * HD : (g + 1) * HD].T
-    copies[1].wait()
 
 
 def placing(core):
@@ -218,16 +213,15 @@
 
 
 def attend(base, q_ref, k_ref, vt_ref, bias_ref, out_ref):
-    for pair in ((0, 1), (2, 3)):
-        scores = [
-            dot(k_ref[:, heads_at(base, i)], q_ref[heads_at(base, i), :], NT) * FACTOR
-            + bias_ref[0:512, :]
-            for i in pair
-        ]
-        parts = [softened(s) for s in scores]
-        outs = [dot(vt_ref[base + i], w[0], NN) for i, w in zip(pair, parts)]
-        for i, out, (_, peak, total) in zip(pair, outs, parts):
-            emit(out_ref, i * 4, out.astype(BF16), state_rows(peak, total))
+    scores = [
+        dot(k_ref[:, heads_at(base, i)], q_ref[heads_at(base, i), :], NT) * FACTOR
+        + bias_ref[0:512, :]
+        for i in range(4)
+    ]
+    parts = [softened(s) for s in scores]
+    outs = [dot(vt_ref[base + i], parts[i][0], NN) for i in range(4)]
+    for i, (_, peak, total) in enumerate(parts):
+        emit(out_ref, i * 4, outs[i].astype(BF16), state_rows(peak, total))
 
 
 def emit(out_ref, first, out, state):
@@ -383,21 +377,20 @@
     )
     tiles = exchange(tiles, CHIPS)
     came = swap(tiles)
-    bias, tables, keys, turned_values = call(
+    bias, tables, turned_values = call(
         ready_body,
         "ready",
         (
             shape((512 + ROWS, 128), F32),
             shape((2, ROWS, 128), F32),
-            shape((512, KVH * HD), BF16),
             shape((KVH, HD, 512), BF16),
         ),
         positions,
         span_segments,
         cache_segments,
-        *(pltpu.with_memory_space_constraint(a, pltpu.HBM) for a in (cache_keys, cache_values)),
-        specs=[VMEM] * 3 + [HBM] * 2,
-        scratch=[pltpu.VMEM((512, KVH * HD), BF16), pltpu.SemaphoreType.DMA((2,))],
+        pltpu.with_memory_space_constraint(cache_values, pltpu.HBM),
+        specs=[VMEM] * 3 + [HBM],
+        scratch=[pltpu.VMEM((512, KVH * HD), BF16), pltpu.SemaphoreType.DMA],
     )
     message = shape((16, 40, 128), BF16)
     parts, q = call(
@@ -407,13 +400,13 @@
         tiles,
         came,
         tables,
-        keys,
+        cache_keys,
         turned_values,
         bias,
     )
     other = swap(parts)
     parts = call(
-        second_body, "second", message, q, keys, turned_values, bias, tiles, came, tables
+        second_body, "second", message, q, cache_keys, turned_values, bias, tiles, came, tables
     )
     parts = call(couple_body, "couple", message, parts, other)
     parts = exchange(parts, PLANE)

time: 73.4 us -> 73.3 us (level)
  no operation moved by 1% of the time
where the time goes in v10:
time: 73.3 us; the launch traced here: 73.1 us
  blocking collectives  59.9 us (82%)
  Pallas kernels  6.44 us (9%)
  starting transfers between devices  5.63 us (8%)
  waiting for transfers between devices  1.05 us (1%)
    all_to_all x4, blocking collectives, exchange(): return lax.all_to_all(tiles, axes, 0, 0, tiled=True)  59.9 us
    pallas_call x9, Pallas kernels, call(): pl.pallas_call(body, name=name, out_shape=out_shape, in_specs=specs or [V...  6.44 us
    ppermute x3, starting transfers between devices, swap(): return lax.ppermute(value, 'c', ((0, 1), (1, 0)))  5.63 us
  transfers between devices with their start and end apart: 3, of which 2 were waited for; matrix products, arithmetic and copies ran while one was open for 0% of the time, Pallas kernels for 4%

profile of v10, /device:TPU:1, one launch (start us, length us, event | category | flops | bytes accessed | tf_op | source)
XLA Modules:
  0.0 73.1 jit_solution(9055906342703035710)
XLA Ops:
  0.0 0.0 copy-start
  0.0 1.1 %pack.1 = (bf16[128,8,128]{2,1,0:T(8,128)(2,1)S(1)}, s32[3,16]{1,0:T(4,128)S(1)}, s32[1,16]{1,0:T(1,128)S(1)}, s32[4,128]{1,0:T(4,128)S(1)}) custom-call(bf16[16,32]{1,0:T(8,128)(2,1)} %refs_0_.1, bf16[4,16]{1,0:T(4,128)(2,1)} %bitcast.5, bf16[4,16]{1,0:T(4,128)(2,1)} %bitcast.6, s32[3,16]{1,0:T(4,128)} %refs_3_.1, s32[1,16]{1,0:T(1,128)} %bitcast.7, ...), custom_call_target="tpu_custom_call" | custom-call | tf_op jit(solution)/shard_map/pack/pallas_call | solution.py:30
  1.1 28.6 %all_to_all.20.own_ref.in_ref = bf16[128,8,128]{2,1,0:T(8,128)(2,1)S(1)} all-to-all(bf16[128,8,128]{2,1,0:T(8,128)(2,1)S(1)} %get-tuple-element.14), channel_id=1, replica_groups=mesh['y'=4,'z'=8,'x'=4,'c'=2] {'y','z','x'}, dimensions={0} | all-to-all | bytes 524288 | tf_op jit(solution)/shard_map/all_to_all | solution.py:51
  29.7 3.0 %collective-permute-start = (bf16[128,8,128]{2,1,0:T(8,128)(2,1)S(1)}, bf16[128,8,128]{2,1,0:T(8,128)(2,1)S(1)}, u32[]{:S(2)}, u32[]{:S(2)}) collective-permute-start(bf16[128,8,128]{2,1,0:T(8,128)(2,1)S(1)} %all_to_all.20.own_ref.in_ref), channel_id=1, source_target_pairs={{0,1},{1,0},{2,3},{3,2},{4,5},{5,4},{6,7},{7,6},{8,9},{9,8},{10,11... | collective-permute-start | bytes 786440 | tf_op jit(solution)/shard_map/ppermute | solution.py:55
  32.8 1.8 %ready.1 = (f32[528,128]{1,0:T(8,128)S(1)}, f32[2,16,128]{2,1,0:T(8,128)S(1)}, bf16[8,128,512]{2,1,0:T(8,128)(2,1)S(1)}) custom-call(s32[3,16]{1,0:T(4,128)S(1)} %get-tuple-element.15.pos_ref, s32[1,16]{1,0:T(1,128)S(1)} %get-tuple-element.16.seg_ref, s32[4,128]{1,0:T(4,128)S(1)} %get-tuple-element.17.held_ref, bf16[512,1024]{1,0:T(8,128)(2,1)} %v_hbm.1), custom_call_target="tpu_custom_call" | custom-call | tf_op jit(solution)/shard_map/ready/pallas_call | solution.py:30
  34.6 0.0 collective-permute-done.came_ref
  34.6 0.0 copy-done
  34.6 1.2 %first.1 = (bf16[16,40,128]{2,1,0:T(8,128)(2,1)S(1)}, bf16[1024,128]{1,0:T(8,128)(2,1)S(1)}) custom-call(bf16[128,8,128]{2,1,0:T(8,128)(2,1)S(1)} %all_to_all.20.own_ref.in_ref, bf16[128,8,128]{2,1,0:T(8,128)(2,1)S(1)} %collective-permute-done.came_ref, f32[2,16,128]{2,1,0:T(8,128)S(1)} %get-tuple-element.18.table_ref, bf16[512,1024]{1,0:T(8,128)(2,1)S(1)} %copy-done, ...), custom_call_target="tpu_custom_call" | custom-call | tf_op jit(solution)/shard_map/first/pallas_call | solution.py:30
  35.7 0.1 collective-permute-start.1
  35.8 1.2 %second.1.own_ref = bf16[16,40,128]{2,1,0:T(8,128)(2,1)S(1)} custom-call(bf16[1024,128]{1,0:T(8,128)(2,1)S(1)} %get-tuple-element.21.q_ref, bf16[512,1024]{1,0:T(8,128)(2,1)S(1)} %copy-done, bf16[8,128,512]{2,1,0:T(8,128)(2,1)S(1)} %get-tuple-element.19.vt_ref, f32[528,128]{1,0:T(8,128)S(1)} %get-tuple-element.20.bias_ref, ...), custom_call_target="tpu_custom_call" | custom-call | tf_op jit(solution)/shard_map/second/pallas_call | solution.py:30
  37.0 0.2 collective-permute-done.1.came_ref
  37.2 0.1 couple.1
  37.4 10.5 %all_to_all.21.in_ref = bf16[16,40,128]{2,1,0:T(8,128)(2,1)S(1)} all-to-all(bf16[16,40,128]{2,1,0:T(8,128)(2,1)S(1)} %couple.1), channel_id=1, replica_groups=mesh['y'=4,'z'=8,'x'=4,'c'=2] {'y','x'}, dimensions={0} | all-to-all | bytes 327680 | tf_op jit(solution)/shard_map/all_to_all | solution.py:51
  47.9 0.1 merge.1
  48.0 9.8 %all_to_all.22.in_ref = bf16[8,40,128]{2,1,0:T(8,128)(2,1)S(1)} all-to-all(bf16[8,40,128]{2,1,0:T(8,128)(2,1)S(1)} %merge.1), channel_id=1, replica_groups=mesh['y'=4,'z'=8,'x'=4,'c'=2] {'z'}, dimensions={0} | all-to-all | bytes 163840 | tf_op jit(solution)/shard_map/all_to_all | solution.py:51
  57.8 2.5 %collective-permute-start.2 = (bf16[32,128]{1,0:T(8,128)(2,1)S(1)}, bf16[32,128]{1,0:T(8,128)(2,1)S(1)}, u32[]{:S(2)}, u32[]{:S(2)}) collective-permute-start(bf16[32,128]{1,0:T(8,128)(2,1)S(1)} %finish.1.own_ref), channel_id=1, source_target_pairs={{0,1},{1,0},{2,3},{3,2},{4,5},{5,4},{6,7},{7,6},{8,9},{9,8},{10,11... | collective-permute-start | bytes 24584 | tf_op jit(solution)/shard_map/ppermute | solution.py:55
  60.3 0.8 %collective-permute-done.2.came_ref = bf16[32,128]{1,0:T(8,128)(2,1)S(1)} collective-permute-done((bf16[32,128]{1,0:T(8,128)(2,1)S(1)}, bf16[32,128]{1,0:T(8,128)(2,1)S(1)}, u32[]{:S(2)}, u32[]{:S(2)}) %collective-permute-start.2) | collective-permute-done | bytes 8224 | tf_op jit(solution)/shard_map/ppermute | solution.py:55
  61.2 10.9 %all_to_all.23.in_ref = bf16[16,64,128]{2,1,0:T(8,128)(2,1)S(1)} all-to-all(bf16[16,64,128]{2,1,0:T(8,128)(2,1)S(1)} %pair.1), channel_id=1, replica_groups=mesh['y'=4,'z'=8,'x'=4,'c'=2] {'y','x'}, dimensions={0} | all-to-all | bytes 524288 | tf_op jit(solution)/shard_map/all_to_all | solution.py:51
  72.1 1.0 %place.1 = bf16[16,8192]{1,0:T(8,128)(2,1)} custom-call(bf16[16,64,128]{2,1,0:T(8,128)(2,1)S(1)} %all_to_all.23.in_ref), custom_call_target="tpu_custom_call" | custom-call | tf_op jit(solution)/shard_map/place/pallas_call | solution.py:30
  (2 shorter events, 0.1 us)
Async XLA Ops:
  0.0 34.6 %copy-start = (bf16[512,1024]{1,0:T(8,128)(2,1)S(1)}, bf16[512,1024]{1,0:T(8,128)(2,1)}, u32[]{:S(2)}) copy-start(bf16[512,1024]{1,0:T(8,128)(2,1)} %k_ref.3) | copy-start | bytes 3145732
  29.7 4.8 %collective-permute-start = (bf16[128,8,128]{2,1,0:T(8,128)(2,1)S(1)}, bf16[128,8,128]{2,1,0:T(8,128)(2,1)S(1)}, u32[]{:S(2)}, u32[]{:S(2)}) collective-permute-start(bf16[128,8,128]{2,1,0:T(8,128)(2,1)S(1)} %all_to_all.20.own_ref.in_ref), channel_id=1, source_target_pairs={{0,1},{1,0},{2,3},{3,2},{4,5},{5,4},{6,7},{7,6},{8,9},{9,8},{10,11... | collective-permute-start | bytes 786440 | tf_op jit(solution)/shard_map/ppermute | solution.py:55
  35.7 1.5 %collective-permute-start.1 = (bf16[16,40,128]{2,1,0:T(8,128)(2,1)S(1)}, bf16[16,40,128]{2,1,0:T(8,128)(2,1)S(1)}, u32[]{:S(2)}, u32[]{:S(2)}) collective-permute-start(bf16[16,40,128]{2,1,0:T(8,128)(2,1)S(1)} %get-tuple-element.22), channel_id=1, source_target_pairs={{0,1},{1,0},{2,3},{3,2},{4,5},{5,4},{6,7},{7,6},{8,9},{9,8},{10,11... | collective-permute-start | bytes 491528 | tf_op jit(solution)/shard_map/ppermute | solution.py:55
  57.8 3.3 %collective-permute-start.2 = (bf16[32,128]{1,0:T(8,128)(2,1)S(1)}, bf16[32,128]{1,0:T(8,128)(2,1)S(1)}, u32[]{:S(2)}, u32[]{:S(2)}) collective-permute-start(bf16[32,128]{1,0:T(8,128)(2,1)S(1)} %finish.1.own_ref), channel_id=1, source_target_pairs={{0,1},{1,0},{2,3},{3,2},{4,5},{5,4},{6,7},{7,6},{8,9},{9,8},{10,11... | collective-permute-start | bytes 24584 | tf_op jit(solution)/shard_map/ppermute | solution.py:55

commit v11 on v10

--- a/solution.py
+++ b/solution.py
@@ -81,20 +81,16 @@
         copy.start()
     for copy in copies:
         copy.wait()
-    turn = (lax.axis_index("x") % 2) * 64
-
-    def spread(count, at):
-        return where_one(lanes((count, 128)) == rows_of((count, 128)) + (at + turn) % 128)
-
-    tile = jnp.zeros((8, 128), F32)
-    for late in range(2):
-        part = dot(q_ref[...], spread(32, late * 32), NN)
-        for ref, at in ((k_ref, 64), (v_ref, 96)):
-            part = part + dot(ref[...], spread(4, at + late * 16), TN)
-        tile = tile + part[late * 8 : (late + 1) * 8]
-    tile = tile.astype(BF16)
-    for d in range(out_ref.shape[0]):
-        out_ref[d] = tile
+    q = dot(q_ref[...], where_one(lanes((32, 128)) % 32 == rows_of((32, 128))), NN)
+    q = jnp.where(lanes((ROWS, 128)) // 32 == rows_of((ROWS, 128)) // 4, q, 0.0).astype(BF16)
+    token = lanes((ROWS, 128)) // 4 - rows_of((ROWS, 128))
+    kv = dot(k_ref[...], where_one(token == 0), NN) + dot(v_ref[...], where_one(token == 16), NN)
+    kv = jnp.where(lanes((4, 128)) % 4 == rows_of((4, 128)), kv, 0.0).astype(BF16)
+    tiles = dot(where_one(rows_of((48, ROWS)) % 6 == lanes((48, ROWS)) % 4), q, NN)
+    tiles = tiles + dot(where_one(rows_of((48, 4)) % 6 == 4), kv, NN)
+    tiles = tiles.astype(BF16)
+    for n in range(out_ref.shape[0] // 48):
+        out_ref[n * 48 : (n + 1) * 48, :] = tiles
 
 
 def turn(angle):
@@ -157,44 +153,40 @@
     cosine, sine = rope_tables(pos_ref[...], lane % 64)
     table_ref[0] = cosine
     table_ref[1] = jnp.where(lane < 64, -sine, sine)
-    pick = where_one(rows_of((ROWS, 128)) == lane % ROWS)
+    pick = where_one(rows_of((ROWS, 128)) == lane // 8)
     kinds = where_one(rows_of((8, ROWS)) == seg_ref[...])
     wanted = dot(kinds, pick, NN).astype(BF16)
     for part in range(4):
         have = where_one(rows_of((8, 128)) == held_ref[part : part + 1, :])
         bias_ref[part * 128 : (part + 1) * 128, :] = (dot(have, wanted, TN) - 1.0) * -HIDDEN
-    seen = dot(kinds, wanted, TN) * jnp.where(rows_of((ROWS, 128)) <= lane % ROWS, 1.0, 0.0)
+    seen = dot(kinds, wanted, TN) * jnp.where(rows_of((ROWS, 128)) <= lane // 8, 1.0, 0.0)
     bias_ref[512:, :] = (seen - 1.0) * -HIDDEN
     copy.wait()
     for g in range(KVH):
         vt_ref[g] = v_ref[:, g * HD : (g + 1) * HD].T
 
 
-def placing(core):
-    row, lane = rows_of((128, 256)), lanes((128, 256))
-    at = (row // 64) * 64 + core * 32 + row % 32 + ((row // 32) % 2) * 128
-    return where_one(lane == at)
-
-
-def join(own_ref, came_ref, table_ref, q_ref):
+def join(own_ref, came_ref, table_ref, q_ref, kv_ref, flat_ref):
     c = lax.axis_index("c")
-    near = lanes((1, 8, 128)) < 64
-
-    def halves(ref):
-        tiles = ref[...].astype(F32).reshape(64, 2, 8, 128)
-        return jnp.where(near, tiles[:, 0], tiles[:, 1]).reshape(512, 128).astype(BF16)
-
-    whole = dot(halves(own_ref), placing(c), NN) + dot(halves(came_ref), placing(1 - c), NN)
-    for late in range(2):
-        part = whole[:, late * 128 : (late + 1) * 128]
-        at = slice(late * 8, (late + 1) * 8)
-        cosine, sine = table_ref[0, at, :], table_ref[1, at, :]
-        turned = move(part, 64).reshape(64, 8, 128)
-        part = (part.reshape(64, 8, 128) * cosine[None] + turned * sine[None]).astype(BF16)
-        for n in range(64):
-            z, p = (n // 2) % 8, n % 2
-            head = (n // 16) * 16 + z * 2 + p
-            q_ref[head * 16 + late * 8 : head * 16 + late * 8 + 8, :] = part[n]
+    shape = (128, 4 * 128)
+    source, target = rows_of(shape), lanes(shape)
+    whole = jnp.zeros((256, 512), F32)
+    for n, ref in enumerate((own_ref, came_ref)):
+        flat_ref[n, 0:768, :] = ref[...].astype(F32)
+        kv_ref[n] = flat_ref[n, pl.ds(4, 128, stride=6), :]
+        for half in range(2):
+            part = jnp.concatenate(
+                [flat_ref[n, pl.ds(j + 6 * half, 64, stride=12), :] for j in range(4)], axis=0
+            )
+            core = 1 - c if n else c
+            at = (source // 32) * 128 + half * 64 + core * 32 + source % 32
+            whole = whole + dot(part.astype(BF16), where_one(target == at), NN)
+    for r in range(ROWS):
+        high, low = divmod(r, 4)
+        part = whole[low * 64 : (low + 1) * 64, high * 128 : (high + 1) * 128]
+        part = rotate(part, table_ref[0, r : r + 1, :], table_ref[1, r : r + 1, :]).astype(BF16)
+        for g in range(KVH):
+            q_ref[g * 128 + r * 8 : g * 128 + r * 8 + 8, :] = part[g * 8 : (g + 1) * 8]
 
 
 FACTOR = LOG2E / HD**0.5
@@ -230,41 +222,38 @@
         out_ref[first + n, 32:40, :] = state
 
 
-def first_body(own_ref, came_ref, table_ref, k_ref, vt_ref, bias_ref, out_ref, q_ref):
-    join(own_ref, came_ref, table_ref, q_ref)
+def first_body(
+    own_ref, came_ref, table_ref, k_ref, vt_ref, bias_ref, out_ref, q_ref, kv_ref, flat_ref
+):
+    join(own_ref, came_ref, table_ref, q_ref, kv_ref, flat_ref)
     attend((1 - lax.axis_index("c")) * 4, q_ref, k_ref, vt_ref, bias_ref, out_ref)
 
 
-def second_body(q_ref, k_ref, vt_ref, bias_ref, in_ref, came_ref, table_ref, out_ref):
+def second_body(q_ref, k_ref, vt_ref, bias_ref, kv_ref, table_ref, out_ref):
     c, y = lax.axis_index("c"), lax.axis_index("y")
     attend(c * 4, q_ref, k_ref, vt_ref, bias_ref, out_ref)
 
     @pl.when((lax.axis_index("z") == 0) & (lax.axis_index("x") == 0))
     def _():
-        lane = lanes((8, 128))
         g = c * 4 + y
-        start = (g // 2) * 32 + (g % 2) * 16
+        chips = pl.ds(pl.multiple_of(g * 16, 16), 16)
+        own, came = kv_ref[0, chips, :], kv_ref[1, chips, :]
+        held = [jnp.where(c == core, own, came).astype(BF16) for core in range(2)]
+        row, lane = rows_of((64, 128)), lanes((64, 128))
         found = []
         for kind in range(2):
-            parts = []
-            for late in range(2):
-                value = jnp.zeros((8, 128), F32)
-                for n in range(16):
-                    own, came = in_ref[start + n].astype(F32), came_ref[start + n].astype(F32)
-                    pair = (jnp.where(c == 0, own, came), jnp.where(c == 0, came, own))
-                    for core in range(2):
-                        at = n * 8 + core * 4
-                        held = (1 - n % 2) * 64 + kind * 32 + late * 16
-                        value = jnp.where(
-                            (lane >= at) & (lane < at + 4), move(pair[core], at - held), value
-                        )
-                parts.append(value)
+            pick = where_one(lane == kind * 64 + (row % 16) * 4 + row // 16)
+            value = jnp.zeros((ROWS, 128), F32)
+            for core in range(2):
+                columns = dot(pick, held[core], NT).astype(BF16)
+                for i in range(4):
+                    at = rows_of((ROWS, 128)) * 8 + core * 4 + i
+                    value = value + dot(
+                        columns[i * 16 : (i + 1) * 16], where_one(lanes((ROWS, 128)) == at), NN
+                    )
             if kind == 0:
-                parts = [
-                    rotate(v, table_ref[0, n * 8 : n * 8 + 8, :], table_ref[1, n * 8 : n * 8 + 8, :])
-                    for n, v in enumerate(parts)
-                ]
-            found.append(jnp.concatenate(parts, axis=0).astype(BF16))
+                value = rotate(value, table_ref[0], table_ref[1])
+            found.append(value.astype(BF16))
         scores = dot(found[0], q_ref[heads_at(c * 4, y), :], NT) * FACTOR + bias_ref[512:, :]
         weights, peak, total = softened(scores)
         own = dot(found[1], weights, TN)
@@ -330,7 +319,8 @@
 
 def place_body(in_ref, out_hbm, out_ref, sems):
     copies = []
-    eye = where_one(rows_of((128, 128)) == lanes((128, 128)))
+    row = rows_of((128, 128))
+    eye = where_one((row % 16) * 8 + row // 16 == lanes((128, 128)))
     for g in range(KVH):
         half, y = divmod(g, 4)
         block = in_ref[y * 4 : (y + 1) * 4, half * 32 : (half + 1) * 32, :].reshape(128, 128)
@@ -370,12 +360,12 @@
     tiles, positions, span_segments, cache_segments = call(
         pack_body,
         "pack",
-        (shape((128, 8, 128), BF16), *(shape(a.shape, a.dtype) for a in small[3:])),
+        (shape((6 * 128, 128), BF16), *(shape(a.shape, a.dtype) for a in small[3:])),
         *(pltpu.with_memory_space_constraint(a, pltpu.HBM) for a in small),
         specs=[HBM] * 6,
         scratch=[pltpu.VMEM(a.shape, a.dtype) for a in small[:3]] + [pltpu.SemaphoreType.DMA((6,))],
     )
-    tiles = exchange(tiles, CHIPS)
+    tiles = exchange(tiles.reshape(-1, 2, 128), CHIPS).reshape(-1, 128)
     came = swap(tiles)
     bias, tables, turned_values = call(
         ready_body,
@@ -393,20 +383,21 @@
         scratch=[pltpu.VMEM((512, KVH * HD), BF16), pltpu.SemaphoreType.DMA],
     )
     message = shape((16, 40, 128), BF16)
-    parts, q = call(
+    parts, q, kv = call(
         first_body,
         "first",
-        (message, shape((H * ROWS, HD), BF16)),
+        (message, shape((H * ROWS, HD), BF16), shape((2, 128, 128), F32)),
         tiles,
         came,
         tables,
         cache_keys,
         turned_values,
         bias,
+        scratch=[pltpu.VMEM((2, 6 * 128 + 16, 128), F32)],
     )
     other = swap(parts)
     parts = call(
-        second_body, "second", message, q, cache_keys, turned_values, bias, tiles, came, tables
+        second_body, "second", message, q, cache_keys, turned_values, bias, kv, tables
     )
     parts = call(couple_body, "couple", message, parts, other)
     parts = exchange(parts, PLANE)

time: 73.3 us -> 72.1 us (0.984)
  blocking collectives: 59.9 us -> 58.5 us
    all_to_all x4, blocking collectives: 59.9 us -> 58.5 us  [exchange(): return lax.all_to_all(tiles, axes, 0, 0, tiled=True)]
  transfers between devices with their start and end apart: 3 -> 3, of which waited for: 2 -> 1; matrix products, arithmetic and copies ran while one was open for 0% -> 0% of each run, Pallas kernels for 4% -> 4%
where the time goes in v11:
time: 72.1 us; the launch traced here: 71.9 us
  blocking collectives  58.5 us (81%)
  Pallas kernels  6.84 us (9%)
  starting transfers between devices  5.58 us (8%)
  waiting for transfers between devices  0.83 us (1%)
    all_to_all x4, blocking collectives, exchange(): return lax.all_to_all(tiles, axes, 0, 0, tiled=True)  58.5 us
    pallas_call x9, Pallas kernels, call(): pl.pallas_call(body, name=name, out_shape=out_shape, in_specs=specs or [V...  6.84 us
    ppermute x3, starting transfers between devices, swap(): return lax.ppermute(value, 'c', ((0, 1), (1, 0)))  5.58 us
  transfers between devices with their start and end apart: 3, of which 1 were waited for; matrix products, arithmetic and copies ran while one was open for 0% of the time, Pallas kernels for 4%

profile of v11, /device:TPU:1, one launch (start us, length us, event | category | flops | bytes accessed | tf_op | source)
XLA Modules:
  0.0 71.9 jit_solution(11048540753059086039)
XLA Ops:
  0.0 0.0 copy-start
  0.0 1.2 %pack.1 = (bf16[768,128]{1,0:T(8,128)(2,1)S(1)}, s32[3,16]{1,0:T(4,128)S(1)}, s32[1,16]{1,0:T(1,128)S(1)}, s32[4,128]{1,0:T(4,128)S(1)}) custom-call(bf16[16,32]{1,0:T(8,128)(2,1)} %refs_0_.1, bf16[4,16]{1,0:T(4,128)(2,1)} %bitcast.10, bf16[4,16]{1,0:T(4,128)(2,1)} %bitcast.11, s32[3,16]{1,0:T(4,128)} %refs_3_.1, s32[1,16]{1,0:T(1,128)} %bitcast.12, ...), custom_call_target="tpu_custom_call" | custom-call | tf_op jit(solution)/shard_map/pack/pallas_call | solution.py:30
  1.2 27.4 %all_to_all.20 = bf16[384,2,128]{2,1,0:T(2,128)(2,1)S(1)} all-to-all(bf16[384,2,128]{2,1,0:T(2,128)(2,1)S(1)} %bitcast.8), channel_id=1, replica_groups=mesh['y'=4,'z'=8,'x'=4,'c'=2] {'y','z','x'}, dimensions={0} | all-to-all | bytes 393216 | tf_op jit(solution)/shard_map/all_to_all | solution.py:51
  28.6 3.0 %collective-permute-start = (bf16[768,128]{1,0:T(8,128)(2,1)S(1)}, bf16[768,128]{1,0:T(8,128)(2,1)S(1)}, u32[]{:S(2)}, u32[]{:S(2)}) collective-permute-start(bf16[768,128]{1,0:T(8,128)(2,1)S(1)} %bitcast.6), channel_id=1, source_target_pairs={{0,1},{1,0},{2,3},{3,2},{4,5},{5,4},{6,7},{7,6},{8,9},{9,8},{10,11... | collective-permute-start | bytes 589832 | tf_op jit(solution)/shard_map/ppermute | solution.py:55
  31.6 1.8 %ready.1 = (f32[528,128]{1,0:T(8,128)S(1)}, f32[2,16,128]{2,1,0:T(8,128)S(1)}, bf16[8,128,512]{2,1,0:T(8,128)(2,1)S(1)}) custom-call(s32[3,16]{1,0:T(4,128)S(1)} %get-tuple-element.16.pos_ref, s32[1,16]{1,0:T(1,128)S(1)} %get-tuple-element.17.seg_ref, s32[4,128]{1,0:T(4,128)S(1)} %get-tuple-element.18.held_ref, bf16[512,1024]{1,0:T(8,128)(2,1)} %v_hbm.1), custom_call_target="tpu_custom_call" | custom-call | tf_op jit(solution)/shard_map/ready/pallas_call | solution.py:30
  33.4 0.0 collective-permute-done.came_ref
  33.4 0.0 copy-done
  33.4 1.2 %first.1 = (bf16[16,40,128]{2,1,0:T(8,128)(2,1)S(1)}, bf16[1024,128]{1,0:T(8,128)(2,1)S(1)}, f32[2,128,128]{2,1,0:T(8,128)S(1)}) custom-call(bf16[768,128]{1,0:T(8,128)(2,1)S(1)} %bitcast.7, bf16[768,128]{1,0:T(8,128)(2,1)S(1)} %collective-permute-done.came_ref, f32[2,16,128]{2,1,0:T(8,128)S(1)} %get-tuple-element.19.table_ref, ...), custom_call_target="tpu_custom_call" | custom-call | tf_op jit(solution)/shard_map/first/pallas_call | solution.py:30
  34.6 0.1 collective-permute-start.1
  34.7 1.4 %second.1.own_ref = bf16[16,40,128]{2,1,0:T(8,128)(2,1)S(1)} custom-call(bf16[1024,128]{1,0:T(8,128)(2,1)S(1)} %get-tuple-element.22.q_ref, bf16[512,1024]{1,0:T(8,128)(2,1)S(1)} %copy-done, bf16[8,128,512]{2,1,0:T(8,128)(2,1)S(1)} %get-tuple-element.20.vt_ref, f32[528,128]{1,0:T(8,128)S(1)} %get-tuple-element.21.bias_ref, ...), custom_call_target="tpu_custom_call" | custom-call | tf_op jit(solution)/shard_map/second/pallas_call | solution.py:30
  36.2 0.0 collective-permute-done.1.came_ref
  36.2 0.1 couple.1
  36.3 10.4 %all_to_all.21.in_ref = bf16[16,40,128]{2,1,0:T(8,128)(2,1)S(1)} all-to-all(bf16[16,40,128]{2,1,0:T(8,128)(2,1)S(1)} %couple.1), channel_id=1, replica_groups=mesh['y'=4,'z'=8,'x'=4,'c'=2] {'y','x'}, dimensions={0} | all-to-all | bytes 327680 | tf_op jit(solution)/shard_map/all_to_all | solution.py:51
  46.7 0.1 merge.1
  46.8 9.8 %all_to_all.22.in_ref = bf16[8,40,128]{2,1,0:T(8,128)(2,1)S(1)} all-to-all(bf16[8,40,128]{2,1,0:T(8,128)(2,1)S(1)} %merge.1), channel_id=1, replica_groups=mesh['y'=4,'z'=8,'x'=4,'c'=2] {'z'}, dimensions={0} | all-to-all | bytes 163840 | tf_op jit(solution)/shard_map/all_to_all | solution.py:51
  56.6 2.5 %collective-permute-start.2 = (bf16[32,128]{1,0:T(8,128)(2,1)S(1)}, bf16[32,128]{1,0:T(8,128)(2,1)S(1)}, u32[]{:S(2)}, u32[]{:S(2)}) collective-permute-start(bf16[32,128]{1,0:T(8,128)(2,1)S(1)} %finish.1.own_ref), channel_id=1, source_target_pairs={{0,1},{1,0},{2,3},{3,2},{4,5},{5,4},{6,7},{7,6},{8,9},{9,8},{10,11... | collective-permute-start | bytes 24584 | tf_op jit(solution)/shard_map/ppermute | solution.py:55
  59.1 0.8 %collective-permute-done.2.came_ref = bf16[32,128]{1,0:T(8,128)(2,1)S(1)} collective-permute-done((bf16[32,128]{1,0:T(8,128)(2,1)S(1)}, bf16[32,128]{1,0:T(8,128)(2,1)S(1)}, u32[]{:S(2)}, u32[]{:S(2)}) %collective-permute-start.2) | collective-permute-done | bytes 8224 | tf_op jit(solution)/shard_map/ppermute | solution.py:55
  60.0 10.9 %all_to_all.23.in_ref = bf16[16,64,128]{2,1,0:T(8,128)(2,1)S(1)} all-to-all(bf16[16,64,128]{2,1,0:T(8,128)(2,1)S(1)} %pair.1), channel_id=1, replica_groups=mesh['y'=4,'z'=8,'x'=4,'c'=2] {'y','x'}, dimensions={0} | all-to-all | bytes 524288 | tf_op jit(solution)/shard_map/all_to_all | solution.py:51
  70.9 1.0 %place.1 = bf16[16,8192]{1,0:T(8,128)(2,1)} custom-call(bf16[16,64,128]{2,1,0:T(8,128)(2,1)S(1)} %all_to_all.23.in_ref), custom_call_target="tpu_custom_call" | custom-call | tf_op jit(solution)/shard_map/place/pallas_call | solution.py:30
  (2 shorter events, 0.1 us)
Async XLA Ops:
  0.0 33.4 %copy-start = (bf16[512,1024]{1,0:T(8,128)(2,1)S(1)}, bf16[512,1024]{1,0:T(8,128)(2,1)}, u32[]{:S(2)}) copy-start(bf16[512,1024]{1,0:T(8,128)(2,1)} %k_ref.3) | copy-start | bytes 3145732
  28.6 4.8 %collective-permute-start = (bf16[768,128]{1,0:T(8,128)(2,1)S(1)}, bf16[768,128]{1,0:T(8,128)(2,1)S(1)}, u32[]{:S(2)}, u32[]{:S(2)}) collective-permute-start(bf16[768,128]{1,0:T(8,128)(2,1)S(1)} %bitcast.6), channel_id=1, source_target_pairs={{0,1},{1,0},{2,3},{3,2},{4,5},{5,4},{6,7},{7,6},{8,9},{9,8},{10,11... | collective-permute-start | bytes 589832 | tf_op jit(solution)/shard_map/ppermute | solution.py:55
  34.6 1.5 %collective-permute-start.1 = (bf16[16,40,128]{2,1,0:T(8,128)(2,1)S(1)}, bf16[16,40,128]{2,1,0:T(8,128)(2,1)S(1)}, u32[]{:S(2)}, u32[]{:S(2)}) collective-permute-start(bf16[16,40,128]{2,1,0:T(8,128)(2,1)S(1)} %get-tuple-element.24), channel_id=1, source_target_pairs={{0,1},{1,0},{2,3},{3,2},{4,5},{5,4},{6,7},{7,6},{8,9},{9,8},{10,11... | collective-permute-start | bytes 491528 | tf_op jit(solution)/shard_map/ppermute | solution.py:55
  56.6 3.3 %collective-permute-start.2 = (bf16[32,128]{1,0:T(8,128)(2,1)S(1)}, bf16[32,128]{1,0:T(8,128)(2,1)S(1)}, u32[]{:S(2)}, u32[]{:S(2)}) collective-permute-start(bf16[32,128]{1,0:T(8,128)(2,1)S(1)} %finish.1.own_ref), channel_id=1, source_target_pairs={{0,1},{1,0},{2,3},{3,2},{4,5},{5,4},{6,7},{7,6},{8,9},{9,8},{10,11... | collective-permute-start | bytes 24584 | tf_op jit(solution)/shard_map/ppermute | solution.py:55

commit v12 on v11

--- a/solution.py
+++ b/solution.py
@@ -15,6 +15,7 @@
 ALL = ("y", "z", "x", "c")
 CHIPS = ("y", "z", "x")
 PLANE = ("y", "x")
+NEAR = ("y", "x", "c")
 LOG2E = 1.4426950408889634
 NONE = -1e30
 HIDDEN = -2e30
@@ -305,16 +306,9 @@
 
 def finish_body(in_ref, out_ref):
     out, _, total = merged(tiles_of(in_ref))
-    out_ref[...] = (out / total).astype(BF16)
-
-
-def pair_body(own_ref, came_ref, out_ref):
-    first = lax.axis_index("c") == 0
-    own, came = own_ref[...].astype(F32), came_ref[...].astype(F32)
-    tiles = (jnp.where(first, own, came).astype(BF16), jnp.where(first, came, own).astype(BF16))
+    out = (out / total).astype(BF16)
     for d in range(out_ref.shape[0]):
-        for n, tile in enumerate(tiles):
-            out_ref[d, n * 32 : (n + 1) * 32, :] = tile
+        out_ref[d] = out
 
 
 def place_body(in_ref, out_hbm, out_ref, sems):
@@ -323,7 +317,7 @@
     eye = where_one((row % 16) * 8 + row // 16 == lanes((128, 128)))
     for g in range(KVH):
         half, y = divmod(g, 4)
-        block = in_ref[y * 4 : (y + 1) * 4, half * 32 : (half + 1) * 32, :].reshape(128, 128)
+        block = jnp.concatenate([in_ref[(y * 4 + n) * 2 + half] for n in range(4)], axis=0)
         block = dot(eye, block, NT).astype(BF16)
         for i in range(8):
             at = (g * 8 + i) * HD
@@ -403,9 +397,8 @@
     parts = exchange(parts, PLANE)
     parts = call(merge_body, "merge", shape((8, 40, 128), BF16), parts)
     parts = exchange(parts, ("z",))
-    tile = call(finish_body, "finish", shape((32, 128), BF16), parts)
-    whole = call(pair_body, "pair", shape((16, 64, 128), BF16), tile, swap(tile))
-    whole = exchange(whole, PLANE)
+    whole = call(finish_body, "finish", shape((32, 32, 128), BF16), parts)
+    whole = exchange(whole, NEAR)
     return call(
         place_body,
         "place",

time: 72.1 us -> 72.3 us (level)
  blocking collectives: 58.5 us -> 62 us
  starting transfers between devices: 5.58 us -> 3.07 us
  waiting for transfers between devices: 0.83 us -> 0.01 us
    all_to_all x4, blocking collectives: 58.5 us -> 62 us  [exchange(): return lax.all_to_all(tiles, axes, 0, 0, tiled=True)]
    ppermute x3 -> x2, starting transfers between devices: 5.58 us -> 3.07 us  [swap(): return lax.ppermute(value, 'c', ((0, 1), (1, 0)))]
    ppermute x3 -> x2, waiting for transfers between devices: 0.83 us -> 0.01 us  [swap(): return lax.ppermute(value, 'c', ((0, 1), (1, 0)))]
    pallas_call x9 -> x8, Pallas kernels: 6.84 us -> 6.84 us  [call(): pl.pallas_call(body, name=name, out_shape=out_shape, in_specs=specs or [V...]
  transfers between devices with their start and end apart: 3 -> 2, of which waited for: 1 -> 0; matrix products, arithmetic and copies ran while one was open for 0% -> 0% of each run, Pallas kernels for 4% -> 4%
where the time goes in v12:
time: 72.3 us; the launch traced here: 72 us
  blocking collectives  62 us (86%)
  Pallas kernels  6.84 us (9%)
  starting transfers between devices  3.07 us (4%)
    all_to_all x4, blocking collectives, exchange(): return lax.all_to_all(tiles, axes, 0, 0, tiled=True)  62 us
    pallas_call x8, Pallas kernels, call(): pl.pallas_call(body, name=name, out_shape=out_shape, in_specs=specs or [V...  6.84 us
    ppermute x2, starting transfers between devices, swap(): return lax.ppermute(value, 'c', ((0, 1), (1, 0)))  3.07 us
  transfers between devices with their start and end apart: 2, of which 0 were waited for; matrix products, arithmetic and copies ran while one was open for 0% of the time, Pallas kernels for 4%

profile of v12, /device:TPU:1, one launch (start us, length us, event | category | flops | bytes accessed | tf_op | source)
XLA Modules:
  0.0 72.0 jit_solution(14106832298060911561)
XLA Ops:
  0.0 0.0 copy-start
  0.0 1.2 %pack.1 = (bf16[768,128]{1,0:T(8,128)(2,1)S(1)}, s32[3,16]{1,0:T(4,128)S(1)}, s32[1,16]{1,0:T(1,128)S(1)}, s32[4,128]{1,0:T(4,128)S(1)}) custom-call(bf16[16,32]{1,0:T(8,128)(2,1)} %refs_0_.1, bf16[4,16]{1,0:T(4,128)(2,1)} %bitcast.10, bf16[4,16]{1,0:T(4,128)(2,1)} %bitcast.11, s32[3,16]{1,0:T(4,128)} %refs_3_.1, s32[1,16]{1,0:T(1,128)} %bitcast.12, ...), custom_call_target="tpu_custom_call" | custom-call | tf_op jit(solution)/shard_map/pack/pallas_call | solution.py:31
  1.2 27.4 %all_to_all.20 = bf16[384,2,128]{2,1,0:T(2,128)(2,1)S(1)} all-to-all(bf16[384,2,128]{2,1,0:T(2,128)(2,1)S(1)} %bitcast.8), channel_id=1, replica_groups=mesh['y'=4,'z'=8,'x'=4,'c'=2] {'y','z','x'}, dimensions={0} | all-to-all | bytes 393216 | tf_op jit(solution)/shard_map/all_to_all | solution.py:52
  28.6 3.0 %collective-permute-start = (bf16[768,128]{1,0:T(8,128)(2,1)S(1)}, bf16[768,128]{1,0:T(8,128)(2,1)S(1)}, u32[]{:S(2)}, u32[]{:S(2)}) collective-permute-start(bf16[768,128]{1,0:T(8,128)(2,1)S(1)} %bitcast.6), channel_id=1, source_target_pairs={{0,1},{1,0},{2,3},{3,2},{4,5},{5,4},{6,7},{7,6},{8,9},{9,8},{10,11... | collective-permute-start | bytes 589832 | tf_op jit(solution)/shard_map/ppermute | solution.py:56
  31.6 1.8 %ready.1 = (f32[528,128]{1,0:T(8,128)S(1)}, f32[2,16,128]{2,1,0:T(8,128)S(1)}, bf16[8,128,512]{2,1,0:T(8,128)(2,1)S(1)}) custom-call(s32[3,16]{1,0:T(4,128)S(1)} %get-tuple-element.16.pos_ref, s32[1,16]{1,0:T(1,128)S(1)} %get-tuple-element.17.seg_ref, s32[4,128]{1,0:T(4,128)S(1)} %get-tuple-element.18.held_ref, bf16[512,1024]{1,0:T(8,128)(2,1)} %v_hbm.1), custom_call_target="tpu_custom_call" | custom-call | tf_op jit(solution)/shard_map/ready/pallas_call | solution.py:31
  33.4 0.0 collective-permute-done.came_ref
  33.4 0.0 copy-done
  33.4 1.2 %first.1 = (bf16[16,40,128]{2,1,0:T(8,128)(2,1)S(1)}, bf16[1024,128]{1,0:T(8,128)(2,1)S(1)}, f32[2,128,128]{2,1,0:T(8,128)S(1)}) custom-call(bf16[768,128]{1,0:T(8,128)(2,1)S(1)} %bitcast.7, bf16[768,128]{1,0:T(8,128)(2,1)S(1)} %collective-permute-done.came_ref, f32[2,16,128]{2,1,0:T(8,128)S(1)} %get-tuple-element.19.table_ref, ...), custom_call_target="tpu_custom_call" | custom-call | tf_op jit(solution)/shard_map/first/pallas_call | solution.py:31
  34.6 0.1 collective-permute-start.1
  34.7 1.4 %second.1.own_ref = bf16[16,40,128]{2,1,0:T(8,128)(2,1)S(1)} custom-call(bf16[1024,128]{1,0:T(8,128)(2,1)S(1)} %get-tuple-element.22.q_ref, bf16[512,1024]{1,0:T(8,128)(2,1)S(1)} %copy-done, bf16[8,128,512]{2,1,0:T(8,128)(2,1)S(1)} %get-tuple-element.20.vt_ref, f32[528,128]{1,0:T(8,128)S(1)} %get-tuple-element.21.bias_ref, ...), custom_call_target="tpu_custom_call" | custom-call | tf_op jit(solution)/shard_map/second/pallas_call | solution.py:31
  36.2 0.0 collective-permute-done.1.came_ref
  36.2 0.1 couple.1
  36.3 10.4 %all_to_all.21.in_ref = bf16[16,40,128]{2,1,0:T(8,128)(2,1)S(1)} all-to-all(bf16[16,40,128]{2,1,0:T(8,128)(2,1)S(1)} %couple.1), channel_id=1, replica_groups=mesh['y'=4,'z'=8,'x'=4,'c'=2] {'y','x'}, dimensions={0} | all-to-all | bytes 327680 | tf_op jit(solution)/shard_map/all_to_all | solution.py:52
  46.7 0.1 merge.1
  46.8 9.8 %all_to_all.22.in_ref = bf16[8,40,128]{2,1,0:T(8,128)(2,1)S(1)} all-to-all(bf16[8,40,128]{2,1,0:T(8,128)(2,1)S(1)} %merge.1), channel_id=1, replica_groups=mesh['y'=4,'z'=8,'x'=4,'c'=2] {'z'}, dimensions={0} | all-to-all | bytes 163840 | tf_op jit(solution)/shard_map/all_to_all | solution.py:52
  56.6 0.1 finish.1
  56.6 14.4 %all_to_all.23.in_ref = bf16[32,32,128]{2,1,0:T(8,128)(2,1)S(1)} all-to-all(bf16[32,32,128]{2,1,0:T(8,128)(2,1)S(1)} %finish.1), channel_id=1, replica_groups=mesh['y'=4,'z'=8,'x'=4,'c'=2] {'y','x','c'}, dimensions={0} | all-to-all | bytes 524288 | tf_op jit(solution)/shard_map/all_to_all | solution.py:52
  71.0 1.0 %place.1 = bf16[16,8192]{1,0:T(8,128)(2,1)} custom-call(bf16[32,32,128]{2,1,0:T(8,128)(2,1)S(1)} %all_to_all.23.in_ref), custom_call_target="tpu_custom_call" | custom-call | tf_op jit(solution)/shard_map/place/pallas_call | solution.py:31
Async XLA Ops:
  0.0 33.4 %copy-start = (bf16[512,1024]{1,0:T(8,128)(2,1)S(1)}, bf16[512,1024]{1,0:T(8,128)(2,1)}, u32[]{:S(2)}) copy-start(bf16[512,1024]{1,0:T(8,128)(2,1)} %k_ref.3) | copy-start | bytes 3145732
  28.6 4.8 %collective-permute-start = (bf16[768,128]{1,0:T(8,128)(2,1)S(1)}, bf16[768,128]{1,0:T(8,128)(2,1)S(1)}, u32[]{:S(2)}, u32[]{:S(2)}) collective-permute-start(bf16[768,128]{1,0:T(8,128)(2,1)S(1)} %bitcast.6), channel_id=1, source_target_pairs={{0,1},{1,0},{2,3},{3,2},{4,5},{5,4},{6,7},{7,6},{8,9},{9,8},{10,11... | collective-permute-start | bytes 589832 | tf_op jit(solution)/shard_map/ppermute | solution.py:56
  34.6 1.5 %collective-permute-start.1 = (bf16[16,40,128]{2,1,0:T(8,128)(2,1)S(1)}, bf16[16,40,128]{2,1,0:T(8,128)(2,1)S(1)}, u32[]{:S(2)}, u32[]{:S(2)}) collective-permute-start(bf16[16,40,128]{2,1,0:T(8,128)(2,1)S(1)} %get-tuple-element.24), channel_id=1, source_target_pairs={{0,1},{1,0},{2,3},{3,2},{4,5},{5,4},{6,7},{7,6},{8,9},{9,8},{10,11... | collective-permute-start | bytes 491528 | tf_op jit(solution)/shard_map/ppermute | solution.py:56

commit v13 on v12

--- a/solution.py
+++ b/solution.py
@@ -15,7 +15,6 @@
 ALL = ("y", "z", "x", "c")
 CHIPS = ("y", "z", "x")
 PLANE = ("y", "x")
-NEAR = ("y", "x", "c")
 LOG2E = 1.4426950408889634
 NONE = -1e30
 HIDDEN = -2e30
@@ -80,16 +79,19 @@
     ]
     for copy in copies:
         copy.start()
+    wide = where_one(lanes((32, 128)) % 32 == rows_of((32, 128)))
+    late = lanes((ROWS, 128)) // 32 == rows_of((ROWS, 128)) // 4
+    token = lanes((ROWS, 128)) // 4 - rows_of((ROWS, 128))
+    keys, values = where_one(token == 0), where_one(token == 16)
+    column = lanes((4, 128)) % 4 == rows_of((4, 128))
+    q_rows = where_one(rows_of((48, ROWS)) % 6 == lanes((48, ROWS)) % 4)
+    kv_rows = where_one(rows_of((48, 4)) % 6 == 4)
     for copy in copies:
         copy.wait()
-    q = dot(q_ref[...], where_one(lanes((32, 128)) % 32 == rows_of((32, 128))), NN)
-    q = jnp.where(lanes((ROWS, 128)) // 32 == rows_of((ROWS, 128)) // 4, q, 0.0).astype(BF16)
-    token = lanes((ROWS, 128)) // 4 - rows_of((ROWS, 128))
-    kv = dot(k_ref[...], where_one(token == 0), NN) + dot(v_ref[...], where_one(token == 16), NN)
-    kv = jnp.where(lanes((4, 128)) % 4 == rows_of((4, 128)), kv, 0.0).astype(BF16)
-    tiles = dot(where_one(rows_of((48, ROWS)) % 6 == lanes((48, ROWS)) % 4), q, NN)
-    tiles = tiles + dot(where_one(rows_of((48, 4)) % 6 == 4), kv, NN)
-    tiles = tiles.astype(BF16)
+    q = jnp.where(late, dot(q_ref[...], wide, NN), 0.0).astype(BF16)
+    kv = dot(k_ref[...], keys, NN) + dot(v_ref[...], values, NN)
+    kv = jnp.where(column, kv, 0.0).astype(BF16)
+    tiles = (dot(q_rows, q, NN) + dot(kv_rows, kv, NN)).astype(BF16)
     for n in range(out_ref.shape[0] // 48):
         out_ref[n * 48 : (n + 1) * 48, :] = tiles
 
@@ -167,27 +169,27 @@
         vt_ref[g] = v_ref[:, g * HD : (g + 1) * HD].T
 
 
-def join(own_ref, came_ref, table_ref, q_ref, kv_ref, flat_ref):
+def join(base, own_ref, came_ref, table_ref, q_ref, flat_ref):
     c = lax.axis_index("c")
     shape = (128, 4 * 128)
     source, target = rows_of(shape), lanes(shape)
-    whole = jnp.zeros((256, 512), F32)
+    rows = pl.ds(pl.multiple_of(base * 96, 384), 384)
+    whole = jnp.zeros((128, 512), F32)
     for n, ref in enumerate((own_ref, came_ref)):
-        flat_ref[n, 0:768, :] = ref[...].astype(F32)
-        kv_ref[n] = flat_ref[n, pl.ds(4, 128, stride=6), :]
+        flat_ref[n, 0:384, :] = ref[rows, :].astype(F32)
         for half in range(2):
             part = jnp.concatenate(
-                [flat_ref[n, pl.ds(j + 6 * half, 64, stride=12), :] for j in range(4)], axis=0
+                [flat_ref[n, pl.ds(j + 6 * half, 32, stride=12), :] for j in range(4)], axis=0
             )
             core = 1 - c if n else c
             at = (source // 32) * 128 + half * 64 + core * 32 + source % 32
             whole = whole + dot(part.astype(BF16), where_one(target == at), NN)
     for r in range(ROWS):
         high, low = divmod(r, 4)
-        part = whole[low * 64 : (low + 1) * 64, high * 128 : (high + 1) * 128]
+        part = whole[low * 32 : (low + 1) * 32, high * 128 : (high + 1) * 128]
         part = rotate(part, table_ref[0, r : r + 1, :], table_ref[1, r : r + 1, :]).astype(BF16)
-        for g in range(KVH):
-            q_ref[g * 128 + r * 8 : g * 128 + r * 8 + 8, :] = part[g * 8 : (g + 1) * 8]
+        for i in range(4):
+            q_ref[i * 128 + r * 8 : i * 128 + r * 8 + 8, :] = part[i * 8 : (i + 1) * 8]
 
 
 FACTOR = LOG2E / HD**0.5
@@ -207,7 +209,7 @@
 
 def attend(base, q_ref, k_ref, vt_ref, bias_ref, out_ref):
     scores = [
-        dot(k_ref[:, heads_at(base, i)], q_ref[heads_at(base, i), :], NT) * FACTOR
+        dot(k_ref[:, heads_at(base, i)], q_ref[i * 128 : (i + 1) * 128, :], NT) * FACTOR
         + bias_ref[0:512, :]
         for i in range(4)
     ]
@@ -224,21 +226,25 @@
 
 
 def first_body(
-    own_ref, came_ref, table_ref, k_ref, vt_ref, bias_ref, out_ref, q_ref, kv_ref, flat_ref
+    own_ref, came_ref, table_ref, k_ref, vt_ref, bias_ref, out_ref, q_ref, flat_ref
 ):
-    join(own_ref, came_ref, table_ref, q_ref, kv_ref, flat_ref)
-    attend((1 - lax.axis_index("c")) * 4, q_ref, k_ref, vt_ref, bias_ref, out_ref)
-
-
-def second_body(q_ref, k_ref, vt_ref, bias_ref, kv_ref, table_ref, out_ref):
+    base = (1 - lax.axis_index("c")) * 4
+    join(base, own_ref, came_ref, table_ref, q_ref, flat_ref)
+    attend(base, q_ref, k_ref, vt_ref, bias_ref, out_ref)
+
+
+def second_body(
+    own_ref, came_ref, table_ref, k_ref, vt_ref, bias_ref, out_ref, q_ref, flat_ref
+):
     c, y = lax.axis_index("c"), lax.axis_index("y")
+    join(c * 4, own_ref, came_ref, table_ref, q_ref, flat_ref)
     attend(c * 4, q_ref, k_ref, vt_ref, bias_ref, out_ref)
 
     @pl.when((lax.axis_index("z") == 0) & (lax.axis_index("x") == 0))
     def _():
-        g = c * 4 + y
-        chips = pl.ds(pl.multiple_of(g * 16, 16), 16)
-        own, came = kv_ref[0, chips, :], kv_ref[1, chips, :]
+        chips = rows_of((16, 6 * 16)) * 6 + 4 == lanes((16, 6 * 16))
+        rows = pl.ds(pl.multiple_of((c * 4 + y) * 96, 96), 96)
+        own, came = [dot(where_one(chips), ref[rows, :], NN) for ref in (own_ref, came_ref)]
         held = [jnp.where(c == core, own, came).astype(BF16) for core in range(2)]
         row, lane = rows_of((64, 128)), lanes((64, 128))
         found = []
@@ -255,7 +261,7 @@
             if kind == 0:
                 value = rotate(value, table_ref[0], table_ref[1])
             found.append(value.astype(BF16))
-        scores = dot(found[0], q_ref[heads_at(c * 4, y), :], NT) * FACTOR + bias_ref[512:, :]
+        scores = dot(found[0], q_ref[heads_at(0, y), :], NT) * FACTOR + bias_ref[512:, :]
         weights, peak, total = softened(scores)
         own = dot(found[1], weights, TN)
         for n in range(4):
@@ -311,23 +317,31 @@
         out_ref[d] = out
 
 
-def place_body(in_ref, out_hbm, out_ref, sems):
-    copies = []
+def upright(in_ref, g):
     row = rows_of((128, 128))
-    eye = where_one((row % 16) * 8 + row // 16 == lanes((128, 128)))
-    for g in range(KVH):
-        half, y = divmod(g, 4)
-        block = jnp.concatenate([in_ref[(y * 4 + n) * 2 + half] for n in range(4)], axis=0)
-        block = dot(eye, block, NT).astype(BF16)
+    order = where_one((row % 16) * 8 + row // 16 == lanes((128, 128)))
+    block = in_ref[g * 4 : (g + 1) * 4].reshape(128, 128)
+    return dot(order, block, NT).astype(BF16)
+
+
+def half_body(in_ref, out_ref):
+    for g in range(4):
+        block = upright(in_ref, g)
         for i in range(8):
             at = (g * 8 + i) * HD
             out_ref[:, at : at + HD] = block[i * ROWS : (i + 1) * ROWS]
-        if g % 2:
-            part = slice((g - 1) * 8 * HD, (g + 1) * 8 * HD)
-            copies.append(
-                pltpu.make_async_copy(out_ref.at[:, part], out_hbm.at[:, part], sems.at[g // 2])
-            )
-            copies[-1].start()
+
+
+def place_body(in_ref, own_ref, out_hbm, out_ref, sems):
+    half = H * HD // 2
+    c = lax.axis_index("c")
+    mine = pl.ds(pl.multiple_of(c * half, half), half)
+    copies = [pltpu.make_async_copy(own_ref, out_hbm.at[:, mine], sems.at[0])]
+    copies[0].start()
+    half_body(in_ref, out_ref)
+    rest = pl.ds(pl.multiple_of((1 - c) * half, half), half)
+    copies.append(pltpu.make_async_copy(out_ref, out_hbm.at[:, rest], sems.at[1]))
+    copies[1].start()
     for copy in copies:
         copy.wait()
 
@@ -377,34 +391,25 @@
         scratch=[pltpu.VMEM((512, KVH * HD), BF16), pltpu.SemaphoreType.DMA],
     )
     message = shape((16, 40, 128), BF16)
-    parts, q, kv = call(
-        first_body,
-        "first",
-        (message, shape((H * ROWS, HD), BF16), shape((2, 128, 128), F32)),
-        tiles,
-        came,
-        tables,
-        cache_keys,
-        turned_values,
-        bias,
-        scratch=[pltpu.VMEM((2, 6 * 128 + 16, 128), F32)],
-    )
+    operands = (tiles, came, tables, cache_keys, turned_values, bias)
+    scratch = [pltpu.VMEM((4 * 128, HD), BF16), pltpu.VMEM((2, 400, 128), F32)]
+    parts = call(first_body, "first", message, *operands, scratch=scratch)
     other = swap(parts)
-    parts = call(
-        second_body, "second", message, q, cache_keys, turned_values, bias, kv, tables
-    )
+    parts = call(second_body, "second", message, *operands, scratch=scratch)
     parts = call(couple_body, "couple", message, parts, other)
     parts = exchange(parts, PLANE)
     parts = call(merge_body, "merge", shape((8, 40, 128), BF16), parts)
     parts = exchange(parts, ("z",))
-    whole = call(finish_body, "finish", shape((32, 32, 128), BF16), parts)
-    whole = exchange(whole, NEAR)
+    whole = call(finish_body, "finish", shape((16, 32, 128), BF16), parts)
+    whole = exchange(whole, PLANE)
+    own = call(half_body, "half", shape((ROWS, H * HD // 2), BF16), whole)
     return call(
         place_body,
         "place",
         shape((ROWS, H * HD), BF16),
-        whole,
-        scratch=[pltpu.VMEM((ROWS, H * HD), BF16), pltpu.SemaphoreType.DMA((4,))],
+        swap(whole),
+        own,
+        scratch=[pltpu.VMEM((ROWS, H * HD // 2), BF16), pltpu.SemaphoreType.DMA((2,))],
         out_specs=HBM,
     )
 

time: 72.3 us -> 72.2 us (level)
  blocking collectives: 62 us -> 56.8 us
  starting transfers between devices: 3.07 us -> 7.05 us
  waiting for transfers between devices: 0.01 us -> 0.78 us
    all_to_all x4, blocking collectives: 62 us -> 56.8 us  [exchange(): return lax.all_to_all(tiles, axes, 0, 0, tiled=True)]
    ppermute x2 -> x3, starting transfers between devices: 3.07 us -> 7.05 us  [swap(): return lax.ppermute(value, 'c', ((0, 1), (1, 0)))]
    ppermute x2 -> x3, waiting for transfers between devices: 0.01 us -> 0.78 us  [swap(): return lax.ppermute(value, 'c', ((0, 1), (1, 0)))]
    pallas_call x8 -> x9, Pallas kernels: 6.84 us -> 7.21 us  [call(): pl.pallas_call(body, name=name, out_shape=out_shape, in_specs=specs or [V...]
  transfers between devices with their start and end apart: 2 -> 3, of which waited for: 0 -> 1; matrix products, arithmetic and copies ran while one was open for 0% -> 0% of each run, Pallas kernels for 4% -> 5%
where the time goes in v13:
time: 72.2 us; the launch traced here: 71.9 us
  blocking collectives  56.8 us (79%)
  Pallas kernels  7.21 us (10%)
  starting transfers between devices  7.05 us (10%)
  waiting for transfers between devices  0.78 us (1%)
    all_to_all x4, blocking collectives, exchange(): return lax.all_to_all(tiles, axes, 0, 0, tiled=True)  56.8 us
    pallas_call x9, Pallas kernels, call(): pl.pallas_call(body, name=name, out_shape=out_shape, in_specs=specs or [V...  7.21 us
    ppermute x3, starting transfers between devices, swap(): return lax.ppermute(value, 'c', ((0, 1), (1, 0)))  7.05 us
  transfers between devices with their start and end apart: 3, of which 1 were waited for; matrix products, arithmetic and copies ran while one was open for 0% of the time, Pallas kernels for 5%

profile of v13, /device:TPU:1, one launch (start us, length us, event | category | flops | bytes accessed | tf_op | source)
XLA Modules:
  0.0 71.9 jit_solution(11222503298857638499)
XLA Ops:
  0.0 0.0 copy-start
  0.0 1.2 %pack.1 = (bf16[768,128]{1,0:T(8,128)(2,1)S(1)}, s32[3,16]{1,0:T(4,128)S(1)}, s32[1,16]{1,0:T(1,128)S(1)}, s32[4,128]{1,0:T(4,128)S(1)}) custom-call(bf16[16,32]{1,0:T(8,128)(2,1)} %refs_0_.1, bf16[4,16]{1,0:T(4,128)(2,1)} %bitcast.11, bf16[4,16]{1,0:T(4,128)(2,1)} %bitcast.12, s32[3,16]{1,0:T(4,128)} %refs_3_.1, s32[1,16]{1,0:T(1,128)} %bitcast.13, ...), custom_call_target="tpu_custom_call" | custom-call | tf_op jit(solution)/shard_map/pack/pallas_call | solution.py:30
  1.2 27.4 %all_to_all.20 = bf16[384,2,128]{2,1,0:T(2,128)(2,1)S(1)} all-to-all(bf16[384,2,128]{2,1,0:T(2,128)(2,1)S(1)} %bitcast.9), channel_id=1, replica_groups=mesh['y'=4,'z'=8,'x'=4,'c'=2] {'y','z','x'}, dimensions={0} | all-to-all | bytes 393216 | tf_op jit(solution)/shard_map/all_to_all | solution.py:51
  28.6 3.0 %collective-permute-start = (bf16[768,128]{1,0:T(8,128)(2,1)S(1)}, bf16[768,128]{1,0:T(8,128)(2,1)S(1)}, u32[]{:S(2)}, u32[]{:S(2)}) collective-permute-start(bf16[768,128]{1,0:T(8,128)(2,1)S(1)} %bitcast.6), channel_id=1, source_target_pairs={{0,1},{1,0},{2,3},{3,2},{4,5},{5,4},{6,7},{7,6},{8,9},{9,8},{10,11... | collective-permute-start | bytes 589832 | tf_op jit(solution)/shard_map/ppermute | solution.py:55
  31.6 1.8 %ready.1 = (f32[528,128]{1,0:T(8,128)S(1)}, f32[2,16,128]{2,1,0:T(8,128)S(1)}, bf16[8,128,512]{2,1,0:T(8,128)(2,1)S(1)}) custom-call(s32[3,16]{1,0:T(4,128)S(1)} %get-tuple-element.13.pos_ref, s32[1,16]{1,0:T(1,128)S(1)} %get-tuple-element.14.seg_ref, s32[4,128]{1,0:T(4,128)S(1)} %get-tuple-element.15.held_ref, bf16[512,1024]{1,0:T(8,128)(2,1)} %v_hbm.1), custom_call_target="tpu_custom_call" | custom-call | tf_op jit(solution)/shard_map/ready/pallas_call | solution.py:30
  33.4 0.0 collective-permute-done.came_ref
  33.4 0.0 copy-done
  33.4 1.1 %first.1 = bf16[16,40,128]{2,1,0:T(8,128)(2,1)S(1)} custom-call(bf16[768,128]{1,0:T(8,128)(2,1)S(1)} %bitcast.7, bf16[768,128]{1,0:T(8,128)(2,1)S(1)} %collective-permute-done.came_ref, f32[2,16,128]{2,1,0:T(8,128)S(1)} %get-tuple-element.16.table_ref, bf16[512,1024]{1,0:T(8,128)(2,1)S(1)} %copy-done, bf16[8,128,512]{2,1,0:T(8,128)(2,1)S(1)} %get-tuple-element.17.vt_ref, ...), custom_call_target="tpu_custom_call" | custom-call | tf_op jit(solution)/shard_map/first/pallas_call | solution.py:30
  34.5 0.1 collective-permute-start.1
  34.6 1.8 %second.1.own_ref = bf16[16,40,128]{2,1,0:T(8,128)(2,1)S(1)} custom-call(bf16[768,128]{1,0:T(8,128)(2,1)S(1)} %bitcast.8, bf16[768,128]{1,0:T(8,128)(2,1)S(1)} %collective-permute-done.came_ref, f32[2,16,128]{2,1,0:T(8,128)S(1)} %get-tuple-element.16.table_ref, bf16[512,1024]{1,0:T(8,128)(2,1)S(1)} %copy-done, ...), custom_call_target="tpu_custom_call" | custom-call | tf_op jit(solution)/shard_map/second/pallas_call | solution.py:30
  36.4 0.0 collective-permute-done.1.came_ref
  36.4 0.1 couple.1
  36.6 9.7 %all_to_all.21.in_ref = bf16[16,40,128]{2,1,0:T(8,128)(2,1)S(1)} all-to-all(bf16[16,40,128]{2,1,0:T(8,128)(2,1)S(1)} %couple.1), channel_id=1, replica_groups=mesh['y'=4,'z'=8,'x'=4,'c'=2] {'y','x'}, dimensions={0} | all-to-all | bytes 327680 | tf_op jit(solution)/shard_map/all_to_all | solution.py:51
  46.3 0.1 merge.1
  46.4 9.8 %all_to_all.22.in_ref = bf16[8,40,128]{2,1,0:T(8,128)(2,1)S(1)} all-to-all(bf16[8,40,128]{2,1,0:T(8,128)(2,1)S(1)} %merge.1), channel_id=1, replica_groups=mesh['y'=4,'z'=8,'x'=4,'c'=2] {'z'}, dimensions={0} | all-to-all | bytes 163840 | tf_op jit(solution)/shard_map/all_to_all | solution.py:51
  56.2 9.9 %all_to_all.23.in_ref = bf16[16,32,128]{2,1,0:T(8,128)(2,1)S(1)} all-to-all(bf16[16,32,128]{2,1,0:T(8,128)(2,1)S(1)} %finish.1), channel_id=1, replica_groups=mesh['y'=4,'z'=8,'x'=4,'c'=2] {'y','x'}, dimensions={0} | all-to-all | bytes 262144 | tf_op jit(solution)/shard_map/all_to_all | solution.py:51
  66.1 4.0 %collective-permute-start.2 = (bf16[16,32,128]{2,1,0:T(8,128)(2,1)S(1)}, bf16[16,32,128]{2,1,0:T(8,128)(2,1)S(1)}, u32[]{:S(2)}, u32[]{:S(2)}) collective-permute-start(bf16[16,32,128]{2,1,0:T(8,128)(2,1)S(1)} %all_to_all.23.in_ref), channel_id=1, source_target_pairs={{0,1},{1,0},{2,3},{3,2},{4,5},{5,4},{6,7},{7,6},{8,9},{9,8},{10,11... | collective-permute-start | bytes 393224 | tf_op jit(solution)/shard_map/ppermute | solution.py:55
  70.1 0.2 half.1.own_ref
  70.3 0.8 %collective-permute-done.2.in_ref = bf16[16,32,128]{2,1,0:T(8,128)(2,1)S(1)} collective-permute-done((bf16[16,32,128]{2,1,0:T(8,128)(2,1)S(1)}, bf16[16,32,128]{2,1,0:T(8,128)(2,1)S(1)}, u32[]{:S(2)}, u32[]{:S(2)}) %collective-permute-start.2) | collective-permute-done | bytes 131104 | tf_op jit(solution)/shard_map/ppermute | solution.py:55
  71.1 0.9 %place.1 = bf16[16,8192]{1,0:T(8,128)(2,1)} custom-call(bf16[16,32,128]{2,1,0:T(8,128)(2,1)S(1)} %collective-permute-done.2.in_ref, bf16[16,4096]{1,0:T(8,128)(2,1)S(1)} %half.1.own_ref), custom_call_target="tpu_custom_call" | custom-call | tf_op jit(solution)/shard_map/place/pallas_call | solution.py:30
  (1 shorter events, 0.0 us)
Async XLA Ops:
  0.0 33.4 %copy-start = (bf16[512,1024]{1,0:T(8,128)(2,1)S(1)}, bf16[512,1024]{1,0:T(8,128)(2,1)}, u32[]{:S(2)}) copy-start(bf16[512,1024]{1,0:T(8,128)(2,1)} %k_ref.3) | copy-start | bytes 3145732
  28.6 4.8 %collective-permute-start = (bf16[768,128]{1,0:T(8,128)(2,1)S(1)}, bf16[768,128]{1,0:T(8,128)(2,1)S(1)}, u32[]{:S(2)}, u32[]{:S(2)}) collective-permute-start(bf16[768,128]{1,0:T(8,128)(2,1)S(1)} %bitcast.6), channel_id=1, source_target_pairs={{0,1},{1,0},{2,3},{3,2},{4,5},{5,4},{6,7},{7,6},{8,9},{9,8},{10,11... | collective-permute-start | bytes 589832 | tf_op jit(solution)/shard_map/ppermute | solution.py:55
  34.5 1.9 %collective-permute-start.1 = (bf16[16,40,128]{2,1,0:T(8,128)(2,1)S(1)}, bf16[16,40,128]{2,1,0:T(8,128)(2,1)S(1)}, u32[]{:S(2)}, u32[]{:S(2)}) collective-permute-start(bf16[16,40,128]{2,1,0:T(8,128)(2,1)S(1)} %first.1), channel_id=1, source_target_pairs={{0,1},{1,0},{2,3},{3,2},{4,5},{5,4},{6,7},{7,6},{8,9},{9,8},{10,11... | collective-permute-start | bytes 491528 | tf_op jit(solution)/shard_map/ppermute | solution.py:55
  66.1 5.0 %collective-permute-start.2 = (bf16[16,32,128]{2,1,0:T(8,128)(2,1)S(1)}, bf16[16,32,128]{2,1,0:T(8,128)(2,1)S(1)}, u32[]{:S(2)}, u32[]{:S(2)}) collective-permute-start(bf16[16,32,128]{2,1,0:T(8,128)(2,1)S(1)} %all_to_all.23.in_ref), channel_id=1, source_target_pairs={{0,1},{1,0},{2,3},{3,2},{4,5},{5,4},{6,7},{7,6},{8,9},{9,8},{10,11... | collective-permute-start | bytes 393224 | tf_op jit(solution)/shard_map/ppermute | solution.py:55

commit v14 on v13

--- a/solution.py
+++ b/solution.py
@@ -149,8 +149,18 @@
     return tile.astype(BF16)
 
 
+def half_of(ref, core):
+    half = KVH * HD // 2
+    return ref.at[:, pl.ds(pl.multiple_of(core * half, half), half)]
+
+
+def turn_half(v_ref, vt_ref):
+    for i in range(4):
+        vt_ref[i] = v_ref[:, i * HD : (i + 1) * HD].T
+
+
 def ready_body(pos_ref, seg_ref, held_ref, v_hbm, bias_ref, table_ref, vt_ref, v_ref, sem):
-    copy = pltpu.make_async_copy(v_hbm, v_ref, sem)
+    copy = pltpu.make_async_copy(half_of(v_hbm, 1 - lax.axis_index("c")), v_ref, sem)
     copy.start()
     lane = lanes((ROWS, 128))
     cosine, sine = rope_tables(pos_ref[...], lane % 64)
@@ -165,8 +175,7 @@
     seen = dot(kinds, wanted, TN) * jnp.where(rows_of((ROWS, 128)) <= lane // 8, 1.0, 0.0)
     bias_ref[512:, :] = (seen - 1.0) * -HIDDEN
     copy.wait()
-    for g in range(KVH):
-        vt_ref[g] = v_ref[:, g * HD : (g + 1) * HD].T
+    turn_half(v_ref, vt_ref)
 
 
 def join(base, own_ref, came_ref, table_ref, q_ref, flat_ref):
@@ -214,7 +223,7 @@
         for i in range(4)
     ]
     parts = [softened(s) for s in scores]
-    outs = [dot(vt_ref[base + i], parts[i][0], NN) for i in range(4)]
+    outs = [dot(vt_ref[i], parts[i][0], NN) for i in range(4)]
     for i, (_, peak, total) in enumerate(parts):
         emit(out_ref, i * 4, outs[i].astype(BF16), state_rows(peak, total))
 
@@ -226,11 +235,16 @@
 
 
 def first_body(
-    own_ref, came_ref, table_ref, k_ref, vt_ref, bias_ref, out_ref, q_ref, flat_ref
+    own_ref, came_ref, table_ref, k_ref, vt_ref, bias_ref, v_hbm,
+    out_ref, turned_ref, q_ref, flat_ref, v_ref, sem,
 ):
+    copy = pltpu.make_async_copy(half_of(v_hbm, lax.axis_index("c")), v_ref, sem)
+    copy.start()
     base = (1 - lax.axis_index("c")) * 4
     join(base, own_ref, came_ref, table_ref, q_ref, flat_ref)
     attend(base, q_ref, k_ref, vt_ref, bias_ref, out_ref)
+    copy.wait()
+    turn_half(v_ref, turned_ref)
 
 
 def second_body(
@@ -312,36 +326,35 @@
 
 def finish_body(in_ref, out_ref):
     out, _, total = merged(tiles_of(in_ref))
-    out = (out / total).astype(BF16)
+    out_ref[...] = (out / total).astype(BF16)
+
+
+def pair_body(own_ref, came_ref, out_ref):
+    first = lax.axis_index("c") == 0
+    own, came = own_ref[...].astype(F32), came_ref[...].astype(F32)
+    tiles = (jnp.where(first, own, came).astype(BF16), jnp.where(first, came, own).astype(BF16))
     for d in range(out_ref.shape[0]):
-        out_ref[d] = out
-
-
-def upright(in_ref, g):
+        for n, tile in enumerate(tiles):
+            out_ref[d, n * 32 : (n + 1) * 32, :] = tile
+
+
+def place_body(in_ref, out_hbm, out_ref, sems):
+    copies = []
     row = rows_of((128, 128))
-    order = where_one((row % 16) * 8 + row // 16 == lanes((128, 128)))
-    block = in_ref[g * 4 : (g + 1) * 4].reshape(128, 128)
-    return dot(order, block, NT).astype(BF16)
-
-
-def half_body(in_ref, out_ref):
-    for g in range(4):
-        block = upright(in_ref, g)
+    eye = where_one((row % 16) * 8 + row // 16 == lanes((128, 128)))
+    for g in range(KVH):
+        half, y = divmod(g, 4)
+        block = in_ref[y * 4 : (y + 1) * 4, half * 32 : (half + 1) * 32, :].reshape(128, 128)
+        block = dot(eye, block, NT).astype(BF16)
         for i in range(8):
             at = (g * 8 + i) * HD
             out_ref[:, at : at + HD] = block[i * ROWS : (i + 1) * ROWS]
-
-
-def place_body(in_ref, own_ref, out_hbm, out_ref, sems):
-    half = H * HD // 2
-    c = lax.axis_index("c")
-    mine = pl.ds(pl.multiple_of(c * half, half), half)
-    copies = [pltpu.make_async_copy(own_ref, out_hbm.at[:, mine], sems.at[0])]
-    copies[0].start()
-    half_body(in_ref, out_ref)
-    rest = pl.ds(pl.multiple_of((1 - c) * half, half), half)
-    copies.append(pltpu.make_async_copy(out_ref, out_hbm.at[:, rest], sems.at[1]))
-    copies[1].start()
+        if g % 2:
+            part = slice((g - 1) * 8 * HD, (g + 1) * 8 * HD)
+            copies.append(
+                pltpu.make_async_copy(out_ref.at[:, part], out_hbm.at[:, part], sems.at[g // 2])
+            )
+            copies[-1].start()
     for copy in copies:
         copy.wait()
 
@@ -375,41 +388,46 @@
     )
     tiles = exchange(tiles.reshape(-1, 2, 128), CHIPS).reshape(-1, 128)
     came = swap(tiles)
-    bias, tables, turned_values = call(
+    values = pltpu.with_memory_space_constraint(cache_values, pltpu.HBM)
+    turned = shape((4, HD, 512), BF16)
+    fetched = [pltpu.VMEM((512, 4 * HD), BF16), pltpu.SemaphoreType.DMA]
+    bias, tables, other_values = call(
         ready_body,
         "ready",
-        (
-            shape((512 + ROWS, 128), F32),
-            shape((2, ROWS, 128), F32),
-            shape((KVH, HD, 512), BF16),
-        ),
+        (shape((512 + ROWS, 128), F32), shape((2, ROWS, 128), F32), turned),
         positions,
         span_segments,
         cache_segments,
-        pltpu.with_memory_space_constraint(cache_values, pltpu.HBM),
+        values,
         specs=[VMEM] * 3 + [HBM],
-        scratch=[pltpu.VMEM((512, KVH * HD), BF16), pltpu.SemaphoreType.DMA],
+        scratch=fetched,
     )
     message = shape((16, 40, 128), BF16)
-    operands = (tiles, came, tables, cache_keys, turned_values, bias)
     scratch = [pltpu.VMEM((4 * 128, HD), BF16), pltpu.VMEM((2, 400, 128), F32)]
-    parts = call(first_body, "first", message, *operands, scratch=scratch)
+    parts, own_values = call(
+        first_body,
+        "first",
+        (message, turned),
+        *(tiles, came, tables, cache_keys, other_values, bias, values),
+        specs=[VMEM] * 6 + [HBM],
+        scratch=scratch + fetched,
+    )
     other = swap(parts)
+    operands = (tiles, came, tables, cache_keys, own_values, bias)
     parts = call(second_body, "second", message, *operands, scratch=scratch)
     parts = call(couple_body, "couple", message, parts, other)
     parts = exchange(parts, PLANE)
     parts = call(merge_body, "merge", shape((8, 40, 128), BF16), parts)
     parts = exchange(parts, ("z",))
-    whole = call(finish_body, "finish", shape((16, 32, 128), BF16), parts)
+    tile = call(finish_body, "finish", shape((32, 128), BF16), parts)
+    whole = call(pair_body, "pair", shape((16, 64, 128), BF16), tile, swap(tile))
     whole = exchange(whole, PLANE)
-    own = call(half_body, "half", shape((ROWS, H * HD // 2), BF16), whole)
     return call(
         place_body,
         "place",
         shape((ROWS, H * HD), BF16),
-        swap(whole),
-        own,
-        scratch=[pltpu.VMEM((ROWS, H * HD // 2), BF16), pltpu.SemaphoreType.DMA((2,))],
+        whole,
+        scratch=[pltpu.VMEM((ROWS, H * HD), BF16), pltpu.SemaphoreType.DMA((4,))],
         out_specs=HBM,
     )
 

time: 72.2 us -> 73 us (1.011)
  blocking collectives: 56.8 us -> 57.9 us
  starting transfers between devices: 7.05 us -> 5.96 us
    ppermute x3, starting transfers between devices: 7.05 us -> 5.96 us  [swap(): return lax.ppermute(value, 'c', ((0, 1), (1, 0)))]
    all_to_all x4, blocking collectives: 56.8 us -> 57.9 us  [exchange(): return lax.all_to_all(tiles, axes, 0, 0, tiled=True)]
where the time goes in v14:
time: 73 us; the launch traced here: 72.6 us
  blocking collectives  57.9 us (79%)
  Pallas kernels  7.89 us (11%)
  starting transfers between devices  5.96 us (8%)
  waiting for transfers between devices  0.83 us (1%)
    all_to_all x4, blocking collectives, exchange(): return lax.all_to_all(tiles, axes, 0, 0, tiled=True)  57.9 us
    pallas_call x9, Pallas kernels, call(): pl.pallas_call(body, name=name, out_shape=out_shape, in_specs=specs or [V...  7.89 us
    ppermute x3, starting transfers between devices, swap(): return lax.ppermute(value, 'c', ((0, 1), (1, 0)))  5.96 us
  transfers between devices with their start and end apart: 3, of which 1 were waited for; matrix products, arithmetic and copies ran while one was open for 0% of the time, Pallas kernels for 5%

profile of v14, /device:TPU:1, one launch (start us, length us, event | category | flops | bytes accessed | tf_op | source)
XLA Modules:
  0.0 72.6 jit_solution(14166752862690172679)
XLA Ops:
  0.0 0.0 copy-start
  0.0 1.2 %pack.1 = (bf16[768,128]{1,0:T(8,128)(2,1)S(1)}, s32[3,16]{1,0:T(4,128)S(1)}, s32[1,16]{1,0:T(1,128)S(1)}, s32[4,128]{1,0:T(4,128)S(1)}) custom-call(bf16[16,32]{1,0:T(8,128)(2,1)} %refs_0_.1, bf16[4,16]{1,0:T(4,128)(2,1)} %bitcast.11, bf16[4,16]{1,0:T(4,128)(2,1)} %bitcast.12, s32[3,16]{1,0:T(4,128)} %refs_3_.1, s32[1,16]{1,0:T(1,128)} %bitcast.13, ...), custom_call_target="tpu_custom_call" | custom-call | tf_op jit(solution)/shard_map/pack/pallas_call | solution.py:30
  1.2 27.4 %all_to_all.20 = bf16[384,2,128]{2,1,0:T(2,128)(2,1)S(1)} all-to-all(bf16[384,2,128]{2,1,0:T(2,128)(2,1)S(1)} %bitcast.9), channel_id=1, replica_groups=mesh['y'=4,'z'=8,'x'=4,'c'=2] {'y','z','x'}, dimensions={0} | all-to-all | bytes 393216 | tf_op jit(solution)/shard_map/all_to_all | solution.py:51
  28.6 3.0 %collective-permute-start = (bf16[768,128]{1,0:T(8,128)(2,1)S(1)}, bf16[768,128]{1,0:T(8,128)(2,1)S(1)}, u32[]{:S(2)}, u32[]{:S(2)}) collective-permute-start(bf16[768,128]{1,0:T(8,128)(2,1)S(1)} %bitcast.6), channel_id=1, source_target_pairs={{0,1},{1,0},{2,3},{3,2},{4,5},{5,4},{6,7},{7,6},{8,9},{9,8},{10,11... | collective-permute-start | bytes 589832 | tf_op jit(solution)/shard_map/ppermute | solution.py:55
  31.6 1.5 %ready.1 = (f32[528,128]{1,0:T(8,128)S(1)}, f32[2,16,128]{2,1,0:T(8,128)S(1)}, bf16[4,128,512]{2,1,0:T(8,128)(2,1)S(1)}) custom-call(s32[3,16]{1,0:T(4,128)S(1)} %get-tuple-element.15.pos_ref, s32[1,16]{1,0:T(1,128)S(1)} %get-tuple-element.16.seg_ref, s32[4,128]{1,0:T(4,128)S(1)} %get-tuple-element.17.held_ref, bf16[512,1024]{1,0:T(8,128)(2,1)} %v_hbm.3), custom_call_target="tpu_custom_call" | custom-call | tf_op jit(solution)/shard_map/ready/pallas_call | solution.py:30
  33.0 0.0 collective-permute-done.came_ref
  33.0 0.0 copy-done
  33.1 2.2 %first.1 = (bf16[16,40,128]{2,1,0:T(8,128)(2,1)S(1)}, bf16[4,128,512]{2,1,0:T(8,128)(2,1)S(1)}) custom-call(bf16[768,128]{1,0:T(8,128)(2,1)S(1)} %bitcast.7, bf16[768,128]{1,0:T(8,128)(2,1)S(1)} %collective-permute-done.came_ref, f32[2,16,128]{2,1,0:T(8,128)S(1)} %get-tuple-element.18.table_ref, bf16[512,1024]{1,0:T(8,128)(2,1)S(1)} %copy-done, ...), custom_call_target="tpu_custom_call" | custom-call | tf_op jit(solution)/shard_map/first/pallas_call | solution.py:30
  35.3 0.1 collective-permute-start.1
  35.4 1.8 %second.1.own_ref = bf16[16,40,128]{2,1,0:T(8,128)(2,1)S(1)} custom-call(bf16[768,128]{1,0:T(8,128)(2,1)S(1)} %bitcast.8, bf16[768,128]{1,0:T(8,128)(2,1)S(1)} %collective-permute-done.came_ref, f32[2,16,128]{2,1,0:T(8,128)S(1)} %get-tuple-element.18.table_ref, bf16[512,1024]{1,0:T(8,128)(2,1)S(1)} %copy-done, ...), custom_call_target="tpu_custom_call" | custom-call | tf_op jit(solution)/shard_map/second/pallas_call | solution.py:30
  37.2 0.0 collective-permute-done.1.came_ref
  37.2 0.1 couple.1
  37.4 9.7 %all_to_all.21.in_ref = bf16[16,40,128]{2,1,0:T(8,128)(2,1)S(1)} all-to-all(bf16[16,40,128]{2,1,0:T(8,128)(2,1)S(1)} %couple.1), channel_id=1, replica_groups=mesh['y'=4,'z'=8,'x'=4,'c'=2] {'y','x'}, dimensions={0} | all-to-all | bytes 327680 | tf_op jit(solution)/shard_map/all_to_all | solution.py:51
  47.1 0.1 merge.1
  47.2 9.8 %all_to_all.22.in_ref = bf16[8,40,128]{2,1,0:T(8,128)(2,1)S(1)} all-to-all(bf16[8,40,128]{2,1,0:T(8,128)(2,1)S(1)} %merge.1), channel_id=1, replica_groups=mesh['y'=4,'z'=8,'x'=4,'c'=2] {'z'}, dimensions={0} | all-to-all | bytes 163840 | tf_op jit(solution)/shard_map/all_to_all | solution.py:51
  57.0 2.9 %collective-permute-start.2 = (bf16[32,128]{1,0:T(8,128)(2,1)S(1)}, bf16[32,128]{1,0:T(8,128)(2,1)S(1)}, u32[]{:S(2)}, u32[]{:S(2)}) collective-permute-start(bf16[32,128]{1,0:T(8,128)(2,1)S(1)} %finish.1.own_ref), channel_id=1, source_target_pairs={{0,1},{1,0},{2,3},{3,2},{4,5},{5,4},{6,7},{7,6},{8,9},{9,8},{10,11... | collective-permute-start | bytes 24584 | tf_op jit(solution)/shard_map/ppermute | solution.py:55
  59.9 0.8 %collective-permute-done.2.came_ref = bf16[32,128]{1,0:T(8,128)(2,1)S(1)} collective-permute-done((bf16[32,128]{1,0:T(8,128)(2,1)S(1)}, bf16[32,128]{1,0:T(8,128)(2,1)S(1)}, u32[]{:S(2)}, u32[]{:S(2)}) %collective-permute-start.2) | collective-permute-done | bytes 8224 | tf_op jit(solution)/shard_map/ppermute | solution.py:55
  60.8 10.9 %all_to_all.23.in_ref = bf16[16,64,128]{2,1,0:T(8,128)(2,1)S(1)} all-to-all(bf16[16,64,128]{2,1,0:T(8,128)(2,1)S(1)} %pair.1), channel_id=1, replica_groups=mesh['y'=4,'z'=8,'x'=4,'c'=2] {'y','x'}, dimensions={0} | all-to-all | bytes 524288 | tf_op jit(solution)/shard_map/all_to_all | solution.py:51
  71.7 1.0 %place.1 = bf16[16,8192]{1,0:T(8,128)(2,1)} custom-call(bf16[16,64,128]{2,1,0:T(8,128)(2,1)S(1)} %all_to_all.23.in_ref), custom_call_target="tpu_custom_call" | custom-call | tf_op jit(solution)/shard_map/place/pallas_call | solution.py:30
  (2 shorter events, 0.1 us)
Async XLA Ops:
  0.0 33.1 %copy-start = (bf16[512,1024]{1,0:T(8,128)(2,1)S(1)}, bf16[512,1024]{1,0:T(8,128)(2,1)}, u32[]{:S(2)}) copy-start(bf16[512,1024]{1,0:T(8,128)(2,1)} %k_ref.3) | copy-start | bytes 3145732
  28.6 4.5 %collective-permute-start = (bf16[768,128]{1,0:T(8,128)(2,1)S(1)}, bf16[768,128]{1,0:T(8,128)(2,1)S(1)}, u32[]{:S(2)}, u32[]{:S(2)}) collective-permute-start(bf16[768,128]{1,0:T(8,128)(2,1)S(1)} %bitcast.6), channel_id=1, source_target_pairs={{0,1},{1,0},{2,3},{3,2},{4,5},{5,4},{6,7},{7,6},{8,9},{9,8},{10,11... | collective-permute-start | bytes 589832 | tf_op jit(solution)/shard_map/ppermute | solution.py:55
  35.3 1.9 %collective-permute-start.1 = (bf16[16,40,128]{2,1,0:T(8,128)(2,1)S(1)}, bf16[16,40,128]{2,1,0:T(8,128)(2,1)S(1)}, u32[]{:S(2)}, u32[]{:S(2)}) collective-permute-start(bf16[16,40,128]{2,1,0:T(8,128)(2,1)S(1)} %get-tuple-element.22), channel_id=1, source_target_pairs={{0,1},{1,0},{2,3},{3,2},{4,5},{5,4},{6,7},{7,6},{8,9},{9,8},{10,11... | collective-permute-start | bytes 491528 | tf_op jit(solution)/shard_map/ppermute | solution.py:55
  57.0 3.7 %collective-permute-start.2 = (bf16[32,128]{1,0:T(8,128)(2,1)S(1)}, bf16[32,128]{1,0:T(8,128)(2,1)S(1)}, u32[]{:S(2)}, u32[]{:S(2)}) collective-permute-start(bf16[32,128]{1,0:T(8,128)(2,1)S(1)} %finish.1.own_ref), channel_id=1, source_target_pairs={{0,1},{1,0},{2,3},{3,2},{4,5},{5,4},{6,7},{7,6},{8,9},{9,8},{10,11... | collective-permute-start | bytes 24584 | tf_op jit(solution)/shard_map/ppermute | solution.py:55

commit v15 on v11

--- a/solution.py
+++ b/solution.py
@@ -231,32 +231,32 @@
 
 def second_body(q_ref, k_ref, vt_ref, bias_ref, kv_ref, table_ref, out_ref):
     c, y = lax.axis_index("c"), lax.axis_index("y")
+    g = c * 4 + y
+    chips = pl.ds(pl.multiple_of(g * 16, 16), 16)
+    own, came = kv_ref[0, chips, :], kv_ref[1, chips, :]
+    held = [jnp.where(c == core, own, came).astype(BF16) for core in range(2)]
+    row, lane = rows_of((64, 128)), lanes((64, 128))
+    found = []
+    for kind in range(2):
+        pick = where_one(lane == kind * 64 + (row % 16) * 4 + row // 16)
+        value = jnp.zeros((ROWS, 128), F32)
+        for core in range(2):
+            columns = dot(pick, held[core], NT).astype(BF16)
+            for i in range(4):
+                at = rows_of((ROWS, 128)) * 8 + core * 4 + i
+                value = value + dot(
+                    columns[i * 16 : (i + 1) * 16], where_one(lanes((ROWS, 128)) == at), NN
+                )
+        if kind == 0:
+            value = rotate(value, table_ref[0], table_ref[1])
+        found.append(value.astype(BF16))
+    scores = dot(found[0], q_ref[heads_at(c * 4, y), :], NT) * FACTOR + bias_ref[512:, :]
+    weights, peak, total = softened(scores)
+    own = dot(found[1], weights, TN)
     attend(c * 4, q_ref, k_ref, vt_ref, bias_ref, out_ref)
 
     @pl.when((lax.axis_index("z") == 0) & (lax.axis_index("x") == 0))
     def _():
-        g = c * 4 + y
-        chips = pl.ds(pl.multiple_of(g * 16, 16), 16)
-        own, came = kv_ref[0, chips, :], kv_ref[1, chips, :]
-        held = [jnp.where(c == core, own, came).astype(BF16) for core in range(2)]
-        row, lane = rows_of((64, 128)), lanes((64, 128))
-        found = []
-        for kind in range(2):
-            pick = where_one(lane == kind * 64 + (row % 16) * 4 + row // 16)
-            value = jnp.zeros((ROWS, 128), F32)
-            for core in range(2):
-                columns = dot(pick, held[core], NT).astype(BF16)
-                for i in range(4):
-                    at = rows_of((ROWS, 128)) * 8 + core * 4 + i
-                    value = value + dot(
-                        columns[i * 16 : (i + 1) * 16], where_one(lanes((ROWS, 128)) == at), NN
-                    )
-            if kind == 0:
-                value = rotate(value, table_ref[0], table_ref[1])
-            found.append(value.astype(BF16))
-        scores = dot(found[0], q_ref[heads_at(c * 4, y), :], NT) * FACTOR + bias_ref[512:, :]
-        weights, peak, total = softened(scores)
-        own = dot(found[1], weights, TN)
         for n in range(4):
             tile = out_ref.at[y * 4 + n]
             out, peaks, totals = merge(

time: 72.1 us -> 72.3 us (level)
  transfers between devices with their start and end apart: 3 -> 3, of which waited for: 1 -> 2; matrix products, arithmetic and copies ran while one was open for 0% -> 0% of each run, Pallas kernels for 4% -> 4%
where the time goes in v15:
time: 72.3 us; the launch traced here: 72 us
  blocking collectives  58.4 us (81%)
  Pallas kernels  6.62 us (9%)
  starting transfers between devices  5.96 us (8%)
  waiting for transfers between devices  0.99 us (1%)
    all_to_all x4, blocking collectives, exchange(): return lax.all_to_all(tiles, axes, 0, 0, tiled=True)  58.4 us
    pallas_call x9, Pallas kernels, call(): pl.pallas_call(body, name=name, out_shape=out_shape, in_specs=specs or [V...  6.62 us
    ppermute x3, starting transfers between devices, swap(): return lax.ppermute(value, 'c', ((0, 1), (1, 0)))  5.96 us
  transfers between devices with their start and end apart: 3, of which 2 were waited for; matrix products, arithmetic and copies ran while one was open for 0% of the time, Pallas kernels for 4%

profile of v15, /device:TPU:1, one launch (start us, length us, event | category | flops | bytes accessed | tf_op | source)
XLA Modules:
  0.0 72.0 jit_solution(18300047347438995831)
XLA Ops:
  0.0 0.0 copy-start
  0.0 1.2 %pack.1 = (bf16[768,128]{1,0:T(8,128)(2,1)S(1)}, s32[3,16]{1,0:T(4,128)S(1)}, s32[1,16]{1,0:T(1,128)S(1)}, s32[4,128]{1,0:T(4,128)S(1)}) custom-call(bf16[16,32]{1,0:T(8,128)(2,1)} %refs_0_.1, bf16[4,16]{1,0:T(4,128)(2,1)} %bitcast.10, bf16[4,16]{1,0:T(4,128)(2,1)} %bitcast.11, s32[3,16]{1,0:T(4,128)} %refs_3_.1, s32[1,16]{1,0:T(1,128)} %bitcast.12, ...), custom_call_target="tpu_custom_call" | custom-call | tf_op jit(solution)/shard_map/pack/pallas_call | solution.py:30
  1.2 27.4 %all_to_all.20 = bf16[384,2,128]{2,1,0:T(2,128)(2,1)S(1)} all-to-all(bf16[384,2,128]{2,1,0:T(2,128)(2,1)S(1)} %bitcast.8), channel_id=1, replica_groups=mesh['y'=4,'z'=8,'x'=4,'c'=2] {'y','z','x'}, dimensions={0} | all-to-all | bytes 393216 | tf_op jit(solution)/shard_map/all_to_all | solution.py:51
  28.6 3.0 %collective-permute-start = (bf16[768,128]{1,0:T(8,128)(2,1)S(1)}, bf16[768,128]{1,0:T(8,128)(2,1)S(1)}, u32[]{:S(2)}, u32[]{:S(2)}) collective-permute-start(bf16[768,128]{1,0:T(8,128)(2,1)S(1)} %bitcast.6), channel_id=1, source_target_pairs={{0,1},{1,0},{2,3},{3,2},{4,5},{5,4},{6,7},{7,6},{8,9},{9,8},{10,11... | collective-permute-start | bytes 589832 | tf_op jit(solution)/shard_map/ppermute | solution.py:55
  31.6 1.8 %ready.1 = (f32[528,128]{1,0:T(8,128)S(1)}, f32[2,16,128]{2,1,0:T(8,128)S(1)}, bf16[8,128,512]{2,1,0:T(8,128)(2,1)S(1)}) custom-call(s32[3,16]{1,0:T(4,128)S(1)} %get-tuple-element.16.pos_ref, s32[1,16]{1,0:T(1,128)S(1)} %get-tuple-element.17.seg_ref, s32[4,128]{1,0:T(4,128)S(1)} %get-tuple-element.18.held_ref, bf16[512,1024]{1,0:T(8,128)(2,1)} %v_hbm.1), custom_call_target="tpu_custom_call" | custom-call | tf_op jit(solution)/shard_map/ready/pallas_call | solution.py:30
  33.4 0.0 collective-permute-done.came_ref
  33.4 0.0 copy-done
  33.4 1.2 %first.1 = (bf16[16,40,128]{2,1,0:T(8,128)(2,1)S(1)}, bf16[1024,128]{1,0:T(8,128)(2,1)S(1)}, f32[2,128,128]{2,1,0:T(8,128)S(1)}) custom-call(bf16[768,128]{1,0:T(8,128)(2,1)S(1)} %bitcast.7, bf16[768,128]{1,0:T(8,128)(2,1)S(1)} %collective-permute-done.came_ref, f32[2,16,128]{2,1,0:T(8,128)S(1)} %get-tuple-element.19.table_ref, ...), custom_call_target="tpu_custom_call" | custom-call | tf_op jit(solution)/shard_map/first/pallas_call | solution.py:30
  34.6 0.1 collective-permute-start.1
  34.7 1.2 %second.1.own_ref = bf16[16,40,128]{2,1,0:T(8,128)(2,1)S(1)} custom-call(bf16[1024,128]{1,0:T(8,128)(2,1)S(1)} %get-tuple-element.22.q_ref, bf16[512,1024]{1,0:T(8,128)(2,1)S(1)} %copy-done, bf16[8,128,512]{2,1,0:T(8,128)(2,1)S(1)} %get-tuple-element.20.vt_ref, f32[528,128]{1,0:T(8,128)S(1)} %get-tuple-element.21.bias_ref, ...), custom_call_target="tpu_custom_call" | custom-call | tf_op jit(solution)/shard_map/second/pallas_call | solution.py:30
  35.9 0.2 collective-permute-done.1.came_ref
  36.1 0.1 couple.1
  36.2 10.2 %all_to_all.21.in_ref = bf16[16,40,128]{2,1,0:T(8,128)(2,1)S(1)} all-to-all(bf16[16,40,128]{2,1,0:T(8,128)(2,1)S(1)} %couple.1), channel_id=1, replica_groups=mesh['y'=4,'z'=8,'x'=4,'c'=2] {'y','x'}, dimensions={0} | all-to-all | bytes 327680 | tf_op jit(solution)/shard_map/all_to_all | solution.py:51
  46.4 0.1 merge.1
  46.5 9.9 %all_to_all.22.in_ref = bf16[8,40,128]{2,1,0:T(8,128)(2,1)S(1)} all-to-all(bf16[8,40,128]{2,1,0:T(8,128)(2,1)S(1)} %merge.1), channel_id=1, replica_groups=mesh['y'=4,'z'=8,'x'=4,'c'=2] {'z'}, dimensions={0} | all-to-all | bytes 163840 | tf_op jit(solution)/shard_map/all_to_all | solution.py:51
  56.4 2.9 %collective-permute-start.2 = (bf16[32,128]{1,0:T(8,128)(2,1)S(1)}, bf16[32,128]{1,0:T(8,128)(2,1)S(1)}, u32[]{:S(2)}, u32[]{:S(2)}) collective-permute-start(bf16[32,128]{1,0:T(8,128)(2,1)S(1)} %finish.1.own_ref), channel_id=1, source_target_pairs={{0,1},{1,0},{2,3},{3,2},{4,5},{5,4},{6,7},{7,6},{8,9},{9,8},{10,11... | collective-permute-start | bytes 24584 | tf_op jit(solution)/shard_map/ppermute | solution.py:55
  59.3 0.8 %collective-permute-done.2.came_ref = bf16[32,128]{1,0:T(8,128)(2,1)S(1)} collective-permute-done((bf16[32,128]{1,0:T(8,128)(2,1)S(1)}, bf16[32,128]{1,0:T(8,128)(2,1)S(1)}, u32[]{:S(2)}, u32[]{:S(2)}) %collective-permute-start.2) | collective-permute-done | bytes 8224 | tf_op jit(solution)/shard_map/ppermute | solution.py:55
  60.2 10.9 %all_to_all.23.in_ref = bf16[16,64,128]{2,1,0:T(8,128)(2,1)S(1)} all-to-all(bf16[16,64,128]{2,1,0:T(8,128)(2,1)S(1)} %pair.1), channel_id=1, replica_groups=mesh['y'=4,'z'=8,'x'=4,'c'=2] {'y','x'}, dimensions={0} | all-to-all | bytes 524288 | tf_op jit(solution)/shard_map/all_to_all | solution.py:51
  71.1 1.0 %place.1 = bf16[16,8192]{1,0:T(8,128)(2,1)} custom-call(bf16[16,64,128]{2,1,0:T(8,128)(2,1)S(1)} %all_to_all.23.in_ref), custom_call_target="tpu_custom_call" | custom-call | tf_op jit(solution)/shard_map/place/pallas_call | solution.py:30
  (2 shorter events, 0.1 us)
Async XLA Ops:
  0.0 33.4 %copy-start = (bf16[512,1024]{1,0:T(8,128)(2,1)S(1)}, bf16[512,1024]{1,0:T(8,128)(2,1)}, u32[]{:S(2)}) copy-start(bf16[512,1024]{1,0:T(8,128)(2,1)} %k_ref.3) | copy-start | bytes 3145732
  28.6 4.8 %collective-permute-start = (bf16[768,128]{1,0:T(8,128)(2,1)S(1)}, bf16[768,128]{1,0:T(8,128)(2,1)S(1)}, u32[]{:S(2)}, u32[]{:S(2)}) collective-permute-start(bf16[768,128]{1,0:T(8,128)(2,1)S(1)} %bitcast.6), channel_id=1, source_target_pairs={{0,1},{1,0},{2,3},{3,2},{4,5},{5,4},{6,7},{7,6},{8,9},{9,8},{10,11... | collective-permute-start | bytes 589832 | tf_op jit(solution)/shard_map/ppermute | solution.py:55
  34.6 1.5 %collective-permute-start.1 = (bf16[16,40,128]{2,1,0:T(8,128)(2,1)S(1)}, bf16[16,40,128]{2,1,0:T(8,128)(2,1)S(1)}, u32[]{:S(2)}, u32[]{:S(2)}) collective-permute-start(bf16[16,40,128]{2,1,0:T(8,128)(2,1)S(1)} %get-tuple-element.24), channel_id=1, source_target_pairs={{0,1},{1,0},{2,3},{3,2},{4,5},{5,4},{6,7},{7,6},{8,9},{9,8},{10,11... | collective-permute-start | bytes 491528 | tf_op jit(solution)/shard_map/ppermute | solution.py:55
  56.4 3.7 %collective-permute-start.2 = (bf16[32,128]{1,0:T(8,128)(2,1)S(1)}, bf16[32,128]{1,0:T(8,128)(2,1)S(1)}, u32[]{:S(2)}, u32[]{:S(2)}) collective-permute-start(bf16[32,128]{1,0:T(8,128)(2,1)S(1)} %finish.1.own_ref), channel_id=1, source_target_pairs={{0,1},{1,0},{2,3},{3,2},{4,5},{5,4},{6,7},{7,6},{8,9},{9,8},{10,11... | collective-permute-start | bytes 24584 | tf_op jit(solution)/shard_map/ppermute | solution.py:55

commit v16 on v11

--- a/solution.py
+++ b/solution.py
@@ -146,7 +146,28 @@
     return tile.astype(BF16)
 
 
-def ready_body(pos_ref, seg_ref, held_ref, v_hbm, bias_ref, table_ref, vt_ref, v_ref, sem):
+def span_columns(ref, core, cosine, sine):
+    g = lax.axis_index("c") * 4 + lax.axis_index("y")
+    chips = where_one(rows_of((16, 96)) * 6 + 4 == lanes((16, 96)))
+    held = dot(chips, ref[pl.ds(pl.multiple_of(g * 96, 96), 96), :], NN).astype(BF16)
+    row, lane = rows_of((64, 128)), lanes((64, 128))
+    found = []
+    for kind in range(2):
+        pick = where_one(lane == kind * 64 + (row % 16) * 4 + row // 16)
+        columns = dot(pick, held, NT).astype(BF16)
+        value = jnp.zeros((ROWS, 128), F32)
+        for i in range(4):
+            at = rows_of((ROWS, 128)) * 8 + core * 4 + i
+            value = value + dot(
+                columns[i * 16 : (i + 1) * 16], where_one(lanes((ROWS, 128)) == at), NN
+            )
+        found.append(value if kind else rotate(value, cosine, sine))
+    return found
+
+
+def ready_body(
+    pos_ref, seg_ref, held_ref, own_ref, v_hbm, bias_ref, table_ref, span_ref, vt_ref, v_ref, sem
+):
     copy = pltpu.make_async_copy(v_hbm, v_ref, sem)
     copy.start()
     lane = lanes((ROWS, 128))
@@ -161,19 +182,22 @@
         bias_ref[part * 128 : (part + 1) * 128, :] = (dot(have, wanted, TN) - 1.0) * -HIDDEN
     seen = dot(kinds, wanted, TN) * jnp.where(rows_of((ROWS, 128)) <= lane // 8, 1.0, 0.0)
     bias_ref[512:, :] = (seen - 1.0) * -HIDDEN
+    for n, part in enumerate(
+        span_columns(own_ref, lax.axis_index("c"), cosine, jnp.where(lane < 64, -sine, sine))
+    ):
+        span_ref[n] = part
     copy.wait()
     for g in range(KVH):
         vt_ref[g] = v_ref[:, g * HD : (g + 1) * HD].T
 
 
-def join(own_ref, came_ref, table_ref, q_ref, kv_ref, flat_ref):
+def join(own_ref, came_ref, table_ref, q_ref, flat_ref):
     c = lax.axis_index("c")
     shape = (128, 4 * 128)
     source, target = rows_of(shape), lanes(shape)
     whole = jnp.zeros((256, 512), F32)
     for n, ref in enumerate((own_ref, came_ref)):
         flat_ref[n, 0:768, :] = ref[...].astype(F32)
-        kv_ref[n] = flat_ref[n, pl.ds(4, 128, stride=6), :]
         for half in range(2):
             part = jnp.concatenate(
                 [flat_ref[n, pl.ds(j + 6 * half, 64, stride=12), :] for j in range(4)], axis=0
@@ -223,37 +247,22 @@
 
 
 def first_body(
-    own_ref, came_ref, table_ref, k_ref, vt_ref, bias_ref, out_ref, q_ref, kv_ref, flat_ref
+    own_ref, came_ref, table_ref, k_ref, vt_ref, bias_ref, out_ref, q_ref, flat_ref
 ):
-    join(own_ref, came_ref, table_ref, q_ref, kv_ref, flat_ref)
+    join(own_ref, came_ref, table_ref, q_ref, flat_ref)
     attend((1 - lax.axis_index("c")) * 4, q_ref, k_ref, vt_ref, bias_ref, out_ref)
 
 
-def second_body(q_ref, k_ref, vt_ref, bias_ref, kv_ref, table_ref, out_ref):
+def second_body(q_ref, k_ref, vt_ref, bias_ref, came_ref, span_ref, table_ref, out_ref):
     c, y = lax.axis_index("c"), lax.axis_index("y")
     attend(c * 4, q_ref, k_ref, vt_ref, bias_ref, out_ref)
 
     @pl.when((lax.axis_index("z") == 0) & (lax.axis_index("x") == 0))
     def _():
-        g = c * 4 + y
-        chips = pl.ds(pl.multiple_of(g * 16, 16), 16)
-        own, came = kv_ref[0, chips, :], kv_ref[1, chips, :]
-        held = [jnp.where(c == core, own, came).astype(BF16) for core in range(2)]
-        row, lane = rows_of((64, 128)), lanes((64, 128))
-        found = []
-        for kind in range(2):
-            pick = where_one(lane == kind * 64 + (row % 16) * 4 + row // 16)
-            value = jnp.zeros((ROWS, 128), F32)
-            for core in range(2):
-                columns = dot(pick, held[core], NT).astype(BF16)
-                for i in range(4):
-                    at = rows_of((ROWS, 128)) * 8 + core * 4 + i
-                    value = value + dot(
-                        columns[i * 16 : (i + 1) * 16], where_one(lanes((ROWS, 128)) == at), NN
-                    )
-            if kind == 0:
-                value = rotate(value, table_ref[0], table_ref[1])
-            found.append(value.astype(BF16))
+        found = [
+            (span_ref[n] + part).astype(BF16)
+            for n, part in enumerate(span_columns(came_ref, 1 - c, table_ref[0], table_ref[1]))
+        ]
         scores = dot(found[0], q_ref[heads_at(c * 4, y), :], NT) * FACTOR + bias_ref[512:, :]
         weights, peak, total = softened(scores)
         own = dot(found[1], weights, TN)
@@ -367,26 +376,28 @@
     )
     tiles = exchange(tiles.reshape(-1, 2, 128), CHIPS).reshape(-1, 128)
     came = swap(tiles)
-    bias, tables, turned_values = call(
+    bias, tables, span, turned_values = call(
         ready_body,
         "ready",
         (
             shape((512 + ROWS, 128), F32),
+            shape((2, ROWS, 128), F32),
             shape((2, ROWS, 128), F32),
             shape((KVH, HD, 512), BF16),
         ),
         positions,
         span_segments,
         cache_segments,
+        tiles,
         pltpu.with_memory_space_constraint(cache_values, pltpu.HBM),
-        specs=[VMEM] * 3 + [HBM],
+        specs=[VMEM] * 4 + [HBM],
         scratch=[pltpu.VMEM((512, KVH * HD), BF16), pltpu.SemaphoreType.DMA],
     )
     message = shape((16, 40, 128), BF16)
-    parts, q, kv = call(
+    parts, q = call(
         first_body,
         "first",
-        (message, shape((H * ROWS, HD), BF16), shape((2, 128, 128), F32)),
+        (message, shape((H * ROWS, HD), BF16)),
         tiles,
         came,
         tables,
@@ -397,7 +408,7 @@
     )
     other = swap(parts)
     parts = call(
-        second_body, "second", message, q, cache_keys, turned_values, bias, kv, tables
+        second_body, "second", message, q, cache_keys, turned_values, bias, came, span, tables
     )
     parts = call(couple_body, "couple", message, parts, other)
     parts = exchange(parts, PLANE)

time: 72.1 us -> 72.3 us (level)
  transfers between devices with their start and end apart: 3 -> 3, of which waited for: 1 -> 1; matrix products, arithmetic and copies ran while one was open for 0% -> 0% of each run, Pallas kernels for 4% -> 5%
where the time goes in v16:
time: 72.3 us; the launch traced here: 72 us
  blocking collectives  58.5 us (81%)
  Pallas kernels  6.98 us (10%)
  starting transfers between devices  5.58 us (8%)
  waiting for transfers between devices  0.83 us (1%)
    all_to_all x4, blocking collectives, exchange(): return lax.all_to_all(tiles, axes, 0, 0, tiled=True)  58.5 us
    pallas_call x9, Pallas kernels, call(): pl.pallas_call(body, name=name, out_shape=out_shape, in_specs=specs or [V...  6.98 us
    ppermute x3, starting transfers between devices, swap(): return lax.ppermute(value, 'c', ((0, 1), (1, 0)))  5.58 us
  transfers between devices with their start and end apart: 3, of which 1 were waited for; matrix products, arithmetic and copies ran while one was open for 0% of the time, Pallas kernels for 5%

profile of v16, /device:TPU:1, one launch (start us, length us, event | category | flops | bytes accessed | tf_op | source)
XLA Modules:
  0.0 72.0 jit_solution(4802643065595358877)
XLA Ops:
  0.0 0.0 copy-start
  0.0 1.2 %pack.1 = (bf16[768,128]{1,0:T(8,128)(2,1)S(1)}, s32[3,16]{1,0:T(4,128)S(1)}, s32[1,16]{1,0:T(1,128)S(1)}, s32[4,128]{1,0:T(4,128)S(1)}) custom-call(bf16[16,32]{1,0:T(8,128)(2,1)} %refs_0_.1, bf16[4,16]{1,0:T(4,128)(2,1)} %bitcast.11, bf16[4,16]{1,0:T(4,128)(2,1)} %bitcast.12, s32[3,16]{1,0:T(4,128)} %refs_3_.1, s32[1,16]{1,0:T(1,128)} %bitcast.13, ...), custom_call_target="tpu_custom_call" | custom-call | tf_op jit(solution)/shard_map/pack/pallas_call | solution.py:30
  1.2 27.4 %all_to_all.20 = bf16[384,2,128]{2,1,0:T(2,128)(2,1)S(1)} all-to-all(bf16[384,2,128]{2,1,0:T(2,128)(2,1)S(1)} %bitcast.9), channel_id=1, replica_groups=mesh['y'=4,'z'=8,'x'=4,'c'=2] {'y','z','x'}, dimensions={0} | all-to-all | bytes 393216 | tf_op jit(solution)/shard_map/all_to_all | solution.py:51
  28.6 3.0 %collective-permute-start = (bf16[768,128]{1,0:T(8,128)(2,1)S(1)}, bf16[768,128]{1,0:T(8,128)(2,1)S(1)}, u32[]{:S(2)}, u32[]{:S(2)}) collective-permute-start(bf16[768,128]{1,0:T(8,128)(2,1)S(1)} %bitcast.6), channel_id=1, source_target_pairs={{0,1},{1,0},{2,3},{3,2},{4,5},{5,4},{6,7},{7,6},{8,9},{9,8},{10,11... | collective-permute-start | bytes 589832 | tf_op jit(solution)/shard_map/ppermute | solution.py:55
  31.6 1.9 %ready.1 = (f32[528,128]{1,0:T(8,128)S(1)}, f32[2,16,128]{2,1,0:T(8,128)S(1)}, f32[2,16,128]{2,1,0:T(8,128)S(1)}, bf16[8,128,512]{2,1,0:T(8,128)(2,1)S(1)}) custom-call(s32[3,16]{1,0:T(4,128)S(1)} %get-tuple-element.16.pos_ref, s32[1,16]{1,0:T(1,128)S(1)} %get-tuple-element.17.seg_ref, s32[4,128]{1,0:T(4,128)S(1)} %get-tuple-element.18.held_ref, ...), custom_call_target="tpu_custom_call" | custom-call | tf_op jit(solution)/shard_map/ready/pallas_call | solution.py:30
  33.5 0.0 collective-permute-done.came_ref
  33.5 0.0 copy-done
  33.5 1.2 %first.1 = (bf16[16,40,128]{2,1,0:T(8,128)(2,1)S(1)}, bf16[1024,128]{1,0:T(8,128)(2,1)S(1)}) custom-call(bf16[768,128]{1,0:T(8,128)(2,1)S(1)} %bitcast.8, bf16[768,128]{1,0:T(8,128)(2,1)S(1)} %collective-permute-done.came_ref, f32[2,16,128]{2,1,0:T(8,128)S(1)} %get-tuple-element.19.table_ref, bf16[512,1024]{1,0:T(8,128)(2,1)S(1)} %copy-done, ...), custom_call_target="tpu_custom_call" | custom-call | tf_op jit(solution)/shard_map/first/pallas_call | solution.py:30
  34.7 0.1 collective-permute-start.1
  34.8 1.4 %second.1.own_ref = bf16[16,40,128]{2,1,0:T(8,128)(2,1)S(1)} custom-call(bf16[1024,128]{1,0:T(8,128)(2,1)S(1)} %get-tuple-element.22.q_ref, bf16[512,1024]{1,0:T(8,128)(2,1)S(1)} %copy-done, bf16[8,128,512]{2,1,0:T(8,128)(2,1)S(1)} %get-tuple-element.20.vt_ref, f32[528,128]{1,0:T(8,128)S(1)} %get-tuple-element.21.bias_ref, ...), custom_call_target="tpu_custom_call" | custom-call | tf_op jit(solution)/shard_map/second/pallas_call | solution.py:30
  36.3 0.0 collective-permute-done.1.came_ref
  36.3 0.1 couple.1
  36.4 10.4 %all_to_all.21.in_ref = bf16[16,40,128]{2,1,0:T(8,128)(2,1)S(1)} all-to-all(bf16[16,40,128]{2,1,0:T(8,128)(2,1)S(1)} %couple.1), channel_id=1, replica_groups=mesh['y'=4,'z'=8,'x'=4,'c'=2] {'y','x'}, dimensions={0} | all-to-all | bytes 327680 | tf_op jit(solution)/shard_map/all_to_all | solution.py:51
  46.9 0.1 merge.1
  46.9 9.8 %all_to_all.22.in_ref = bf16[8,40,128]{2,1,0:T(8,128)(2,1)S(1)} all-to-all(bf16[8,40,128]{2,1,0:T(8,128)(2,1)S(1)} %merge.1), channel_id=1, replica_groups=mesh['y'=4,'z'=8,'x'=4,'c'=2] {'z'}, dimensions={0} | all-to-all | bytes 163840 | tf_op jit(solution)/shard_map/all_to_all | solution.py:51
  56.8 2.5 %collective-permute-start.2 = (bf16[32,128]{1,0:T(8,128)(2,1)S(1)}, bf16[32,128]{1,0:T(8,128)(2,1)S(1)}, u32[]{:S(2)}, u32[]{:S(2)}) collective-permute-start(bf16[32,128]{1,0:T(8,128)(2,1)S(1)} %finish.1.own_ref), channel_id=1, source_target_pairs={{0,1},{1,0},{2,3},{3,2},{4,5},{5,4},{6,7},{7,6},{8,9},{9,8},{10,11... | collective-permute-start | bytes 24584 | tf_op jit(solution)/shard_map/ppermute | solution.py:55
  59.3 0.8 %collective-permute-done.2.came_ref = bf16[32,128]{1,0:T(8,128)(2,1)S(1)} collective-permute-done((bf16[32,128]{1,0:T(8,128)(2,1)S(1)}, bf16[32,128]{1,0:T(8,128)(2,1)S(1)}, u32[]{:S(2)}, u32[]{:S(2)}) %collective-permute-start.2) | collective-permute-done | bytes 8224 | tf_op jit(solution)/shard_map/ppermute | solution.py:55
  60.1 10.9 %all_to_all.23.in_ref = bf16[16,64,128]{2,1,0:T(8,128)(2,1)S(1)} all-to-all(bf16[16,64,128]{2,1,0:T(8,128)(2,1)S(1)} %pair.1), channel_id=1, replica_groups=mesh['y'=4,'z'=8,'x'=4,'c'=2] {'y','x'}, dimensions={0} | all-to-all | bytes 524288 | tf_op jit(solution)/shard_map/all_to_all | solution.py:51
  71.0 1.0 %place.1 = bf16[16,8192]{1,0:T(8,128)(2,1)} custom-call(bf16[16,64,128]{2,1,0:T(8,128)(2,1)S(1)} %all_to_all.23.in_ref), custom_call_target="tpu_custom_call" | custom-call | tf_op jit(solution)/shard_map/place/pallas_call | solution.py:30
  (2 shorter events, 0.1 us)
Async XLA Ops:
  0.0 33.5 %copy-start = (bf16[512,1024]{1,0:T(8,128)(2,1)S(1)}, bf16[512,1024]{1,0:T(8,128)(2,1)}, u32[]{:S(2)}) copy-start(bf16[512,1024]{1,0:T(8,128)(2,1)} %k_ref.3) | copy-start | bytes 3145732
  28.6 4.9 %collective-permute-start = (bf16[768,128]{1,0:T(8,128)(2,1)S(1)}, bf16[768,128]{1,0:T(8,128)(2,1)S(1)}, u32[]{:S(2)}, u32[]{:S(2)}) collective-permute-start(bf16[768,128]{1,0:T(8,128)(2,1)S(1)} %bitcast.6), channel_id=1, source_target_pairs={{0,1},{1,0},{2,3},{3,2},{4,5},{5,4},{6,7},{7,6},{8,9},{9,8},{10,11... | collective-permute-start | bytes 589832 | tf_op jit(solution)/shard_map/ppermute | solution.py:55
  34.7 1.5 %collective-permute-start.1 = (bf16[16,40,128]{2,1,0:T(8,128)(2,1)S(1)}, bf16[16,40,128]{2,1,0:T(8,128)(2,1)S(1)}, u32[]{:S(2)}, u32[]{:S(2)}) collective-permute-start(bf16[16,40,128]{2,1,0:T(8,128)(2,1)S(1)} %get-tuple-element.24), channel_id=1, source_target_pairs={{0,1},{1,0},{2,3},{3,2},{4,5},{5,4},{6,7},{7,6},{8,9},{9,8},{10,11... | collective-permute-start | bytes 491528 | tf_op jit(solution)/shard_map/ppermute | solution.py:55
  56.8 3.3 %collective-permute-start.2 = (bf16[32,128]{1,0:T(8,128)(2,1)S(1)}, bf16[32,128]{1,0:T(8,128)(2,1)S(1)}, u32[]{:S(2)}, u32[]{:S(2)}) collective-permute-start(bf16[32,128]{1,0:T(8,128)(2,1)S(1)} %finish.1.own_ref), channel_id=1, source_target_pairs={{0,1},{1,0},{2,3},{3,2},{4,5},{5,4},{6,7},{7,6},{8,9},{9,8},{10,11... | collective-permute-start | bytes 24584 | tf_op jit(solution)/shard_map/ppermute | solution.py:55

commit v17 on v11

--- a/solution.py
+++ b/solution.py
@@ -14,7 +14,7 @@
 ROWS = 16
 ALL = ("y", "z", "x", "c")
 CHIPS = ("y", "z", "x")
-PLANE = ("y", "x")
+PLANE = ("x", "y")
 LOG2E = 1.4426950408889634
 NONE = -1e30
 HIDDEN = -2e30

time: 72.1 us -> 71.8 us (level)
    all_to_all x4, blocking collectives: 58.5 us -> 57.8 us  [exchange(): return lax.all_to_all(tiles, axes, 0, 0, tiled=True)]
where the time goes in v17:
time: 71.8 us; the launch traced here: 71.5 us
  blocking collectives  57.8 us (81%)
  Pallas kernels  6.84 us (10%)
  starting transfers between devices  5.96 us (8%)
  waiting for transfers between devices  0.83 us (1%)
    all_to_all x4, blocking collectives, exchange(): return lax.all_to_all(tiles, axes, 0, 0, tiled=True)  57.8 us
    pallas_call x9, Pallas kernels, call(): pl.pallas_call(body, name=name, out_shape=out_shape, in_specs=specs or [V...  6.84 us
    ppermute x3, starting transfers between devices, swap(): return lax.ppermute(value, 'c', ((0, 1), (1, 0)))  5.96 us
  transfers between devices with their start and end apart: 3, of which 1 were waited for; matrix products, arithmetic and copies ran while one was open for 0% of the time, Pallas kernels for 4%

profile of v17, /device:TPU:1, one launch (start us, length us, event | category | flops | bytes accessed | tf_op | source)
XLA Modules:
  0.0 71.5 jit_solution(13295748581781316349)
XLA Ops:
  0.0 0.0 copy-start
  0.0 1.2 %pack.1 = (bf16[768,128]{1,0:T(8,128)(2,1)S(1)}, s32[3,16]{1,0:T(4,128)S(1)}, s32[1,16]{1,0:T(1,128)S(1)}, s32[4,128]{1,0:T(4,128)S(1)}) custom-call(bf16[16,32]{1,0:T(8,128)(2,1)} %refs_0_.1, bf16[4,16]{1,0:T(4,128)(2,1)} %bitcast.10, bf16[4,16]{1,0:T(4,128)(2,1)} %bitcast.11, s32[3,16]{1,0:T(4,128)} %refs_3_.1, s32[1,16]{1,0:T(1,128)} %bitcast.12, ...), custom_call_target="tpu_custom_call" | custom-call | tf_op jit(solution)/shard_map/pack/pallas_call | solution.py:30
  1.2 27.4 %all_to_all.20 = bf16[384,2,128]{2,1,0:T(2,128)(2,1)S(1)} all-to-all(bf16[384,2,128]{2,1,0:T(2,128)(2,1)S(1)} %bitcast.8), channel_id=1, replica_groups=mesh['y'=4,'z'=8,'x'=4,'c'=2] {'y','z','x'}, dimensions={0} | all-to-all | bytes 393216 | tf_op jit(solution)/shard_map/all_to_all | solution.py:51
  28.6 3.0 %collective-permute-start = (bf16[768,128]{1,0:T(8,128)(2,1)S(1)}, bf16[768,128]{1,0:T(8,128)(2,1)S(1)}, u32[]{:S(2)}, u32[]{:S(2)}) collective-permute-start(bf16[768,128]{1,0:T(8,128)(2,1)S(1)} %bitcast.6), channel_id=1, source_target_pairs={{0,1},{1,0},{2,3},{3,2},{4,5},{5,4},{6,7},{7,6},{8,9},{9,8},{10,11... | collective-permute-start | bytes 589832 | tf_op jit(solution)/shard_map/ppermute | solution.py:55
  31.6 1.8 %ready.1 = (f32[528,128]{1,0:T(8,128)S(1)}, f32[2,16,128]{2,1,0:T(8,128)S(1)}, bf16[8,128,512]{2,1,0:T(8,128)(2,1)S(1)}) custom-call(s32[3,16]{1,0:T(4,128)S(1)} %get-tuple-element.16.pos_ref, s32[1,16]{1,0:T(1,128)S(1)} %get-tuple-element.17.seg_ref, s32[4,128]{1,0:T(4,128)S(1)} %get-tuple-element.18.held_ref, bf16[512,1024]{1,0:T(8,128)(2,1)} %v_hbm.1), custom_call_target="tpu_custom_call" | custom-call | tf_op jit(solution)/shard_map/ready/pallas_call | solution.py:30
  33.4 0.0 collective-permute-done.came_ref
  33.4 0.0 copy-done
  33.4 1.2 %first.1 = (bf16[16,40,128]{2,1,0:T(8,128)(2,1)S(1)}, bf16[1024,128]{1,0:T(8,128)(2,1)S(1)}, f32[2,128,128]{2,1,0:T(8,128)S(1)}) custom-call(bf16[768,128]{1,0:T(8,128)(2,1)S(1)} %bitcast.7, bf16[768,128]{1,0:T(8,128)(2,1)S(1)} %collective-permute-done.came_ref, f32[2,16,128]{2,1,0:T(8,128)S(1)} %get-tuple-element.19.table_ref, ...), custom_call_target="tpu_custom_call" | custom-call | tf_op jit(solution)/shard_map/first/pallas_call | solution.py:30
  34.6 0.1 collective-permute-start.1
  34.7 1.4 %second.1.own_ref = bf16[16,40,128]{2,1,0:T(8,128)(2,1)S(1)} custom-call(bf16[1024,128]{1,0:T(8,128)(2,1)S(1)} %get-tuple-element.22.q_ref, bf16[512,1024]{1,0:T(8,128)(2,1)S(1)} %copy-done, bf16[8,128,512]{2,1,0:T(8,128)(2,1)S(1)} %get-tuple-element.20.vt_ref, f32[528,128]{1,0:T(8,128)S(1)} %get-tuple-element.21.bias_ref, ...), custom_call_target="tpu_custom_call" | custom-call | tf_op jit(solution)/shard_map/second/pallas_call | solution.py:30
  36.2 0.0 collective-permute-done.1.came_ref
  36.2 0.1 couple.1
  36.3 10.0 %all_to_all.21.in_ref = bf16[16,40,128]{2,1,0:T(8,128)(2,1)S(1)} all-to-all(bf16[16,40,128]{2,1,0:T(8,128)(2,1)S(1)} %couple.1), channel_id=1, replica_groups=mesh['y'=4,'z'=8,'x'=4,'c'=2] {'x','y'}, dimensions={0} | all-to-all | bytes 327680 | tf_op jit(solution)/shard_map/all_to_all | solution.py:51
  46.3 0.1 merge.1
  46.3 9.8 %all_to_all.22.in_ref = bf16[8,40,128]{2,1,0:T(8,128)(2,1)S(1)} all-to-all(bf16[8,40,128]{2,1,0:T(8,128)(2,1)S(1)} %merge.1), channel_id=1, replica_groups=mesh['y'=4,'z'=8,'x'=4,'c'=2] {'z'}, dimensions={0} | all-to-all | bytes 163840 | tf_op jit(solution)/shard_map/all_to_all | solution.py:51
  56.2 2.9 %collective-permute-start.2 = (bf16[32,128]{1,0:T(8,128)(2,1)S(1)}, bf16[32,128]{1,0:T(8,128)(2,1)S(1)}, u32[]{:S(2)}, u32[]{:S(2)}) collective-permute-start(bf16[32,128]{1,0:T(8,128)(2,1)S(1)} %finish.1.own_ref), channel_id=1, source_target_pairs={{0,1},{1,0},{2,3},{3,2},{4,5},{5,4},{6,7},{7,6},{8,9},{9,8},{10,11... | collective-permute-start | bytes 24584 | tf_op jit(solution)/shard_map/ppermute | solution.py:55
  59.1 0.8 %collective-permute-done.2.came_ref = bf16[32,128]{1,0:T(8,128)(2,1)S(1)} collective-permute-done((bf16[32,128]{1,0:T(8,128)(2,1)S(1)}, bf16[32,128]{1,0:T(8,128)(2,1)S(1)}, u32[]{:S(2)}, u32[]{:S(2)}) %collective-permute-start.2) | collective-permute-done | bytes 8224 | tf_op jit(solution)/shard_map/ppermute | solution.py:55
  59.9 10.6 %all_to_all.23.in_ref = bf16[16,64,128]{2,1,0:T(8,128)(2,1)S(1)} all-to-all(bf16[16,64,128]{2,1,0:T(8,128)(2,1)S(1)} %pair.1), channel_id=1, replica_groups=mesh['y'=4,'z'=8,'x'=4,'c'=2] {'x','y'}, dimensions={0} | all-to-all | bytes 524288 | tf_op jit(solution)/shard_map/all_to_all | solution.py:51
  70.6 1.0 %place.1 = bf16[16,8192]{1,0:T(8,128)(2,1)} custom-call(bf16[16,64,128]{2,1,0:T(8,128)(2,1)S(1)} %all_to_all.23.in_ref), custom_call_target="tpu_custom_call" | custom-call | tf_op jit(solution)/shard_map/place/pallas_call | solution.py:30
  (2 shorter events, 0.1 us)
Async XLA Ops:
  0.0 33.4 %copy-start = (bf16[512,1024]{1,0:T(8,128)(2,1)S(1)}, bf16[512,1024]{1,0:T(8,128)(2,1)}, u32[]{:S(2)}) copy-start(bf16[512,1024]{1,0:T(8,128)(2,1)} %k_ref.3) | copy-start | bytes 3145732
  28.6 4.8 %collective-permute-start = (bf16[768,128]{1,0:T(8,128)(2,1)S(1)}, bf16[768,128]{1,0:T(8,128)(2,1)S(1)}, u32[]{:S(2)}, u32[]{:S(2)}) collective-permute-start(bf16[768,128]{1,0:T(8,128)(2,1)S(1)} %bitcast.6), channel_id=1, source_target_pairs={{0,1},{1,0},{2,3},{3,2},{4,5},{5,4},{6,7},{7,6},{8,9},{9,8},{10,11... | collective-permute-start | bytes 589832 | tf_op jit(solution)/shard_map/ppermute | solution.py:55
  34.6 1.5 %collective-permute-start.1 = (bf16[16,40,128]{2,1,0:T(8,128)(2,1)S(1)}, bf16[16,40,128]{2,1,0:T(8,128)(2,1)S(1)}, u32[]{:S(2)}, u32[]{:S(2)}) collective-permute-start(bf16[16,40,128]{2,1,0:T(8,128)(2,1)S(1)} %get-tuple-element.24), channel_id=1, source_target_pairs={{0,1},{1,0},{2,3},{3,2},{4,5},{5,4},{6,7},{7,6},{8,9},{9,8},{10,11... | collective-permute-start | bytes 491528 | tf_op jit(solution)/shard_map/ppermute | solution.py:55
  56.2 3.7 %collective-permute-start.2 = (bf16[32,128]{1,0:T(8,128)(2,1)S(1)}, bf16[32,128]{1,0:T(8,128)(2,1)S(1)}, u32[]{:S(2)}, u32[]{:S(2)}) collective-permute-start(bf16[32,128]{1,0:T(8,128)(2,1)S(1)} %finish.1.own_ref), channel_id=1, source_target_pairs={{0,1},{1,0},{2,3},{3,2},{4,5},{5,4},{6,7},{7,6},{8,9},{9,8},{10,11... | collective-permute-start | bytes 24584 | tf_op jit(solution)/shard_map/ppermute | solution.py:55

commit v18 on v17

--- a/solution.py
+++ b/solution.py
@@ -238,19 +238,19 @@
         g = c * 4 + y
         chips = pl.ds(pl.multiple_of(g * 16, 16), 16)
         own, came = kv_ref[0, chips, :], kv_ref[1, chips, :]
-        held = [jnp.where(c == core, own, came).astype(BF16) for core in range(2)]
-        row, lane = rows_of((64, 128)), lanes((64, 128))
+        held = [jnp.where(c == core, own, came) for core in range(2)]
+        held = jnp.concatenate(held, axis=0).astype(BF16)
+        row, lane = rows_of((128, 128)), lanes((128, 128))
+        pick = where_one(lane == row // 64 * 64 + (row % 16) * 4 + (row // 16) % 4)
+        row, lane = rows_of((32, 256)), lanes((32, 256))
+        place = where_one(row == lane // 128 * 16 + lane % 128 // 8)
+        columns = dot(dot(pick, held, NT).astype(BF16), place, NN)
+        row, lane = rows_of((128, 256)), lanes((128, 256))
+        columns = jnp.where(lane % 8 == lane // 128 * 4 + (row // 16) % 4, columns, 0.0)
+        columns = columns[:, :128] + columns[:, 128:]
         found = []
         for kind in range(2):
-            pick = where_one(lane == kind * 64 + (row % 16) * 4 + row // 16)
-            value = jnp.zeros((ROWS, 128), F32)
-            for core in range(2):
-                columns = dot(pick, held[core], NT).astype(BF16)
-                for i in range(4):
-                    at = rows_of((ROWS, 128)) * 8 + core * 4 + i
-                    value = value + dot(
-                        columns[i * 16 : (i + 1) * 16], where_one(lanes((ROWS, 128)) == at), NN
-                    )
+            value = sum(columns[(kind * 4 + i) * 16 : (kind * 4 + i + 1) * 16] for i in range(4))
             if kind == 0:
                 value = rotate(value, table_ref[0], table_ref[1])
             found.append(value.astype(BF16))

time: 71.8 us -> 71.8 us (level)
  transfers between devices with their start and end apart: 3 -> 3, of which waited for: 1 -> 2; matrix products, arithmetic and copies ran while one was open for 0% -> 0% of each run, Pallas kernels for 4% -> 4%
where the time goes in v18:
time: 71.8 us; the launch traced here: 71.5 us
  blocking collectives  57.9 us (81%)
  Pallas kernels  6.71 us (9%)
  starting transfers between devices  5.96 us (8%)
  waiting for transfers between devices  0.9 us (1%)
    all_to_all x4, blocking collectives, exchange(): return lax.all_to_all(tiles, axes, 0, 0, tiled=True)  57.9 us
    pallas_call x9, Pallas kernels, call(): pl.pallas_call(body, name=name, out_shape=out_shape, in_specs=specs or [V...  6.71 us
    ppermute x3, starting transfers between devices, swap(): return lax.ppermute(value, 'c', ((0, 1), (1, 0)))  5.96 us
  transfers between devices with their start and end apart: 3, of which 2 were waited for; matrix products, arithmetic and copies ran while one was open for 0% of the time, Pallas kernels for 4%

profile of v18, /device:TPU:1, one launch (start us, length us, event | category | flops | bytes accessed | tf_op | source)
XLA Modules:
  0.0 71.5 jit_solution(9730186793190390634)
XLA Ops:
  0.0 0.0 copy-start
  0.0 1.2 %pack.1 = (bf16[768,128]{1,0:T(8,128)(2,1)S(1)}, s32[3,16]{1,0:T(4,128)S(1)}, s32[1,16]{1,0:T(1,128)S(1)}, s32[4,128]{1,0:T(4,128)S(1)}) custom-call(bf16[16,32]{1,0:T(8,128)(2,1)} %refs_0_.1, bf16[4,16]{1,0:T(4,128)(2,1)} %bitcast.10, bf16[4,16]{1,0:T(4,128)(2,1)} %bitcast.11, s32[3,16]{1,0:T(4,128)} %refs_3_.1, s32[1,16]{1,0:T(1,128)} %bitcast.12, ...), custom_call_target="tpu_custom_call" | custom-call | tf_op jit(solution)/shard_map/pack/pallas_call | solution.py:30
  1.2 27.4 %all_to_all.20 = bf16[384,2,128]{2,1,0:T(2,128)(2,1)S(1)} all-to-all(bf16[384,2,128]{2,1,0:T(2,128)(2,1)S(1)} %bitcast.8), channel_id=1, replica_groups=mesh['y'=4,'z'=8,'x'=4,'c'=2] {'y','z','x'}, dimensions={0} | all-to-all | bytes 393216 | tf_op jit(solution)/shard_map/all_to_all | solution.py:51
  28.6 3.0 %collective-permute-start = (bf16[768,128]{1,0:T(8,128)(2,1)S(1)}, bf16[768,128]{1,0:T(8,128)(2,1)S(1)}, u32[]{:S(2)}, u32[]{:S(2)}) collective-permute-start(bf16[768,128]{1,0:T(8,128)(2,1)S(1)} %bitcast.6), channel_id=1, source_target_pairs={{0,1},{1,0},{2,3},{3,2},{4,5},{5,4},{6,7},{7,6},{8,9},{9,8},{10,11... | collective-permute-start | bytes 589832 | tf_op jit(solution)/shard_map/ppermute | solution.py:55
  31.6 1.8 %ready.1 = (f32[528,128]{1,0:T(8,128)S(1)}, f32[2,16,128]{2,1,0:T(8,128)S(1)}, bf16[8,128,512]{2,1,0:T(8,128)(2,1)S(1)}) custom-call(s32[3,16]{1,0:T(4,128)S(1)} %get-tuple-element.16.pos_ref, s32[1,16]{1,0:T(1,128)S(1)} %get-tuple-element.17.seg_ref, s32[4,128]{1,0:T(4,128)S(1)} %get-tuple-element.18.held_ref, bf16[512,1024]{1,0:T(8,128)(2,1)} %v_hbm.1), custom_call_target="tpu_custom_call" | custom-call | tf_op jit(solution)/shard_map/ready/pallas_call | solution.py:30
  33.4 0.0 collective-permute-done.came_ref
  33.4 0.0 copy-done
  33.4 1.2 %first.1 = (bf16[16,40,128]{2,1,0:T(8,128)(2,1)S(1)}, bf16[1024,128]{1,0:T(8,128)(2,1)S(1)}, f32[2,128,128]{2,1,0:T(8,128)S(1)}) custom-call(bf16[768,128]{1,0:T(8,128)(2,1)S(1)} %bitcast.7, bf16[768,128]{1,0:T(8,128)(2,1)S(1)} %collective-permute-done.came_ref, f32[2,16,128]{2,1,0:T(8,128)S(1)} %get-tuple-element.19.table_ref, ...), custom_call_target="tpu_custom_call" | custom-call | tf_op jit(solution)/shard_map/first/pallas_call | solution.py:30
  34.6 0.1 collective-permute-start.1
  34.7 1.3 %second.1.own_ref = bf16[16,40,128]{2,1,0:T(8,128)(2,1)S(1)} custom-call(bf16[1024,128]{1,0:T(8,128)(2,1)S(1)} %get-tuple-element.22.q_ref, bf16[512,1024]{1,0:T(8,128)(2,1)S(1)} %copy-done, bf16[8,128,512]{2,1,0:T(8,128)(2,1)S(1)} %get-tuple-element.20.vt_ref, f32[528,128]{1,0:T(8,128)S(1)} %get-tuple-element.21.bias_ref, ...), custom_call_target="tpu_custom_call" | custom-call | tf_op jit(solution)/shard_map/second/pallas_call | solution.py:30
  36.0 0.1 collective-permute-done.1.came_ref
  36.1 0.1 couple.1
  36.2 10.0 %all_to_all.21.in_ref = bf16[16,40,128]{2,1,0:T(8,128)(2,1)S(1)} all-to-all(bf16[16,40,128]{2,1,0:T(8,128)(2,1)S(1)} %couple.1), channel_id=1, replica_groups=mesh['y'=4,'z'=8,'x'=4,'c'=2] {'x','y'}, dimensions={0} | all-to-all | bytes 327680 | tf_op jit(solution)/shard_map/all_to_all | solution.py:51
  46.3 0.1 merge.1
  46.3 9.8 %all_to_all.22.in_ref = bf16[8,40,128]{2,1,0:T(8,128)(2,1)S(1)} all-to-all(bf16[8,40,128]{2,1,0:T(8,128)(2,1)S(1)} %merge.1), channel_id=1, replica_groups=mesh['y'=4,'z'=8,'x'=4,'c'=2] {'z'}, dimensions={0} | all-to-all | bytes 163840 | tf_op jit(solution)/shard_map/all_to_all | solution.py:51
  56.2 2.9 %collective-permute-start.2 = (bf16[32,128]{1,0:T(8,128)(2,1)S(1)}, bf16[32,128]{1,0:T(8,128)(2,1)S(1)}, u32[]{:S(2)}, u32[]{:S(2)}) collective-permute-start(bf16[32,128]{1,0:T(8,128)(2,1)S(1)} %finish.1.own_ref), channel_id=1, source_target_pairs={{0,1},{1,0},{2,3},{3,2},{4,5},{5,4},{6,7},{7,6},{8,9},{9,8},{10,11... | collective-permute-start | bytes 24584 | tf_op jit(solution)/shard_map/ppermute | solution.py:55
  59.1 0.8 %collective-permute-done.2.came_ref = bf16[32,128]{1,0:T(8,128)(2,1)S(1)} collective-permute-done((bf16[32,128]{1,0:T(8,128)(2,1)S(1)}, bf16[32,128]{1,0:T(8,128)(2,1)S(1)}, u32[]{:S(2)}, u32[]{:S(2)}) %collective-permute-start.2) | collective-permute-done | bytes 8224 | tf_op jit(solution)/shard_map/ppermute | solution.py:55
  59.9 10.6 %all_to_all.23.in_ref = bf16[16,64,128]{2,1,0:T(8,128)(2,1)S(1)} all-to-all(bf16[16,64,128]{2,1,0:T(8,128)(2,1)S(1)} %pair.1), channel_id=1, replica_groups=mesh['y'=4,'z'=8,'x'=4,'c'=2] {'x','y'}, dimensions={0} | all-to-all | bytes 524288 | tf_op jit(solution)/shard_map/all_to_all | solution.py:51
  70.6 1.0 %place.1 = bf16[16,8192]{1,0:T(8,128)(2,1)} custom-call(bf16[16,64,128]{2,1,0:T(8,128)(2,1)S(1)} %all_to_all.23.in_ref), custom_call_target="tpu_custom_call" | custom-call | tf_op jit(solution)/shard_map/place/pallas_call | solution.py:30
  (2 shorter events, 0.1 us)
Async XLA Ops:
  0.0 33.4 %copy-start = (bf16[512,1024]{1,0:T(8,128)(2,1)S(1)}, bf16[512,1024]{1,0:T(8,128)(2,1)}, u32[]{:S(2)}) copy-start(bf16[512,1024]{1,0:T(8,128)(2,1)} %k_ref.3) | copy-start | bytes 3145732
  28.6 4.8 %collective-permute-start = (bf16[768,128]{1,0:T(8,128)(2,1)S(1)}, bf16[768,128]{1,0:T(8,128)(2,1)S(1)}, u32[]{:S(2)}, u32[]{:S(2)}) collective-permute-start(bf16[768,128]{1,0:T(8,128)(2,1)S(1)} %bitcast.6), channel_id=1, source_target_pairs={{0,1},{1,0},{2,3},{3,2},{4,5},{5,4},{6,7},{7,6},{8,9},{9,8},{10,11... | collective-permute-start | bytes 589832 | tf_op jit(solution)/shard_map/ppermute | solution.py:55
  34.6 1.5 %collective-permute-start.1 = (bf16[16,40,128]{2,1,0:T(8,128)(2,1)S(1)}, bf16[16,40,128]{2,1,0:T(8,128)(2,1)S(1)}, u32[]{:S(2)}, u32[]{:S(2)}) collective-permute-start(bf16[16,40,128]{2,1,0:T(8,128)(2,1)S(1)} %get-tuple-element.24), channel_id=1, source_target_pairs={{0,1},{1,0},{2,3},{3,2},{4,5},{5,4},{6,7},{7,6},{8,9},{9,8},{10,11... | collective-permute-start | bytes 491528 | tf_op jit(solution)/shard_map/ppermute | solution.py:55
  56.2 3.7 %collective-permute-start.2 = (bf16[32,128]{1,0:T(8,128)(2,1)S(1)}, bf16[32,128]{1,0:T(8,128)(2,1)S(1)}, u32[]{:S(2)}, u32[]{:S(2)}) collective-permute-start(bf16[32,128]{1,0:T(8,128)(2,1)S(1)} %finish.1.own_ref), channel_id=1, source_target_pairs={{0,1},{1,0},{2,3},{3,2},{4,5},{5,4},{6,7},{7,6},{8,9},{9,8},{10,11... | collective-permute-start | bytes 24584 | tf_op jit(solution)/shard_map/ppermute | solution.py:55

commit v19 on v15

--- a/solution.py
+++ b/solution.py
@@ -14,7 +14,7 @@
 ROWS = 16
 ALL = ("y", "z", "x", "c")
 CHIPS = ("y", "z", "x")
-PLANE = ("y", "x")
+PLANE = ("x", "y")
 LOG2E = 1.4426950408889634
 NONE = -1e30
 HIDDEN = -2e30
@@ -234,19 +234,19 @@
     g = c * 4 + y
     chips = pl.ds(pl.multiple_of(g * 16, 16), 16)
     own, came = kv_ref[0, chips, :], kv_ref[1, chips, :]
-    held = [jnp.where(c == core, own, came).astype(BF16) for core in range(2)]
-    row, lane = rows_of((64, 128)), lanes((64, 128))
+    held = [jnp.where(c == core, own, came) for core in range(2)]
+    held = jnp.concatenate(held, axis=0).astype(BF16)
+    row, lane = rows_of((128, 128)), lanes((128, 128))
+    pick = where_one(lane == row // 64 * 64 + (row % 16) * 4 + (row // 16) % 4)
+    row, lane = rows_of((32, 256)), lanes((32, 256))
+    place = where_one(row == lane // 128 * 16 + lane % 128 // 8)
+    columns = dot(dot(pick, held, NT).astype(BF16), place, NN)
+    row, lane = rows_of((128, 256)), lanes((128, 256))
+    columns = jnp.where(lane % 8 == lane // 128 * 4 + (row // 16) % 4, columns, 0.0)
+    columns = columns[:, :128] + columns[:, 128:]
     found = []
     for kind in range(2):
-        pick = where_one(lane == kind * 64 + (row % 16) * 4 + row // 16)
-        value = jnp.zeros((ROWS, 128), F32)
-        for core in range(2):
-            columns = dot(pick, held[core], NT).astype(BF16)
-            for i in range(4):
-                at = rows_of((ROWS, 128)) * 8 + core * 4 + i
-                value = value + dot(
-                    columns[i * 16 : (i + 1) * 16], where_one(lanes((ROWS, 128)) == at), NN
-                )
+        value = sum(columns[(kind * 4 + i) * 16 : (kind * 4 + i + 1) * 16] for i in range(4))
         if kind == 0:
             value = rotate(value, table_ref[0], table_ref[1])
         found.append(value.astype(BF16))

time: 72.3 us -> 71.9 us (level)
  no operation moved by 1% of the time
where the time goes in v19:
time: 71.9 us; the launch traced here: 71.6 us
  blocking collectives  57.9 us (81%)
  Pallas kernels  6.52 us (9%)
  starting transfers between devices  5.96 us (8%)
  waiting for transfers between devices  1.1 us (2%)
    all_to_all x4, blocking collectives, exchange(): return lax.all_to_all(tiles, axes, 0, 0, tiled=True)  57.9 us
    pallas_call x9, Pallas kernels, call(): pl.pallas_call(body, name=name, out_shape=out_shape, in_specs=specs or [V...  6.52 us
    ppermute x3, starting transfers between devices, swap(): return lax.ppermute(value, 'c', ((0, 1), (1, 0)))  5.96 us
  transfers between devices with their start and end apart: 3, of which 2 were waited for; matrix products, arithmetic and copies ran while one was open for 0% of the time, Pallas kernels for 4%

profile of v19, /device:TPU:1, one launch (start us, length us, event | category | flops | bytes accessed | tf_op | source)
XLA Modules:
  0.0 71.6 jit_solution(17819601781058550639)
XLA Ops:
  0.0 0.0 copy-start
  0.0 1.2 %pack.1 = (bf16[768,128]{1,0:T(8,128)(2,1)S(1)}, s32[3,16]{1,0:T(4,128)S(1)}, s32[1,16]{1,0:T(1,128)S(1)}, s32[4,128]{1,0:T(4,128)S(1)}) custom-call(bf16[16,32]{1,0:T(8,128)(2,1)} %refs_0_.1, bf16[4,16]{1,0:T(4,128)(2,1)} %bitcast.10, bf16[4,16]{1,0:T(4,128)(2,1)} %bitcast.11, s32[3,16]{1,0:T(4,128)} %refs_3_.1, s32[1,16]{1,0:T(1,128)} %bitcast.12, ...), custom_call_target="tpu_custom_call" | custom-call | tf_op jit(solution)/shard_map/pack/pallas_call | solution.py:30
  1.2 27.4 %all_to_all.20 = bf16[384,2,128]{2,1,0:T(2,128)(2,1)S(1)} all-to-all(bf16[384,2,128]{2,1,0:T(2,128)(2,1)S(1)} %bitcast.8), channel_id=1, replica_groups=mesh['y'=4,'z'=8,'x'=4,'c'=2] {'y','z','x'}, dimensions={0} | all-to-all | bytes 393216 | tf_op jit(solution)/shard_map/all_to_all | solution.py:51
  28.6 3.0 %collective-permute-start = (bf16[768,128]{1,0:T(8,128)(2,1)S(1)}, bf16[768,128]{1,0:T(8,128)(2,1)S(1)}, u32[]{:S(2)}, u32[]{:S(2)}) collective-permute-start(bf16[768,128]{1,0:T(8,128)(2,1)S(1)} %bitcast.6), channel_id=1, source_target_pairs={{0,1},{1,0},{2,3},{3,2},{4,5},{5,4},{6,7},{7,6},{8,9},{9,8},{10,11... | collective-permute-start | bytes 589832 | tf_op jit(solution)/shard_map/ppermute | solution.py:55
  31.6 1.8 %ready.1 = (f32[528,128]{1,0:T(8,128)S(1)}, f32[2,16,128]{2,1,0:T(8,128)S(1)}, bf16[8,128,512]{2,1,0:T(8,128)(2,1)S(1)}) custom-call(s32[3,16]{1,0:T(4,128)S(1)} %get-tuple-element.16.pos_ref, s32[1,16]{1,0:T(1,128)S(1)} %get-tuple-element.17.seg_ref, s32[4,128]{1,0:T(4,128)S(1)} %get-tuple-element.18.held_ref, bf16[512,1024]{1,0:T(8,128)(2,1)} %v_hbm.1), custom_call_target="tpu_custom_call" | custom-call | tf_op jit(solution)/shard_map/ready/pallas_call | solution.py:30
  33.4 0.0 collective-permute-done.came_ref
  33.4 0.0 copy-done
  33.4 1.2 %first.1 = (bf16[16,40,128]{2,1,0:T(8,128)(2,1)S(1)}, bf16[1024,128]{1,0:T(8,128)(2,1)S(1)}, f32[2,128,128]{2,1,0:T(8,128)S(1)}) custom-call(bf16[768,128]{1,0:T(8,128)(2,1)S(1)} %bitcast.7, bf16[768,128]{1,0:T(8,128)(2,1)S(1)} %collective-permute-done.came_ref, f32[2,16,128]{2,1,0:T(8,128)S(1)} %get-tuple-element.19.table_ref, ...), custom_call_target="tpu_custom_call" | custom-call | tf_op jit(solution)/shard_map/first/pallas_call | solution.py:30
  34.6 0.1 collective-permute-start.1
  34.7 1.1 %second.1.own_ref = bf16[16,40,128]{2,1,0:T(8,128)(2,1)S(1)} custom-call(bf16[1024,128]{1,0:T(8,128)(2,1)S(1)} %get-tuple-element.22.q_ref, bf16[512,1024]{1,0:T(8,128)(2,1)S(1)} %copy-done, bf16[8,128,512]{2,1,0:T(8,128)(2,1)S(1)} %get-tuple-element.20.vt_ref, f32[528,128]{1,0:T(8,128)S(1)} %get-tuple-element.21.bias_ref, ...), custom_call_target="tpu_custom_call" | custom-call | tf_op jit(solution)/shard_map/second/pallas_call | solution.py:30
  35.8 0.3 collective-permute-done.1.came_ref
  36.1 0.1 couple.1
  36.2 10.0 %all_to_all.21.in_ref = bf16[16,40,128]{2,1,0:T(8,128)(2,1)S(1)} all-to-all(bf16[16,40,128]{2,1,0:T(8,128)(2,1)S(1)} %couple.1), channel_id=1, replica_groups=mesh['y'=4,'z'=8,'x'=4,'c'=2] {'x','y'}, dimensions={0} | all-to-all | bytes 327680 | tf_op jit(solution)/shard_map/all_to_all | solution.py:51
  46.2 0.1 merge.1
  46.3 9.8 %all_to_all.22.in_ref = bf16[8,40,128]{2,1,0:T(8,128)(2,1)S(1)} all-to-all(bf16[8,40,128]{2,1,0:T(8,128)(2,1)S(1)} %merge.1), channel_id=1, replica_groups=mesh['y'=4,'z'=8,'x'=4,'c'=2] {'z'}, dimensions={0} | all-to-all | bytes 163840 | tf_op jit(solution)/shard_map/all_to_all | solution.py:51
  56.2 2.9 %collective-permute-start.2 = (bf16[32,128]{1,0:T(8,128)(2,1)S(1)}, bf16[32,128]{1,0:T(8,128)(2,1)S(1)}, u32[]{:S(2)}, u32[]{:S(2)}) collective-permute-start(bf16[32,128]{1,0:T(8,128)(2,1)S(1)} %finish.1.own_ref), channel_id=1, source_target_pairs={{0,1},{1,0},{2,3},{3,2},{4,5},{5,4},{6,7},{7,6},{8,9},{9,8},{10,11... | collective-permute-start | bytes 24584 | tf_op jit(solution)/shard_map/ppermute | solution.py:55
  59.1 0.8 %collective-permute-done.2.came_ref = bf16[32,128]{1,0:T(8,128)(2,1)S(1)} collective-permute-done((bf16[32,128]{1,0:T(8,128)(2,1)S(1)}, bf16[32,128]{1,0:T(8,128)(2,1)S(1)}, u32[]{:S(2)}, u32[]{:S(2)}) %collective-permute-start.2) | collective-permute-done | bytes 8224 | tf_op jit(solution)/shard_map/ppermute | solution.py:55
  59.9 10.7 %all_to_all.23.in_ref = bf16[16,64,128]{2,1,0:T(8,128)(2,1)S(1)} all-to-all(bf16[16,64,128]{2,1,0:T(8,128)(2,1)S(1)} %pair.1), channel_id=1, replica_groups=mesh['y'=4,'z'=8,'x'=4,'c'=2] {'x','y'}, dimensions={0} | all-to-all | bytes 524288 | tf_op jit(solution)/shard_map/all_to_all | solution.py:51
  70.6 1.0 %place.1 = bf16[16,8192]{1,0:T(8,128)(2,1)} custom-call(bf16[16,64,128]{2,1,0:T(8,128)(2,1)S(1)} %all_to_all.23.in_ref), custom_call_target="tpu_custom_call" | custom-call | tf_op jit(solution)/shard_map/place/pallas_call | solution.py:30
  (2 shorter events, 0.1 us)
Async XLA Ops:
  0.0 33.4 %copy-start = (bf16[512,1024]{1,0:T(8,128)(2,1)S(1)}, bf16[512,1024]{1,0:T(8,128)(2,1)}, u32[]{:S(2)}) copy-start(bf16[512,1024]{1,0:T(8,128)(2,1)} %k_ref.3) | copy-start | bytes 3145732
  28.6 4.8 %collective-permute-start = (bf16[768,128]{1,0:T(8,128)(2,1)S(1)}, bf16[768,128]{1,0:T(8,128)(2,1)S(1)}, u32[]{:S(2)}, u32[]{:S(2)}) collective-permute-start(bf16[768,128]{1,0:T(8,128)(2,1)S(1)} %bitcast.6), channel_id=1, source_target_pairs={{0,1},{1,0},{2,3},{3,2},{4,5},{5,4},{6,7},{7,6},{8,9},{9,8},{10,11... | collective-permute-start | bytes 589832 | tf_op jit(solution)/shard_map/ppermute | solution.py:55
  34.6 1.5 %collective-permute-start.1 = (bf16[16,40,128]{2,1,0:T(8,128)(2,1)S(1)}, bf16[16,40,128]{2,1,0:T(8,128)(2,1)S(1)}, u32[]{:S(2)}, u32[]{:S(2)}) collective-permute-start(bf16[16,40,128]{2,1,0:T(8,128)(2,1)S(1)} %get-tuple-element.24), channel_id=1, source_target_pairs={{0,1},{1,0},{2,3},{3,2},{4,5},{5,4},{6,7},{7,6},{8,9},{9,8},{10,11... | collective-permute-start | bytes 491528 | tf_op jit(solution)/shard_map/ppermute | solution.py:55
  56.2 3.7 %collective-permute-start.2 = (bf16[32,128]{1,0:T(8,128)(2,1)S(1)}, bf16[32,128]{1,0:T(8,128)(2,1)S(1)}, u32[]{:S(2)}, u32[]{:S(2)}) collective-permute-start(bf16[32,128]{1,0:T(8,128)(2,1)S(1)} %finish.1.own_ref), channel_id=1, source_target_pairs={{0,1},{1,0},{2,3},{3,2},{4,5},{5,4},{6,7},{7,6},{8,9},{9,8},{10,11... | collective-permute-start | bytes 24584 | tf_op jit(solution)/shard_map/ppermute | solution.py:55

commit v20 on v19

--- a/solution.py
+++ b/solution.py
@@ -79,18 +79,23 @@
     ]
     for copy in copies:
         copy.start()
-    for copy in copies:
+    wide = where_one(lanes((32, 128)) % 32 == rows_of((32, 128)))
+    late = lanes((ROWS, 128)) // 32 == rows_of((ROWS, 128)) // 4
+    token = lanes((ROWS, 128)) // 4 - rows_of((ROWS, 128))
+    keys, values = where_one(token == 0), where_one(token == 16)
+    column = lanes((4, 128)) % 4 == rows_of((4, 128))
+    q_rows = where_one(rows_of((48, ROWS)) % 6 == lanes((48, ROWS)) % 4)
+    kv_rows = where_one(rows_of((48, 4)) % 6 == 4)
+    for copy in copies[:3]:
         copy.wait()
-    q = dot(q_ref[...], where_one(lanes((32, 128)) % 32 == rows_of((32, 128))), NN)
-    q = jnp.where(lanes((ROWS, 128)) // 32 == rows_of((ROWS, 128)) // 4, q, 0.0).astype(BF16)
-    token = lanes((ROWS, 128)) // 4 - rows_of((ROWS, 128))
-    kv = dot(k_ref[...], where_one(token == 0), NN) + dot(v_ref[...], where_one(token == 16), NN)
-    kv = jnp.where(lanes((4, 128)) % 4 == rows_of((4, 128)), kv, 0.0).astype(BF16)
-    tiles = dot(where_one(rows_of((48, ROWS)) % 6 == lanes((48, ROWS)) % 4), q, NN)
-    tiles = tiles + dot(where_one(rows_of((48, 4)) % 6 == 4), kv, NN)
-    tiles = tiles.astype(BF16)
+    q = jnp.where(late, dot(q_ref[...], wide, NN), 0.0).astype(BF16)
+    kv = dot(k_ref[...], keys, NN) + dot(v_ref[...], values, NN)
+    kv = jnp.where(column, kv, 0.0).astype(BF16)
+    tiles = (dot(q_rows, q, NN) + dot(kv_rows, kv, NN)).astype(BF16)
     for n in range(out_ref.shape[0] // 48):
         out_ref[n * 48 : (n + 1) * 48, :] = tiles
+    for copy in copies[3:]:
+        copy.wait()
 
 
 def turn(angle):

time: 71.9 us -> 71.8 us (level)
  no operation moved by 1% of the time
where the time goes in v20:
time: 71.8 us; the launch traced here: 71.5 us
  blocking collectives  57.9 us (81%)
  Pallas kernels  6.48 us (9%)
  starting transfers between devices  5.96 us (8%)
  waiting for transfers between devices  1.1 us (2%)
    all_to_all x4, blocking collectives, exchange(): return lax.all_to_all(tiles, axes, 0, 0, tiled=True)  57.9 us
    pallas_call x9, Pallas kernels, call(): pl.pallas_call(body, name=name, out_shape=out_shape, in_specs=specs or [V...  6.48 us
    ppermute x3, starting transfers between devices, swap(): return lax.ppermute(value, 'c', ((0, 1), (1, 0)))  5.96 us
  transfers between devices with their start and end apart: 3, of which 2 were waited for; matrix products, arithmetic and copies ran while one was open for 0% of the time, Pallas kernels for 4%

profile of v20, /device:TPU:1, one launch (start us, length us, event | category | flops | bytes accessed | tf_op | source)
XLA Modules:
  0.0 71.5 jit_solution(16348305629616266570)
XLA Ops:
  0.0 0.0 copy-start
  0.0 1.1 %pack.1 = (bf16[768,128]{1,0:T(8,128)(2,1)S(1)}, s32[3,16]{1,0:T(4,128)S(1)}, s32[1,16]{1,0:T(1,128)S(1)}, s32[4,128]{1,0:T(4,128)S(1)}) custom-call(bf16[16,32]{1,0:T(8,128)(2,1)} %refs_0_.1, bf16[4,16]{1,0:T(4,128)(2,1)} %bitcast.10, bf16[4,16]{1,0:T(4,128)(2,1)} %bitcast.11, s32[3,16]{1,0:T(4,128)} %refs_3_.1, s32[1,16]{1,0:T(1,128)} %bitcast.12, ...), custom_call_target="tpu_custom_call" | custom-call | tf_op jit(solution)/shard_map/pack/pallas_call | solution.py:30
  1.1 27.4 %all_to_all.20 = bf16[384,2,128]{2,1,0:T(2,128)(2,1)S(1)} all-to-all(bf16[384,2,128]{2,1,0:T(2,128)(2,1)S(1)} %bitcast.8), channel_id=1, replica_groups=mesh['y'=4,'z'=8,'x'=4,'c'=2] {'y','z','x'}, dimensions={0} | all-to-all | bytes 393216 | tf_op jit(solution)/shard_map/all_to_all | solution.py:51
  28.5 3.0 %collective-permute-start = (bf16[768,128]{1,0:T(8,128)(2,1)S(1)}, bf16[768,128]{1,0:T(8,128)(2,1)S(1)}, u32[]{:S(2)}, u32[]{:S(2)}) collective-permute-start(bf16[768,128]{1,0:T(8,128)(2,1)S(1)} %bitcast.6), channel_id=1, source_target_pairs={{0,1},{1,0},{2,3},{3,2},{4,5},{5,4},{6,7},{7,6},{8,9},{9,8},{10,11... | collective-permute-start | bytes 589832 | tf_op jit(solution)/shard_map/ppermute | solution.py:55
  31.5 1.8 %ready.1 = (f32[528,128]{1,0:T(8,128)S(1)}, f32[2,16,128]{2,1,0:T(8,128)S(1)}, bf16[8,128,512]{2,1,0:T(8,128)(2,1)S(1)}) custom-call(s32[3,16]{1,0:T(4,128)S(1)} %get-tuple-element.16.pos_ref, s32[1,16]{1,0:T(1,128)S(1)} %get-tuple-element.17.seg_ref, s32[4,128]{1,0:T(4,128)S(1)} %get-tuple-element.18.held_ref, bf16[512,1024]{1,0:T(8,128)(2,1)} %v_hbm.1), custom_call_target="tpu_custom_call" | custom-call | tf_op jit(solution)/shard_map/ready/pallas_call | solution.py:30
  33.3 0.0 collective-permute-done.came_ref
  33.3 0.0 copy-done
  33.3 1.2 %first.1 = (bf16[16,40,128]{2,1,0:T(8,128)(2,1)S(1)}, bf16[1024,128]{1,0:T(8,128)(2,1)S(1)}, f32[2,128,128]{2,1,0:T(8,128)S(1)}) custom-call(bf16[768,128]{1,0:T(8,128)(2,1)S(1)} %bitcast.7, bf16[768,128]{1,0:T(8,128)(2,1)S(1)} %collective-permute-done.came_ref, f32[2,16,128]{2,1,0:T(8,128)S(1)} %get-tuple-element.19.table_ref, ...), custom_call_target="tpu_custom_call" | custom-call | tf_op jit(solution)/shard_map/first/pallas_call | solution.py:30
  34.6 0.1 collective-permute-start.1
  34.7 1.1 %second.1.own_ref = bf16[16,40,128]{2,1,0:T(8,128)(2,1)S(1)} custom-call(bf16[1024,128]{1,0:T(8,128)(2,1)S(1)} %get-tuple-element.22.q_ref, bf16[512,1024]{1,0:T(8,128)(2,1)S(1)} %copy-done, bf16[8,128,512]{2,1,0:T(8,128)(2,1)S(1)} %get-tuple-element.20.vt_ref, f32[528,128]{1,0:T(8,128)S(1)} %get-tuple-element.21.bias_ref, ...), custom_call_target="tpu_custom_call" | custom-call | tf_op jit(solution)/shard_map/second/pallas_call | solution.py:30
  35.8 0.3 collective-permute-done.1.came_ref
  36.0 0.1 couple.1
  36.2 10.0 %all_to_all.21.in_ref = bf16[16,40,128]{2,1,0:T(8,128)(2,1)S(1)} all-to-all(bf16[16,40,128]{2,1,0:T(8,128)(2,1)S(1)} %couple.1), channel_id=1, replica_groups=mesh['y'=4,'z'=8,'x'=4,'c'=2] {'x','y'}, dimensions={0} | all-to-all | bytes 327680 | tf_op jit(solution)/shard_map/all_to_all | solution.py:51
  46.2 0.1 merge.1
  46.3 9.8 %all_to_all.22.in_ref = bf16[8,40,128]{2,1,0:T(8,128)(2,1)S(1)} all-to-all(bf16[8,40,128]{2,1,0:T(8,128)(2,1)S(1)} %merge.1), channel_id=1, replica_groups=mesh['y'=4,'z'=8,'x'=4,'c'=2] {'z'}, dimensions={0} | all-to-all | bytes 163840 | tf_op jit(solution)/shard_map/all_to_all | solution.py:51
  56.1 2.9 %collective-permute-start.2 = (bf16[32,128]{1,0:T(8,128)(2,1)S(1)}, bf16[32,128]{1,0:T(8,128)(2,1)S(1)}, u32[]{:S(2)}, u32[]{:S(2)}) collective-permute-start(bf16[32,128]{1,0:T(8,128)(2,1)S(1)} %finish.1.own_ref), channel_id=1, source_target_pairs={{0,1},{1,0},{2,3},{3,2},{4,5},{5,4},{6,7},{7,6},{8,9},{9,8},{10,11... | collective-permute-start | bytes 24584 | tf_op jit(solution)/shard_map/ppermute | solution.py:55
  59.0 0.8 %collective-permute-done.2.came_ref = bf16[32,128]{1,0:T(8,128)(2,1)S(1)} collective-permute-done((bf16[32,128]{1,0:T(8,128)(2,1)S(1)}, bf16[32,128]{1,0:T(8,128)(2,1)S(1)}, u32[]{:S(2)}, u32[]{:S(2)}) %collective-permute-start.2) | collective-permute-done | bytes 8224 | tf_op jit(solution)/shard_map/ppermute | solution.py:55
  59.9 10.7 %all_to_all.23.in_ref = bf16[16,64,128]{2,1,0:T(8,128)(2,1)S(1)} all-to-all(bf16[16,64,128]{2,1,0:T(8,128)(2,1)S(1)} %pair.1), channel_id=1, replica_groups=mesh['y'=4,'z'=8,'x'=4,'c'=2] {'x','y'}, dimensions={0} | all-to-all | bytes 524288 | tf_op jit(solution)/shard_map/all_to_all | solution.py:51
  70.6 1.0 %place.1 = bf16[16,8192]{1,0:T(8,128)(2,1)} custom-call(bf16[16,64,128]{2,1,0:T(8,128)(2,1)S(1)} %all_to_all.23.in_ref), custom_call_target="tpu_custom_call" | custom-call | tf_op jit(solution)/shard_map/place/pallas_call | solution.py:30
  (2 shorter events, 0.1 us)
Async XLA Ops:
  0.0 33.3 %copy-start = (bf16[512,1024]{1,0:T(8,128)(2,1)S(1)}, bf16[512,1024]{1,0:T(8,128)(2,1)}, u32[]{:S(2)}) copy-start(bf16[512,1024]{1,0:T(8,128)(2,1)} %k_ref.3) | copy-start | bytes 3145732
  28.5 4.8 %collective-permute-start = (bf16[768,128]{1,0:T(8,128)(2,1)S(1)}, bf16[768,128]{1,0:T(8,128)(2,1)S(1)}, u32[]{:S(2)}, u32[]{:S(2)}) collective-permute-start(bf16[768,128]{1,0:T(8,128)(2,1)S(1)} %bitcast.6), channel_id=1, source_target_pairs={{0,1},{1,0},{2,3},{3,2},{4,5},{5,4},{6,7},{7,6},{8,9},{9,8},{10,11... | collective-permute-start | bytes 589832 | tf_op jit(solution)/shard_map/ppermute | solution.py:55
  34.6 1.5 %collective-permute-start.1 = (bf16[16,40,128]{2,1,0:T(8,128)(2,1)S(1)}, bf16[16,40,128]{2,1,0:T(8,128)(2,1)S(1)}, u32[]{:S(2)}, u32[]{:S(2)}) collective-permute-start(bf16[16,40,128]{2,1,0:T(8,128)(2,1)S(1)} %get-tuple-element.24), channel_id=1, source_target_pairs={{0,1},{1,0},{2,3},{3,2},{4,5},{5,4},{6,7},{7,6},{8,9},{9,8},{10,11... | collective-permute-start | bytes 491528 | tf_op jit(solution)/shard_map/ppermute | solution.py:55
  56.1 3.7 %collective-permute-start.2 = (bf16[32,128]{1,0:T(8,128)(2,1)S(1)}, bf16[32,128]{1,0:T(8,128)(2,1)S(1)}, u32[]{:S(2)}, u32[]{:S(2)}) collective-permute-start(bf16[32,128]{1,0:T(8,128)(2,1)S(1)} %finish.1.own_ref), channel_id=1, source_target_pairs={{0,1},{1,0},{2,3},{3,2},{4,5},{5,4},{6,7},{7,6},{8,9},{9,8},{10,11... | collective-permute-start | bytes 24584 | tf_op jit(solution)/shard_map/ppermute | solution.py:55
